TPU v7x, 128 devices: a whole 4x4x4 slice. The times are simulated.
128 devices in a mesh: rep: 2 (over core), dp: 64 (over x, y, z).
Axes of the slice: x: 4, y: 4, z: 4, core: 2. Of those that a mesh axis runs over, the one named last changes fastest.
Arguments:
- x: bfloat16 [128, 2048, 896], P(('rep', 'dp')), parts along dimension 0
- dy: bfloat16 [128, 2048, 896], P(('rep', 'dp')), parts along dimension 0
- w_gate: bfloat16 [2, 896, 2560], replicated
- w_up: bfloat16 [2, 896, 2560], replicated
- w_down: bfloat16 [2, 2560, 896], replicated
- m_w_gate: float32 [2, 896, 2560], P(None, 'dp')
- m_w_up: float32 [2, 896, 2560], P(None, 'dp')
- m_w_down: float32 [2, 2560, 896], P(None, 'dp')
- v_w_gate: float32 [2, 896, 2560], P(None, 'dp')
- v_w_up: float32 [2, 896, 2560], P(None, 'dp')
- v_w_down: float32 [2, 2560, 896], P(None, 'dp')
Outputs:
- output 1: bfloat16 [4, 896, 2560], P('rep'), parts along dimension 0
- output 2: bfloat16 [4, 896, 2560], P('rep'), parts along dimension 0
- output 3: bfloat16 [4, 2560, 896], P('rep'), parts along dimension 0
- output 4: float32 [4, 896, 2560], P('rep', 'dp'), parts along dimension 0
- output 5: float32 [4, 896, 2560], P('rep', 'dp'), parts along dimension 0
- output 6: float32 [4, 2560, 896], P('rep', 'dp'), parts along dimension 0
- output 7: float32 [4, 896, 2560], P('rep', 'dp'), parts along dimension 0
- output 8: float32 [4, 896, 2560], P('rep', 'dp'), parts along dimension 0
- output 9: float32 [4, 2560, 896], P('rep', 'dp'), parts along dimension 0
There are 2 independent parts. A program takes and returns all parts, laid end to end along the dimension named above; an argument that names none is the same for every part.
All inputs are finite; a program needn't handle non-finite values.
Results may differ from a plain program's by a relative error of at most 0.022.
Values are sent between devices in bfloat16 or wider.
A program may use at most 1.5 GiB of HBM per device.

v0:
```python
import jax
import jax.numpy as jnp
from jax import lax

NAMES = ("w_gate", "w_up", "w_down")


def matmul(a, w):
    return jnp.dot(a, w, preferred_element_type=jnp.float32).astype(jnp.bfloat16)


def normed(h):
    wide = h.astype(jnp.float32)
    scale = lax.rsqrt(jnp.mean(wide**2, -1, keepdims=True) + 1e-6)
    return (wide * scale).astype(jnp.bfloat16)


def layer(h, w):
    a = normed(h)
    gate = jnp.dot(a, w["w_gate"], preferred_element_type=jnp.float32)
    up = jnp.dot(a, w["w_up"], preferred_element_type=jnp.float32)
    return h + matmul((jax.nn.silu(gate) * up).astype(jnp.bfloat16), w["w_down"])


def adamw(w, m, v, g):
    m = 0.9 * m + 0.1 * g
    v = 0.95 * v + 0.05 * g * g
    step = m * lax.rsqrt(v + 1e-8) + 0.1 * w
    return (w - 0.02 * step).astype(jnp.bfloat16), m, v


def clipped(gradients, sum_of_squares, count):
    factor = jnp.minimum(1.0, 0.5 * lax.rsqrt(sum_of_squares / count + 1e-30))
    return [g * factor for g in gradients]


def stack(weights, h):
    for number in range(weights["w_gate"].shape[0]):
        h = layer(h, {name: w[number] for name, w in weights.items()})
    return h


def solution(mesh):
    groups = mesh.shape["rep"]

    def step(x, dy, *arrays):
        weights, m, v = (arrays[i : i + 3] for i in (0, 3, 6))
        x, dy = (t.reshape(groups, -1, *t.shape[1:]) for t in (x, dy))

        def of_a_group(x, dy):
            _, back = jax.vjp(lambda w: stack(w, x), dict(zip(NAMES, weights, strict=True)))
            by_weights = back(dy)[0]
            gradients = [by_weights[name].astype(jnp.float32) for name in NAMES]
            gradients = clipped(gradients, sum(jnp.sum(g * g) for g in gradients), sum(g.size for g in gradients))
            new = [adamw(w.astype(jnp.float32), m, v, g) for w, m, v, g in zip(weights, m, v, gradients, strict=True)]
            return tuple(one[which] for which in range(3) for one in new)

        return tuple(t.reshape(-1, *t.shape[2:]) for t in jax.vmap(of_a_group)(x, dy))

    return step
```

profile of v0, /device:TPU:0, one launch (start us, length us, event | category | flops | bytes accessed | tf_op | source)
XLA Modules:
  0.0 1618.6 jit_solution(15453062991119043267)
XLA Ops:
  16.2 14.2 fusion.71
  30.4 22.5 %fusion.69 = f32[2048,2560]{1,0:T(8,128)} fusion(bf16[2,896,2560]{2,1,0:T(8,128)(2,1)} %param.3, bf16[1,2048,896]{2,1,0:T(8,128)(2,1)} %param.2, f32[2048]{0:T(1024)S(1)} %add_rsqrt_fusion), kind=kOutput, calls=%fused_computation.77 | convolution fusion | flops 9400745984 | bytes 29237248 | tf_op jit(solution)/vmap(jvp())/dot_general | solution.py:21
  52.9 15.3 fusion.30
  68.3 15.2 fusion.43
  83.5 18.4 %fusion.60 = f32[2048,2560]{1,0:T(8,128)} fusion(bf16[2,896,2560]{2,1,0:T(8,128)(2,1)} %param, bf16[1,1,2048,896]{2,3,1,0:T(8,128)(2,1)S(1)} %get-tuple-element.66, f32[2048]{0:T(1024)S(1)} %bitcast.397), kind=kOutput, calls=%fused_computation.68 | convolution fusion | flops 9400745984 | bytes 29237248 | tf_op jit(solution)/vmap(jvp())/dot_general | solution.py:20
  101.9 17.6 %fusion.63 = f32[2048,2560]{1,0:T(8,128)} fusion(bf16[2,896,2560]{2,1,0:T(8,128)(2,1)} %param.3, bf16[1,1,2048,896]{2,3,1,0:T(8,128)(2,1)S(1)} %get-tuple-element.66, f32[2048]{0:T(1024)S(1)} %bitcast.398), kind=kOutput, calls=%fused_computation.71 | convolution fusion | flops 9400745984 | bytes 29237248 | tf_op jit(solution)/vmap(jvp())/dot_general | solution.py:21
  119.6 15.7 convolution_convert_fusion.1
  141.3 22.6 %fusion.10 = bf16[2048,2560]{1,0:T(8,128)(2,1)} fusion(f32[2048,2560]{1,0:T(8,128)} %fusion.60, f32[2048,2560]{1,0:T(8,128)} %fusion.63, bf16[2048,2560]{1,0:T(8,128)(2,1)} %convolution_convert_fusion.1), kind=kLoop, calls=%fused_computation.11 | loop fusion | flops 62914560 | bytes 62914560
  163.9 15.3 fusion.58
  179.1 20.5 %fusion.45 = (f32[2048]{0:T(1024)}, bf16[2048,896]{0,1:T(8,128)(2,1)}) fusion(bf16[1,1,2048,896]{2,3,1,0:T(8,128)(2,1)S(1)} %copy-done.4, bf16[2048,896]{0,1:T(8,128)(2,1)} %fusion.58, bf16[2,896,2560]{2,1,0:T(8,128)(2,1)} %param.3, bf16[2048,2560]{1,0:T(8,128)(2,1)} %convolution_convert_fusion.1, f32[2048,2560]{1,0:T(8,128)} %fusion.60), kind=kOutput, calls=%fused_computation.58 | convolution fusion | flops 9437706240 | bytes 47063040 | tf_op jit(solution)/vmap(transpose(jvp()))/dot_general | solution.py:21
  200.4 6.5 fusion.85
  207.0 15.7 convolution_bitcast_fusion
  222.7 22.2 %fusion.46 = f32[1,2560,896]{2,1,0:T(8,128)} fusion(f32[2048,2560]{1,0:T(8,128)} %fusion.63, f32[2048,2560]{1,0:T(8,128)} %fusion.60, bf16[1,2048,896]{2,1,0:T(8,128)(2,1)} %param.5), kind=kOutput, calls=%fused_computation.60 | convolution fusion | flops 9426698240 | bytes 54788096 | tf_op jit(solution)/vmap(transpose(jvp()))/dot_general | solution.py:9
  245.1 16.9 %convolution_convert_fusion = bf16[2048,2560]{1,0:T(8,128)(2,1)} fusion(bf16[2048,896]{0,1:T(8,128)(2,1)} %fusion.85, bf16[2,2560,896]{2,1,0:T(8,128)(2,1)} %param.4), kind=kOutput, calls=%fused_computation.39 | convolution fusion | flops 9400483840 | bytes 18743296 | tf_op jit(solution)/vmap(transpose(jvp()))/dot_general | solution.py:9
  262.0 19.2 %fusion.49 = f32[1,896,2560]{2,1,0:T(8,128)} fusion(bf16[2048,2560]{1,0:T(8,128)(2,1)} %convolution_convert_fusion.1, f32[2048,2560]{1,0:T(8,128)} %fusion.60, bf16[1,1,2048,896]{2,3,1,0:T(8,128)(2,1)} %copy-done.3, f32[2048]{0:T(1024)S(1)} %bitcast.400), kind=kOutput, calls=%fused_computation.61 | convolution fusion | flops 9432203264 | bytes 44310528 | tf_op jit(solution)/vmap(transpose(jvp()))/dot_general | solution.py:21
  281.1 19.5 %fusion.55 = f32[1,896,2560]{2,1,0:T(8,128)} fusion(bf16[2048,2560]{1,0:T(8,128)(2,1)} %convolution_convert_fusion, f32[2048,2560]{1,0:T(8,128)} %copy-done, bf16[1,2048,896]{1,2,0:T(8,128)(2,1)} %copy.11, f32[2048]{0:T(1024)S(1)} %copy-done.27), kind=kOutput, calls=%fused_computation.63 | convolution fusion | flops 9432203264 | bytes 44310528 | tf_op jit(solution)/vmap(transpose(jvp()))/dot_general | solution.py:21
  300.7 15.6 convolution_bitcast_fusion.1
  316.2 26.6 %fusion.52 = f32[1,896,2560]{2,1,0:T(8,128)} fusion(f32[2048,2560]{1,0:T(8,128)} %copy-done, f32[2048,2560]{1,0:T(8,128)} %fusion.69, bf16[2048,2560]{1,0:T(8,128)(2,1)} %convolution_convert_fusion, bf16[1,2048,896]{1,2,0:T(8,128)(2,1)} %copy.11, f32[2048]{0:T(1024)S(1)} %copy-done.27), kind=kOutput, calls=%fused_computation.62 | convolution fusion | flops 9458417664 | bytes 65282048 | tf_op jit(solution)/vmap(transpose(jvp()))/dot_general | solution.py:20
  342.8 690.2 %fusion.145 = (f32[16,2560]{1,0:T(8,128)S(1)}, f32[16,2560]{1,0:T(8,128)S(1)}, f32[16,2560]{1,0:T(8,128)S(1)}, f32[16,2560]{1,0:T(8,128)S(1)}) fusion(f32[1,896,2560]{2,1,0:T(8,128)} %fusion.52, f32[1,896,2560]{2,1,0:T(8,128)} %convolution_bitcast_fusion.1, f32[1,896,2560]{2,1,0:T(8,128)} %fusion.55, f32[1,896,2560]{2,1,0:T(8,128)} %fusion.49), kind=kCustom, calls=%all-reduce-scatter.4 | all-reduce-scatter fusion | flops 10485761 | bytes 37356032
  1042.8 8.4 collective-permute-start.15
  1058.6 8.6 collective-permute-start.21
  1082.6 7.6 collective-permute-start.28
  1139.8 7.5 concatenate.3
  1147.2 8.3 concatenate
  1155.7 13.9 concatenate.1
  1175.8 173.0 %all-reduce.10 = f32[1]{0:T(128)} all-reduce(f32[1]{0:T(128)} %bitcast.50), channel_id=3, replica_groups=mesh['rep'=2,'dp'=64] {'dp'}, use_global_device_ids=true, to_apply=%region_3.4.clone | all-reduce | flops 1 | bytes 8 | tf_op jit(solution)/vmap()/reduce_sum | solution.py:54
  1360.0 68.0 %all-gather.14.cloned.1.call-done = bf16[1,2,2560,896]{3,2,1,0:T(8,128)(2,1)} async-done(((bf16[1,2,40,896]{3,2,1,0:T(8,128)(2,1)}), bf16[1,2,2560,896]{3,2,1,0:T(8,128)(2,1)}) %all-gather.14.cloned.1.call-update) | async-done | bytes 9175056 | tf_op jit(solution)/reshape | solution.py:58
  1428.0 83.5 %all-gather.12.cloned.1.call-done = bf16[1,2,896,2560]{3,1,0,2:T(2,128)(2,1)} async-done(((bf16[1,2,14,2560]{3,1,0,2:T(2,128)(2,1)}), bf16[1,2,896,2560]{3,1,0,2:T(2,128)(2,1)}) %all-gather.12.cloned.1.call-update) | async-done | bytes 9175056 | tf_op jit(solution)/reshape | solution.py:58
  1511.4 8.7 copy.19
  1520.2 74.7 %all-gather.10.cloned.1.call-done = bf16[1,2,896,2560]{3,1,0,2:T(2,128)(2,1)} async-done(((bf16[1,2,14,2560]{3,1,0,2:T(2,128)(2,1)}), bf16[1,2,896,2560]{3,1,0,2:T(2,128)(2,1)}) %all-gather.10.cloned.1.call-update) | async-done | bytes 9175056 | tf_op jit(solution)/reshape | solution.py:58
  1594.9 8.7 copy.18
  1603.6 8.0 copy.65
  (172 shorter events, 110.8 us)
Async XLA Ops:
  7.2 1165.4 %reduce-scatter.31.cloned.1.call-start = ((), (), s32[]{:S(2)}) async-start(), calls=%async_computation.6 | async-start | bytes 9318400
  222.7 950.9 %reduce-scatter.29.cloned.1.call-start = ((), (), s32[]{:S(2)}) async-start(), calls=%async_computation.5 | async-start | bytes 9318400
  245.0 1183.0 %all-gather.14.cloned.1.call-start = ((), (), s32[]{:S(2)}) async-start(), calls=%async_computation.4 | async-start | bytes 9318400 | tf_op jit(solution)/reshape | solution.py:58
  1035.9 22.8 %collective-permute-start.16 = (bf16[16,2560]{1,0:T(8,128)(2,1)S(1)}, bf16[16,2560]{1,0:T(8,128)(2,1)S(1)}, u32[]{:S(2)}, u32[]{:S(2)}) collective-permute-start(bf16[16,2560]{1,0:T(8,128)(2,1)S(1)} %convert.100), channel_id=1, source_target_pairs={{0,1},{1,2},{2,3},{3,4},{4,5},{5,6},{6,7},{7,8},{8,9},{9,10},{10,1... | collective-permute-start | bytes 245768
  1037.2 30.1 %collective-permute-start.17 = (bf16[16,2560]{1,0:T(8,128)(2,1)S(1)}, bf16[16,2560]{1,0:T(8,128)(2,1)S(1)}, u32[]{:S(2)}, u32[]{:S(2)}) collective-permute-start(bf16[16,2560]{1,0:T(8,128)(2,1)S(1)} %convert.100), channel_id=1, source_target_pairs={{0,2},{1,3},{2,4},{3,5},{4,6},{5,7},{6,8},{7,9},{8,10},{9,11},{10,... | collective-permute-start | bytes 245768
  1038.5 34.4 %collective-permute-start.18 = (bf16[16,2560]{1,0:T(8,128)(2,1)S(1)}, bf16[16,2560]{1,0:T(8,128)(2,1)S(1)}, u32[]{:S(2)}, u32[]{:S(2)}) collective-permute-start(bf16[16,2560]{1,0:T(8,128)(2,1)S(1)} %convert.100), channel_id=1, source_target_pairs={{0,3},{1,4},{2,5},{3,6},{4,7},{5,8},{6,9},{7,10},{8,11},{9,12},{10... | collective-permute-start | bytes 245768
  1042.8 13.6 collective-permute-start.15
  1051.2 23.6 %collective-permute-start.19 = (bf16[16,2560]{1,0:T(8,128)(2,1)S(1)}, bf16[16,2560]{1,0:T(8,128)(2,1)S(1)}, u32[]{:S(2)}, u32[]{:S(2)}) collective-permute-start(bf16[16,2560]{1,0:T(8,128)(2,1)S(1)} %convert.100), channel_id=1, source_target_pairs={{0,4},{1,5},{2,6},{3,7},{4,8},{5,9},{6,10},{7,11},{8,12},{9,13},{1... | collective-permute-start | bytes 245768
  1056.4 21.8 %collective-permute-start.20 = (bf16[16,2560]{1,0:T(8,128)(2,1)S(1)}, bf16[16,2560]{1,0:T(8,128)(2,1)S(1)}, u32[]{:S(2)}, u32[]{:S(2)}) collective-permute-start(bf16[16,2560]{1,0:T(8,128)(2,1)S(1)} %convert.100), channel_id=1, source_target_pairs={{0,5},{1,6},{2,7},{3,8},{4,9},{5,10},{6,11},{7,12},{8,13},{9,14},{... | collective-permute-start | bytes 245768
  1058.6 22.6 %collective-permute-start.21 = (bf16[16,2560]{1,0:T(8,128)(2,1)S(1)}, bf16[16,2560]{1,0:T(8,128)(2,1)S(1)}, u32[]{:S(2)}, u32[]{:S(2)}) collective-permute-start(bf16[16,2560]{1,0:T(8,128)(2,1)S(1)} %convert.100), channel_id=1, source_target_pairs={{0,6},{1,7},{2,8},{3,9},{4,10},{5,11},{6,12},{7,13},{8,14},{9,15},... | collective-permute-start | bytes 245768
  1067.3 15.3 collective-permute-start.22
  1072.8 17.4 %collective-permute-start.24 = (bf16[16,2560]{1,0:T(8,128)(2,1)S(1)}, bf16[16,2560]{1,0:T(8,128)(2,1)S(1)}, u32[]{:S(2)}, u32[]{:S(2)}) collective-permute-start(bf16[16,2560]{1,0:T(8,128)(2,1)S(1)} %convert.101), channel_id=1, source_target_pairs={{0,1},{1,2},{2,3},{3,4},{4,5},{5,6},{6,7},{7,8},{8,9},{9,10},{10,1... | collective-permute-start | bytes 245768
  1074.9 18.0 %collective-permute-start.25 = (bf16[16,2560]{1,0:T(8,128)(2,1)S(1)}, bf16[16,2560]{1,0:T(8,128)(2,1)S(1)}, u32[]{:S(2)}, u32[]{:S(2)}) collective-permute-start(bf16[16,2560]{1,0:T(8,128)(2,1)S(1)} %convert.101), channel_id=1, source_target_pairs={{0,2},{1,3},{2,4},{3,5},{4,6},{5,7},{6,8},{7,9},{8,10},{9,11},{10,... | collective-permute-start | bytes 245768
  1078.2 19.2 %collective-permute-start.26 = (bf16[16,2560]{1,0:T(8,128)(2,1)S(1)}, bf16[16,2560]{1,0:T(8,128)(2,1)S(1)}, u32[]{:S(2)}, u32[]{:S(2)}) collective-permute-start(bf16[16,2560]{1,0:T(8,128)(2,1)S(1)} %convert.101), channel_id=1, source_target_pairs={{0,3},{1,4},{2,5},{3,6},{4,7},{5,8},{6,9},{7,10},{8,11},{9,12},{10... | collective-permute-start | bytes 245768
  1081.3 17.9 %collective-permute-start.27 = (bf16[16,2560]{1,0:T(8,128)(2,1)S(1)}, bf16[16,2560]{1,0:T(8,128)(2,1)S(1)}, u32[]{:S(2)}, u32[]{:S(2)}) collective-permute-start(bf16[16,2560]{1,0:T(8,128)(2,1)S(1)} %convert.101), channel_id=1, source_target_pairs={{0,4},{1,5},{2,6},{3,7},{4,8},{5,9},{6,10},{7,11},{8,12},{9,13},{1... | collective-permute-start | bytes 245768
  1082.6 20.0 %collective-permute-start.28 = (bf16[16,2560]{1,0:T(8,128)(2,1)S(1)}, bf16[16,2560]{1,0:T(8,128)(2,1)S(1)}, u32[]{:S(2)}, u32[]{:S(2)}) collective-permute-start(bf16[16,2560]{1,0:T(8,128)(2,1)S(1)} %convert.101), channel_id=1, source_target_pairs={{0,5},{1,6},{2,7},{3,8},{4,9},{5,10},{6,11},{7,12},{8,13},{9,14},{... | collective-permute-start | bytes 245768
  1090.2 17.7 %collective-permute-start.29 = (bf16[16,2560]{1,0:T(8,128)(2,1)S(1)}, bf16[16,2560]{1,0:T(8,128)(2,1)S(1)}, u32[]{:S(2)}, u32[]{:S(2)}) collective-permute-start(bf16[16,2560]{1,0:T(8,128)(2,1)S(1)} %convert.101), channel_id=1, source_target_pairs={{0,6},{1,7},{2,8},{3,9},{4,10},{5,11},{6,12},{7,13},{8,14},{9,15},... | collective-permute-start | bytes 245768
  1092.9 17.1 %collective-permute-start.30 = (bf16[16,2560]{1,0:T(8,128)(2,1)S(1)}, bf16[16,2560]{1,0:T(8,128)(2,1)S(1)}, u32[]{:S(2)}, u32[]{:S(2)}) collective-permute-start(bf16[16,2560]{1,0:T(8,128)(2,1)S(1)} %convert.101), channel_id=1, source_target_pairs={{0,7},{1,8},{2,9},{3,10},{4,11},{5,12},{6,13},{7,14},{8,15},{9,16}... | collective-permute-start | bytes 245768
  1097.5 14.1 collective-permute-start
  1099.2 15.9 collective-permute-start.1
  1102.6 14.4 collective-permute-start.2
  1108.0 11.5 collective-permute-start.3
  1111.6 11.9 collective-permute-start.5
  1117.0 11.6 collective-permute-start.10
  1119.5 12.5 collective-permute-start.11
  1121.5 34.1 %collective-permute-start.12 = (bf16[16,2560]{1,0:T(8,128)(2,1)}, bf16[16,2560]{1,0:T(8,128)(2,1)}, u32[]{:S(2)}, u32[]{:S(2)}) collective-permute-start(bf16[16,2560]{1,0:T(8,128)(2,1)} %convert.103), channel_id=1, source_target_pairs={{0,5},{1,6},{2,7},{3,8},{4,9},{5,10},{6,11},{7,12},{8,13},{9,14},{... | collective-permute-start | bytes 245768
  1123.5 32.1 %collective-permute-start.13 = (bf16[16,2560]{1,0:T(8,128)(2,1)}, bf16[16,2560]{1,0:T(8,128)(2,1)}, u32[]{:S(2)}, u32[]{:S(2)}) collective-permute-start(bf16[16,2560]{1,0:T(8,128)(2,1)} %convert.103), channel_id=1, source_target_pairs={{0,6},{1,7},{2,8},{3,9},{4,10},{5,11},{6,12},{7,13},{8,14},{9,15},... | collective-permute-start | bytes 245768
  1126.3 29.4 %collective-permute-start.14 = (bf16[16,2560]{1,0:T(8,128)(2,1)}, bf16[16,2560]{1,0:T(8,128)(2,1)}, u32[]{:S(2)}, u32[]{:S(2)}) collective-permute-start(bf16[16,2560]{1,0:T(8,128)(2,1)} %convert.103), channel_id=1, source_target_pairs={{0,7},{1,8},{2,9},{3,10},{4,11},{5,12},{6,13},{7,14},{8,15},{9,16}... | collective-permute-start | bytes 245768
  1128.6 27.0 %collective-permute-start.8 = (bf16[16,2560]{1,0:T(8,128)(2,1)}, bf16[16,2560]{1,0:T(8,128)(2,1)}, u32[]{:S(2)}, u32[]{:S(2)}) collective-permute-start(bf16[16,2560]{1,0:T(8,128)(2,1)} %convert.103), channel_id=1, source_target_pairs={{0,1},{1,2},{2,3},{3,4},{4,5},{5,6},{6,7},{7,8},{8,9},{9,10},{10,1... | collective-permute-start | bytes 245768
  1132.0 23.6 %collective-permute-start.9 = (bf16[16,2560]{1,0:T(8,128)(2,1)}, bf16[16,2560]{1,0:T(8,128)(2,1)}, u32[]{:S(2)}, u32[]{:S(2)}) collective-permute-start(bf16[16,2560]{1,0:T(8,128)(2,1)} %convert.103), channel_id=1, source_target_pairs={{0,2},{1,3},{2,4},{3,5},{4,6},{5,7},{6,8},{7,9},{8,10},{9,11},{10,... | collective-permute-start | bytes 245768
  1351.5 159.9 %all-gather.12.cloned.1.call-start = ((), (), s32[]{:S(2)}) async-start(), calls=%async_computation.3 | async-start | bytes 9318400 | tf_op jit(solution)/reshape | solution.py:58
  1353.8 241.2 %all-gather.10.cloned.1.call-start = ((), (), s32[]{:S(2)}) async-start(), calls=%async_computation.2 | async-start | bytes 9318400 | tf_op jit(solution)/reshape | solution.py:58
  (37 other events, 2240.2 us)
Sparse Core Ops, SparseCore 0:
  222.8 394.9 reduce-scatter.30
  620.2 396.4 reduce-scatter.28
  1351.6 76.3 all-gather.13
  1431.3 80.1 all-gather.11
  1514.7 80.1 all-gather.9
where the time goes:
time: 1630 us; the launch traced here: 1620 us
  blocking collectives  863 us (53%)
  matrix products  275 us (17%)
  waiting for transfers between devices  226 us (14%)
  starting transfers between devices  102 us (6%)
  local copies, waits for them, and re-layouts  76.1 us (5%)
  other arithmetic  56.6 us (3%)
  between operations  19.1 us (1%)
    unnamed x1, blocking collectives  690 us
    reshape x3, waiting for transfers between devices, step(): t.reshape(-1, *t.shape[2:])  226 us
    reduce_sum x1, blocking collectives, of_a_group(): jnp.sum(g * g)  173 us
    unnamed x34, starting transfers between devices  102 us
    dot_general x5, matrix products, layer(): up = jnp.dot(a, w['w_up'], preferred_element_type=jnp.float32)  99.4 us
    dot_general x5, matrix products, layer(): gate = jnp.dot(a, w['w_gate'], preferred_element_type=jnp.float32)  90 us
    dot_general x5, matrix products, matmul(): jnp.dot(a, w, preferred_element_type=jnp.float32).astype(jnp.bfloat16)  85.7 us
    unnamed x81, local copies, waits for them, and re-layouts  72.8 us
  transfers between devices with their start and end apart: 37, of which 3 were waited for; matrix products, arithmetic and copies ran while one was open for 53% of the time, Pallas kernels for 0%

commit v1 on v0

v1 whole, which is shorter than its diff:
```python
import functools
import jax
import jax.numpy as jnp
from jax import lax
from jax.experimental import pallas as pl
from jax.experimental.pallas import tpu as pltpu
from jax.sharding import PartitionSpec as P

MESH = pl.DeviceIdType.MESH
STRIDE = (16, 4, 1)
ORDERS = ((0, 1, 2), (0, 1, 2), (1, 2, 0), (1, 2, 0), (2, 0, 1), (2, 0, 1))
SIGNS = (1, -1, 1, -1, 1, -1)


def place():
    me = lax.axis_index("dp")
    return (me // 16, (me // 4) % 4, me % 4)


def neighbour(at, axis, step):
    there = [c for c in at]
    there[axis] = (at[axis] + step + 4) % 4
    return {"dp": there[0] * 16 + there[1] * 4 + there[2]}


def remote(src, dst, send, recv, to):
    return pltpu.make_async_remote_copy(src_ref=src, dst_ref=dst, send_sem=send, recv_sem=recv, device_id=to, device_id_type=MESH)


def enter(at):
    barrier = pltpu.get_barrier_semaphore()
    for axis in range(3):
        for step in range(1, 4):
            pl.semaphore_signal(barrier, inc=1, device_id=neighbour(at, axis, step), device_id_type=MESH)
    pl.semaphore_wait(barrier, 9)


def norm_exchange(at, buf, send, recv, total):
    for axis in range(3):
        buf[axis, 3] = total
        for off in range(1, 4):
            remote(buf.at[axis, 3], buf.at[axis, off - 1], send.at[axis], recv.at[axis, off - 1], neighbour(at, axis, off)).start()
        for off in range(1, 4):
            remote(buf.at[axis, 3], buf.at[axis, off - 1], send.at[axis], recv.at[axis, off - 1], neighbour(at, axis, off)).wait_recv()
            total = total + buf[axis, off - 1]
    return total


def rs_kernel(*refs):
    terms, (out, squares), scratch = refs[:6], refs[6:8], refs[8:]
    r1, r2, r3, own, f1, f2, sums, send1, send2, send3, recv1, recv2, recv3, load, send4, recv4 = scratch
    at = place()
    enter(at)

    def block(c, a, i):
        o = ORDERS[c]
        index = [slice(None)] * 3
        index[o[0]] = a
        index[o[1]] = i
        return terms[c].at[tuple(index)]

    def split(c):
        o, s = ORDERS[c], SIGNS[c]
        return o, s, at[o[0]], at[o[1]], at[o[2]]

    def first(c, step, j):
        o, s, p1, p2, p3 = split(c)
        i = (p2 - s * (1 + j) + 8) % 4
        src = block(c, (p1 - s + 4) % 4, i) if step == 0 else r1.at[c, step - 1, j]
        return remote(src, r1.at[c, step, j], send1.at[c], recv1.at[c, step, j], neighbour(at, o[0], s))

    def loading(c, step, j):
        o, s, p1, p2, p3 = split(c)
        i = (p2 - s * (1 + j) + 8) % 4
        return pltpu.make_async_copy(block(c, (p1 - s * (2 + step) + 12) % 4, i), own.at[c, step, j], load.at[c, step, j])

    def second(c, step, k):
        o, s, p1, p2, p3 = split(c)
        i = (p3 - s * (1 + k) + 8) % 4
        src = r1.at[c, 2, 0, i] if step == 0 else r2.at[c, step - 1, k]
        return remote(src, r2.at[c, step, k], send2.at[c], recv2.at[c, step, k], neighbour(at, o[1], s))

    def third(c, step):
        o, s, p1, p2, p3 = split(c)
        src = r2.at[c, 2, 0] if step == 0 else r3.at[c, step - 1]
        return remote(src, r3.at[c, step], send3.at[c], recv3.at[c, step], neighbour(at, o[2], s))

    for j in range(4):
        for c in range(6):
            first(c, 0, j).start()
    for step in range(3):
        for j in range(4):
            for c in range(6):
                loading(c, step, j).start()

    for step in range(3):
        for j in range(4):
            for c in range(6):
                first(c, step, j).wait_recv()
                loading(c, step, j).wait()
                for k in range(4):
                    both = r1[c, step, j, k].astype(jnp.float32) + own[c, step, j, k].astype(jnp.float32)
                    if step == 2 and j == 3:
                        f1[c, k] = both
                    r1[c, step, j, k] = both.astype(jnp.bfloat16)
                if step < 2:
                    first(c, step + 1, j).start()
                elif j == 0:
                    for k in range(4):
                        second(c, 0, k).start()
    for step in range(3):
        for k in range(4):
            for c in range(6):
                o, s, p1, p2, p3 = split(c)
                i = (p3 - s * (1 + k) + 8) % 4
                second(c, step, k).wait_recv()
                if step < 2:
                    both = r2[c, step, k].astype(jnp.float32) + r1[c, 2, step + 1, i].astype(jnp.float32)
                else:
                    both = r2[c, step, k].astype(jnp.float32) + f1[c, i]
                if step == 2 and k == 3:
                    f2[c] = both
                r2[c, step, k] = both.astype(jnp.bfloat16)
                if step < 2:
                    second(c, step + 1, k).start()
                elif k == 0:
                    third(c, 0).start()
    for step in range(3):
        for c in range(6):
            third(c, step).wait_recv()
            if step < 2:
                both = r3[c, step].astype(jnp.float32) + r2[c, 2, step + 1].astype(jnp.float32)
                r3[c, step] = both.astype(jnp.bfloat16)
                third(c, step + 1).start()
            else:
                out[c] = (r3[c, step].astype(jnp.float32) + f2[c]).astype(jnp.bfloat16)
    total = jnp.zeros((8, 128), jnp.float32)
    for c in range(6):
        g = out[c].astype(jnp.float32)
        total = total + jnp.sum((g * g).reshape(-1, 8, 128), axis=0)
    squares[...] = norm_exchange(at, sums, send4, recv4, total)

    for c in range(6):
        pltpu.make_async_copy(r1.at[c], r1.at[c], send1.at[c]).wait()
        pltpu.make_async_copy(r2.at[c], r2.at[c], send2.at[c]).wait()
        pltpu.make_async_copy(r3.at[c], r3.at[c], send3.at[c]).wait()
    for axis in range(3):
        pltpu.make_async_copy(sums.at[axis, pl.ds(0, 3)], sums.at[axis, pl.ds(0, 3)], send4.at[axis]).wait()


def reduce_scatter(terms):
    rows = terms[0].shape[3]
    bf16, f32 = jnp.bfloat16, jnp.float32
    dma = pltpu.SemaphoreType.DMA
    return pl.pallas_call(
        rs_kernel,
        out_shape=(jax.ShapeDtypeStruct((6, rows, 128), bf16), jax.ShapeDtypeStruct((8, 128), f32)),
        in_specs=[pl.BlockSpec(memory_space=pl.ANY)] * 6,
        out_specs=(pl.BlockSpec(memory_space=pltpu.VMEM), pl.BlockSpec(memory_space=pltpu.VMEM)),
        scratch_shapes=[
            pltpu.VMEM((6, 3, 4, 4, rows, 128), bf16),
            pltpu.VMEM((6, 3, 4, rows, 128), bf16),
            pltpu.VMEM((6, 3, rows, 128), bf16),
            pltpu.VMEM((6, 3, 4, 4, rows, 128), bf16),
            pltpu.VMEM((6, 4, rows, 128), f32),
            pltpu.VMEM((6, rows, 128), f32),
            pltpu.VMEM((3, 4, 8, 128), f32),
            dma((6,)), dma((6,)), dma((6,)),
            dma((6, 3, 4)), dma((6, 3, 4)), dma((6, 3)),
            dma((6, 3, 4)),
            dma((3,)), dma((3, 3)),
        ],
        compiler_params=pltpu.CompilerParams(collective_id=0, has_side_effects=True, vmem_limit_bytes=60 * 1024 * 1024),
        name="scatter",
    )(*terms)


def ag_order(latency=1.8):
    import heapq

    free, out, seen, count = {}, [], [], 0
    heap = []

    def send(t, c, phase, key, size):
        nonlocal count
        axis = ORDERS[2 * c][2 - phase]
        start = max(t, free.get(axis, 0.0))
        free[axis] = start + size
        count += 1
        heapq.heappush(heap, (start + size + latency, count, c, phase, key))

    def hold(t, c, phase, key):
        d1, d2, d3 = key
        if phase == 0 and d3 < 3:
            send(t, c, 0, (0, 0, d3 + 1), 1)
        if phase <= 1 and d2 < 3:
            send(t, c, 1, (0, d2 + 1, d3), 1)
        if d2 == 0 or phase == 2:
            if d1 < 3:
                send(t, c, 2, (d1 + 1, d2, d3), 1 if d3 is not None else 4)
        elif phase == 1:
            seen.append((c, d2))
            if seen.count((c, d2)) == 4:
                send(t, c, 2, (1, d2, None), 4)

    for c in range(3):
        hold(0.0, c, 0, (0, 0, 0))
    while heap:
        t, _, c, phase, key = heapq.heappop(heap)
        out.append((c, phase, key))
        hold(t, c, phase, key)
    return out, t


def ag_kernel(*refs):
    mine, outs, scratch = refs[0], refs[1:7], refs[7:]
    sends, recv1, recv2, recv3, recv4, local = scratch
    at = place()
    enter(at)

    def where(c, d1, d2, d3):
        o, s = ORDERS[c], SIGNS[c]
        index = [None] * 3
        for axis, d in zip(o, (d1, d2, d3), strict=True):
            index[axis] = slice(None) if d is None else (at[axis] - s * d + 4) % 4
        return outs[c].at[tuple(index)]

    def copy(c, phase, key, of_receiver):
        o, s = ORDERS[c], SIGNS[c]
        d1, d2, d3 = key
        back = [d1, d2, d3]
        if not of_receiver:
            back[2 - phase] -= 1
        place_there = where(c, *back)
        src = mine.at[c] if not of_receiver and tuple(back) == (0, 0, 0) else place_there
        if phase == 0:
            recv = recv1.at[c, d3 - 1]
        elif phase == 1:
            recv = recv2.at[c, d2 - 1, d3]
        elif d3 is not None:
            recv = recv3.at[c, d1 - 1, d3]
        else:
            recv = recv4.at[c, d1 - 1, d2 - 1]
        return remote(src, place_there, sends.at[c, phase], recv, neighbour(at, o[2 - phase], s))

    seen = []

    def hold(c, phase, key):
        d1, d2, d3 = key
        todo = []
        if phase == 0 and d3 < 3:
            todo.append((0, (0, 0, d3 + 1)))
        if phase <= 1 and d2 < 3:
            todo.append((1, (0, d2 + 1, d3)))
        if d2 == 0 or phase == 2:
            if d1 < 3:
                todo.append((2, (d1 + 1, d2, d3)))
        elif phase == 1:
            seen.append((c, d2))
            if seen.count((c, d2)) == 4:
                todo.append((2, (1, d2, None)))
        for phase, key in todo:
            copy(c, phase, key, False).start()

    for c in range(6):
        hold(c, 0, (0, 0, 0))
    for c in range(6):
        pltpu.make_async_copy(mine.at[c], where(c, 0, 0, 0), local.at[c]).start()
    for pair, phase, key in ag_order()[0]:
        for c in (2 * pair, 2 * pair + 1):
            copy(c, phase, key, True).wait_recv()
            hold(c, phase, key)
    for c in range(6):
        pltpu.make_async_copy(mine.at[c], where(c, 0, 0, 0), local.at[c]).wait()
        pltpu.make_async_copy(outs[c].at[0, 0, pl.ds(0, 3)], outs[c].at[0, 0, pl.ds(0, 3)], sends.at[c, 0]).wait()
        pltpu.make_async_copy(outs[c].at[0, pl.ds(0, 3)], outs[c].at[0, pl.ds(0, 3)], sends.at[c, 1]).wait()
        pltpu.make_async_copy(outs[c].at[pl.ds(0, 3)], outs[c].at[pl.ds(0, 3)], sends.at[c, 2]).wait()


def all_gather(mine):
    rows = mine.shape[1]
    dma = pltpu.SemaphoreType.DMA
    return pl.pallas_call(
        ag_kernel,
        out_shape=tuple(jax.ShapeDtypeStruct((4, 4, 4, rows, 128), jnp.bfloat16) for _ in range(6)),
        in_specs=[pl.BlockSpec(memory_space=pltpu.VMEM)],
        out_specs=tuple(pl.BlockSpec(memory_space=pl.ANY) for _ in range(6)),
        scratch_shapes=[dma((6, 3)), dma((6, 3)), dma((6, 3, 4)), dma((6, 3, 4)), dma((6, 3, 3)), dma((6,))],
        compiler_params=pltpu.CompilerParams(collective_id=1, has_side_effects=True),
        name="gather",
    )(mine)


NAMES = ("w_gate", "w_up", "w_down")
LANES = 128


def tiles_of(t, rows, columns):
    n = columns // LANES
    if t < 2:
        return [(0, rows, j * LANES, j * rows) for j in range(n)]
    return [(8 * i, 8, j * LANES, (i * n + j) * 8) for i in range(rows // 8) for j in range(n)]


def adam_kernel(count, g, total, *refs):
    ws, ms, vs, new, new_m, new_v, wide_g, wide_w = refs[0:3], refs[3:6], refs[6:9], refs[9], refs[10:13], refs[13:16], refs[16], refs[17]
    factor = jnp.minimum(1.0, 0.5 * lax.rsqrt(jnp.full((1, 1), jnp.sum(total[...])) / count + 1e-30))
    for t in range(3):
        for l in range(2):
            c = 2 * t + l
            wide_g[...] = g[c].astype(jnp.float32) * factor
            for row, rows, column, at in tiles_of(t, *ms[t].shape[1:]):
                here = (l, pl.ds(row, rows), pl.ds(column, LANES))
                grad = wide_g[pl.ds(at, rows), :]
                m = 0.9 * ms[t][here] + 0.1 * grad
                v = 0.95 * vs[t][here] + 0.05 * grad * grad
                w = ws[t][here].astype(jnp.float32)
                new_m[t][here] = m
                new_v[t][here] = v
                wide_w[pl.ds(at, rows), :] = w - 0.02 * (m * lax.rsqrt(v + 1e-8) + 0.1 * w)
            new[c] = wide_w[...].astype(jnp.bfloat16)


def adam(count, g, total, ws, ms, vs):
    vmem = pl.BlockSpec(memory_space=pltpu.VMEM)
    like = [jax.ShapeDtypeStruct(m.shape, jnp.float32) for m in ms]
    out = pl.pallas_call(
        functools.partial(adam_kernel, count),
        out_shape=(jax.ShapeDtypeStruct(g.shape, jnp.bfloat16), *like, *like),
        in_specs=[vmem] * 11,
        out_specs=(vmem,) * 7,
        scratch_shapes=[pltpu.VMEM(g.shape[1:], jnp.float32)] * 2,
        name="adam",
    )(g, total, *ws, *ms, *vs)
    return out[0], out[1:4], out[4:7]


def natural_kernel(*refs):
    blocks, outs, wide = refs[:6], refs[6:9], refs[9:]
    for t in range(3):
        for l in range(2):
            for z in range(4):
                block = blocks[2 * t + l][z].astype(jnp.float32)
                rows = outs[t].shape[1] // 4
                for row, n, column, at in tiles_of(t, rows, outs[t].shape[2]):
                    wide[t][pl.ds(z * rows + row, n), pl.ds(column, LANES)] = block[at : at + n]
            outs[t][l] = wide[t][...].astype(jnp.bfloat16)


def natural(blocks):
    blocks = [b.reshape(64, *b.shape[3:]) for b in blocks]
    shapes = ((2, 896, 2560), (2, 896, 2560), (2, 2560, 896))
    return pl.pallas_call(
        natural_kernel,
        grid=(16,),
        out_shape=tuple(jax.ShapeDtypeStruct(s, jnp.bfloat16) for s in shapes),
        in_specs=[pl.BlockSpec((4, 280, 128), lambda i: (i, 0, 0))] * 6,
        out_specs=tuple(pl.BlockSpec((2, s[1] // 16, s[2]), lambda i: (0, i, 0)) for s in shapes),
        scratch_shapes=[pltpu.VMEM((s[1] // 16, s[2]), jnp.float32) for s in shapes],
        name="natural",
    )(*blocks)


def matmul(a, w):
    return jnp.dot(a, w, preferred_element_type=jnp.float32).astype(jnp.bfloat16)


def normed(h):
    wide = h.astype(jnp.float32)
    scale = lax.rsqrt(jnp.mean(wide**2, -1, keepdims=True) + 1e-6)
    return (wide * scale).astype(jnp.bfloat16)


def layer(h, w):
    a = normed(h)
    gate = jnp.dot(a, w["w_gate"], preferred_element_type=jnp.float32)
    up = jnp.dot(a, w["w_up"], preferred_element_type=jnp.float32)
    return h + matmul((jax.nn.silu(gate) * up).astype(jnp.bfloat16), w["w_down"])


def stack(weights, h):
    for number in range(2):
        h = layer(h, {name: w[number] for name, w in weights.items()})
    return h


def in_blocks(t, g):
    if t < 2:
        g = g.reshape(64, 14, 20, LANES).transpose(0, 2, 1, 3)
    else:
        g = g.reshape(64, 5, 8, 7, LANES).transpose(0, 1, 3, 2, 4)
    return g.reshape(4, 4, 4, 280, LANES)


def solution(mesh):
    rep, dp = mesh.axis_names

    def step(x, dy, *arrays):
        weights, m, v = (arrays[i : i + 3] for i in (0, 3, 6))
        _, back = jax.vjp(lambda w: stack(w, x[0]), dict(zip(NAMES, weights, strict=True)))
        by_weights = back(dy[0])[0]
        terms = [in_blocks(t, by_weights[NAMES[t]][l]) for t in range(3) for l in range(2)]
        g, total = reduce_scatter(terms)
        me = lax.axis_index(dp)
        mine = [lax.dynamic_slice_in_dim(w, me * b.shape[1], b.shape[1], 1) for w, b in zip(weights, m, strict=True)]
        new, new_m, new_v = adam(sum(w.size for w in weights), g, total, mine, m, v)
        return (*natural(all_gather(new)), *new_m, *new_v)

    whole, rows, sequences = P(None, None, None), P(None, dp, None), P((rep, dp), None, None)
    return jax.shard_map(
        step,
        mesh=mesh,
        in_specs=(sequences, sequences, *[whole] * 3, *[rows] * 6),
        out_specs=(*[P(rep, None, None)] * 3, *[P(rep, dp, None)] * 6),
        check_vma=False,
    )
```

time: 1630 us -> 676 us (0.41)
  blocking collectives: 863 us -> 0 us
  Pallas kernels: 0 us -> 254 us
  waiting for transfers between devices: 226 us -> 0 us
  starting transfers between devices: 102 us -> 0 us
  other arithmetic: 56.6 us -> 29.8 us
  between operations: 19.1 us -> 1.13 us
  local copies, waits for them, and re-layouts: 76.1 us -> 93.4 us
    unnamed x1 -> x0, blocking collectives: 690 us -> none
    pallas_call x0 -> x4, Pallas kernels: none -> 254 us  [the longest x1 125 us: reduce_scatter(): pl.pallas_call(rs_kernel, out_shape=(jax.ShapeDtypeStruct((6, rows, 128),...]
    reshape x3 -> x0, waiting for transfers between devices: 226 us -> none  [step(): t.reshape(-1, *t.shape[2:])]
    reduce_sum x1 -> x0, blocking collectives: 173 us -> none  [of_a_group(): jnp.sum(g * g)]
    unnamed x34 -> x0, starting transfers between devices: 102 us -> none
    unnamed x81 -> x50, local copies, waits for them, and re-layouts: 72.8 us -> 19.1 us
    unnamed x8 -> x1, other arithmetic: 45.1 us -> 0.01 us
    another operation x1 -> x4, local copies, waits for them, and re-layouts: 0.65 us -> 35.2 us  [in_blocks(): g = g.reshape(64, 14, 20, LANES).transpose(0, 2, 1, 3)]
  transfers between devices with their start and end apart: 37 -> 0, of which waited for: 3 -> 0; matrix products, arithmetic and copies ran while one was open for 53% -> 0% of each run, Pallas kernels for 0% -> 0%
where the time goes in v1:
time: 676 us; the launch traced here: 668 us
  matrix products  289 us (43%)
  Pallas kernels  254 us (38%)
  local copies, waits for them, and re-layouts  93.4 us (14%)
  other arithmetic  29.8 us (4%)
    pallas_call x1, Pallas kernels, reduce_scatter(): pl.pallas_call(rs_kernel, out_shape=(jax.ShapeDtypeStruct((6, rows, 128),...  125 us
    dot_general x5, matrix products, layer(): gate = jnp.dot(a, w['w_gate'], preferred_element_type=jnp.float32)  106 us
    pallas_call x1, Pallas kernels, all_gather(): pl.pallas_call(ag_kernel, out_shape=tuple((jax.ShapeDtypeStruct((4, 4, 4,...  101 us
    dot_general x5, matrix products, layer(): up = jnp.dot(a, w['w_up'], preferred_element_type=jnp.float32)  98.7 us
    dot_general x5, matrix products, matmul(): jnp.dot(a, w, preferred_element_type=jnp.float32).astype(jnp.bfloat16)  84.6 us
    another operation x4, local copies, waits for them, and re-layouts, in_blocks(): g = g.reshape(64, 14, 20, LANES).transpose(0, 2, 1, 3)  35.2 us
    pallas_call x1, Pallas kernels, natural(): pl.pallas_call(natural_kernel, grid=(16,), out_shape=tuple((jax.ShapeDtyp...  24.8 us
    reshape x4, local copies, waits for them, and re-layouts, in_blocks(): return g.reshape(4, 4, 4, 280, LANES)  20.3 us

profile of v1, /device:TPU:0, one launch (start us, length us, event | category | flops | bytes accessed | tf_op | source)
XLA Modules:
  0.0 667.6 jit_solution(12168220267354431151)
XLA Ops:
  0.6 6.1 copy.34
  9.6 18.3 %fusion.52 = f32[2048,2560]{1,0:T(8,128)} fusion(bf16[2,896,2560]{2,1,0:T(8,128)(2,1)} %param.13, bf16[1,2048,896]{2,1,0:T(8,128)(2,1)} %param.11, f32[2048]{0:T(1024)S(1)} %add_rsqrt_fusion), kind=kOutput, calls=%fused_computation.78 | convolution fusion | flops 9400745984 | bytes 29237248 | tf_op jit(solution)/shard_map/jvp()/dot_general | solution.py:376
  27.9 24.6 %multiply_convert_fusion.1 = (bf16[2048,2560]{1,0:T(8,128)(2,1)}, f32[2048,2560]{1,0:T(8,128)}) fusion(f32[2048,2560]{1,0:T(8,128)} %fusion.52, bf16[2,896,2560]{2,1,0:T(8,128)(2,1)} %param.14, bf16[1,2048,896]{2,1,0:T(8,128)(2,1)S(1)} %copy-done.1, f32[2048]{0:T(1024)S(1)} %add_rsqrt_fusion), kind=kOutput, calls=%fused_computation.17 | convolution fusion | flops 9432203264 | bytes 60694528 | tf_op jit(solution)/shard_map/jvp()/dot_general | solution.py:377
  52.5 14.8 %fusion.19 = (f32[2048]{0:T(1024)S(1)}, bf16[2048,896]{0,1:T(8,128)(2,1)S(1)}) fusion(bf16[2048,2560]{1,0:T(8,128)(2,1)} %get-tuple-element.69, bf16[2,2560,896]{2,1,0:T(8,128)(2,1)} %param.15, bf16[1,2048,896]{1,2,0:T(8,128)(2,1)S(1)} %copy-done), kind=kOutput, calls=%fused_computation.43 | convolution fusion | flops 9404413952 | bytes 22421504 | tf_op jit(solution)/shard_map/jvp()/dot_general | solution.py:365
  67.4 18.4 %fusion.44 = f32[2048,2560]{1,0:T(8,128)} fusion(bf16[2,896,2560]{2,1,0:T(8,128)(2,1)} %param.14, bf16[2048,896]{0,1:T(8,128)(2,1)S(1)} %get-tuple-element.72, f32[2048]{0:T(1024)S(1)} %fusion.80), kind=kOutput, calls=%fused_computation.70 | convolution fusion | flops 9400745984 | bytes 29237248 | tf_op jit(solution)/shard_map/jvp()/dot_general | solution.py:377
  85.8 16.3 %convolution_convert_fusion.1 = bf16[2048,2560]{1,0:T(8,128)(2,1)} fusion(bf16[2,2560,896]{2,1,0:T(8,128)(2,1)} %param.15, bf16[1,2048,896]{2,1,0:T(8,128)(2,1)S(1)} %copy-done.2), kind=kOutput, calls=%fused_computation.27 | convolution fusion | flops 9400483840 | bytes 18743296 | tf_op jit(solution)/shard_map/transpose(jvp())/dot_general | solution.py:365
  102.0 31.5 %fusion.2 = (bf16[2048,2560]{1,0:T(8,128)(2,1)}, f32[2048,2560]{1,0:T(8,128)}) fusion(f32[2048,2560]{1,0:T(8,128)} %fusion.44, bf16[2048,2560]{1,0:T(8,128)(2,1)} %convolution_convert_fusion.1, bf16[2,896,2560]{2,1,0:T(8,128)(2,1)} %param.13, bf16[2048,896]{0,1:T(8,128)(2,1)} %copy-done.3, f32[2048]{0:T(1024)S(1)} %fusion.80), kind=kOutput, calls=%fused_computation.8 | convolution fusion | flops 9463660544 | bytes 71180288 | tf_op jit(solution)/shard_map/jvp()/dot_general | solution.py:376
  133.6 21.8 %fusion.28 = bf16[1,2560,896]{2,1,0:T(8,128)(2,1)} fusion(f32[2048,2560]{1,0:T(8,128)} %fusion.44, bf16[1,2048,896]{2,1,0:T(8,128)(2,1)} %param.12, f32[2048,2560]{1,0:T(8,128)} %get-tuple-element.74), kind=kOutput, calls=%fused_computation.53 | convolution fusion | flops 9428992000 | bytes 50200576 | tf_op jit(solution)/shard_map/transpose(jvp())/dot_general | solution.py:365
  155.4 18.2 %fusion.12 = bf16[2048,896]{0,1:T(8,128)(2,1)} fusion(bf16[2048,2560]{1,0:T(8,128)(2,1)} %convolution_convert_fusion.1, bf16[2,896,2560]{2,1,0:T(8,128)(2,1)} %param.14, f32[2048,2560]{1,0:T(8,128)} %get-tuple-element.74), kind=kOutput, calls=%fused_computation.21 | convolution fusion | flops 9426698240 | bytes 39714816 | tf_op jit(solution)/shard_map/transpose(jvp())/dot_general | solution.py:377
  173.6 17.1 %fusion.21 = (f32[2048]{0:T(1024)S(1)}, bf16[2048,896]{0,1:T(8,128)(2,1)}) fusion(bf16[2048,896]{0,1:T(8,128)(2,1)} %copy-done.3, bf16[2048,896]{0,1:T(8,128)(2,1)} %fusion.12, bf16[2048,2560]{1,0:T(8,128)(2,1)} %get-tuple-element.73, bf16[2,896,2560]{2,1,0:T(8,128)(2,1)} %param.13), kind=kOutput, calls=%fused_computation.45 | convolution fusion | flops 9404413952 | bytes 26091520 | tf_op jit(solution)/shard_map/transpose(jvp())/dot_general | solution.py:376
  190.7 6.1 copy.35
  196.7 6.9 %fusion.64 = bf16[2048,896]{0,1:T(8,128)(2,1)S(1)} fusion(bf16[2048,896]{0,1:T(8,128)(2,1)} %copy-done.3, bf16[2048,896]{0,1:T(8,128)(2,1)} %get-tuple-element.76, bf16[1,2048,896]{1,2,0:T(8,128)(2,1)} %copy.35, f32[2048]{0:T(1024)S(1)} %multiply_multiply_fusion, f32[2048]{0:T(1024)S(1)} %fusion.80), kind=kLoop, calls=%fused_computation.90 | loop fusion | flops 12845056 | bytes 14696448 | tf_op jit(solution)/shard_map/transpose(jvp())/add_any | solution.py:369
  203.6 15.3 %fusion.32 = bf16[1,2560,896]{2,1,0:T(8,128)(2,1)S(1)} fusion(bf16[2048,2560]{1,0:T(8,128)(2,1)} %get-tuple-element.69, bf16[2048,896]{0,1:T(8,128)(2,1)S(1)} %fusion.64), kind=kOutput, calls=%fused_computation.57 | convolution fusion | flops 9397534720 | bytes 18743296 | tf_op jit(solution)/shard_map/transpose(jvp())/dot_general | solution.py:365
  222.8 18.9 %fusion.30 = bf16[1,896,2560]{2,1,0:T(8,128)(2,1)} fusion(bf16[2048,2560]{1,0:T(8,128)(2,1)} %convolution_convert_fusion.1, bf16[2048,896]{0,1:T(8,128)(2,1)} %copy-done.3, f32[2048]{0:T(1024)S(1)} %fusion.80, f32[2048,2560]{1,0:T(8,128)} %get-tuple-element.74), kind=kOutput, calls=%fused_computation.55 | convolution fusion | flops 9434497024 | bytes 39723008 | tf_op jit(solution)/shard_map/transpose(jvp())/dot_general | solution.py:377
  241.8 16.4 %convolution_convert_fusion = bf16[2048,2560]{1,0:T(8,128)(2,1)} fusion(bf16[2048,896]{0,1:T(8,128)(2,1)} %copy-done.5, bf16[2,2560,896]{2,1,0:T(8,128)(2,1)} %param.15), kind=kOutput, calls=%fused_computation.26 | convolution fusion | flops 9400483840 | bytes 18743296 | tf_op jit(solution)/shard_map/transpose(jvp())/dot_general | solution.py:365
  258.2 18.6 %fusion.29 = bf16[1,896,2560]{2,1,0:T(8,128)(2,1)} fusion(bf16[2048,2560]{1,0:T(8,128)(2,1)} %convolution_convert_fusion, f32[2048,2560]{1,0:T(8,128)} %fusion.52, bf16[1,2048,896]{1,2,0:T(8,128)(2,1)} %copy.34, f32[2048]{0:T(1024)S(1)} %copy-done.17), kind=kOutput, calls=%fused_computation.54 | convolution fusion | flops 9434497024 | bytes 39723008 | tf_op jit(solution)/shard_map/transpose(jvp())/dot_general | solution.py:377
  276.8 8.1 %pad_add_fusion.1 = (bf16[1,896,2560]{2,1,0:T(8,128)(2,1)}, bf16[1,896,2560]{2,1,0:T(8,128)(2,1)}) fusion(bf16[1,896,2560]{2,1,0:T(8,128)(2,1)} %fusion.29, bf16[1,896,2560]{2,1,0:T(8,128)(2,1)} %fusion.30), kind=kLoop, calls=%fused_computation.63 | loop fusion | flops 4587520 | bytes 18350080 | tf_op jit(solution)/shard_map/transpose(jvp())/add_any | solution.py:383
  284.9 8.7 %reshape_squeeze.20 = bf16[64,14,20,128]{3,2,1,0:T(8,128)(2,1)} reshape(bf16[1,896,2560]{2,1,0:T(8,128)(2,1)} %get-tuple-element.66) | data formatting | bytes 9175040 | tf_op jit(solution)/shard_map/reshape;squeeze | solution.py:389
  297.4 5.1 copy.42.refs_2_
  302.5 8.9 %reshape_squeeze.21 = bf16[64,14,20,128]{3,2,1,0:T(8,128)(2,1)} reshape(bf16[1,896,2560]{2,1,0:T(8,128)(2,1)} %get-tuple-element.65) | data formatting | bytes 9175040 | tf_op jit(solution)/shard_map/reshape;squeeze | solution.py:389
  311.4 3.9 copy.39
  315.4 5.1 copy.43.refs_3_
  320.4 13.7 %fusion.31 = bf16[1,896,2560]{2,1,0:T(8,128)(2,1)} fusion(bf16[2048,2560]{1,0:T(8,128)(2,1)} %get-tuple-element.73, bf16[2048,896]{0,1:T(8,128)(2,1)S(1)} %copy-done.4, f32[2048]{0:T(1024)S(1)} %fusion.80), kind=kOutput, calls=%fused_computation.56 | convolution fusion | flops 9400745984 | bytes 18751488 | tf_op jit(solution)/shard_map/transpose(jvp())/dot_general | solution.py:376
  334.1 24.9 %fusion.33 = bf16[1,896,2560]{2,1,0:T(8,128)(2,1)} fusion(f32[2048,2560]{1,0:T(8,128)} %fusion.52, f32[2048,2560]{1,0:T(8,128)} %get-tuple-element.70, bf16[2048,2560]{1,0:T(8,128)(2,1)} %convolution_convert_fusion, bf16[1,2048,896]{1,2,0:T(8,128)(2,1)} %copy.34, f32[2048]{0:T(1024)S(1)} %copy-done.17), kind=kOutput, calls=%fused_computation.58 | convolution fusion | flops 9460711424 | bytes 60694528 | tf_op jit(solution)/shard_map/transpose(jvp())/dot_general | solution.py:376
  359.0 8.1 %pad_add_fusion.2 = (bf16[1,896,2560]{2,1,0:T(8,128)(2,1)}, bf16[1,896,2560]{2,1,0:T(8,128)(2,1)}) fusion(bf16[1,896,2560]{2,1,0:T(8,128)(2,1)} %fusion.33, bf16[1,896,2560]{2,1,0:T(8,128)(2,1)} %fusion.31), kind=kLoop, calls=%fused_computation.64 | loop fusion | flops 4587520 | bytes 18350080 | tf_op jit(solution)/shard_map/transpose(jvp())/add_any | solution.py:383
  367.1 8.7 %reshape_squeeze.18 = bf16[64,14,20,128]{3,2,1,0:T(8,128)(2,1)} reshape(bf16[1,896,2560]{2,1,0:T(8,128)(2,1)} %get-tuple-element.68) | data formatting | bytes 9175040 | tf_op jit(solution)/shard_map/reshape;squeeze | solution.py:389
  379.6 5.1 copy.40.refs_0_
  384.7 8.9 %reshape_squeeze.19 = bf16[64,14,20,128]{3,2,1,0:T(8,128)(2,1)} reshape(bf16[1,896,2560]{2,1,0:T(8,128)(2,1)} %get-tuple-element.67) | data formatting | bytes 9175040 | tf_op jit(solution)/shard_map/reshape;squeeze | solution.py:389
  397.4 5.1 copy.41.refs_1_
  402.5 124.8 %scatter.1 = (bf16[6,280,128]{2,1,0:T(8,128)(2,1)}, f32[8,128]{1,0:T(8,128)}) custom-call(bf16[4,4,4,280,128]{4,3,2,1,0:T(8,128)(2,1)} %copy.40.refs_0_, bf16[4,4,4,280,128]{4,3,2,1,0:T(8,128)(2,1)} %copy.41.refs_1_, bf16[4,4,4,280,128]{4,3,2,1,0:T(8,128)(2,1)} %copy.42.refs_2_, bf16[4,4,4,280,128]{4,3,2,1,0:T(8,128)(2,1)} %copy.43.refs_3_, ...), custom_call_target="tpu_custom_call" | custom-call | tf_op jit(solution)/shard_map/scatter/pallas_call | solution.py:155
  537.3 101.5 %gather.1 = (bf16[4,4,4,280,128]{4,3,2,1,0:T(8,128)(2,1)}, bf16[4,4,4,280,128]{4,3,2,1,0:T(8,128)(2,1)}, bf16[4,4,4,280,128]{4,3,2,1,0:T(8,128)(2,1)}, bf16[4,4,...) custom-call(bf16[6,280,128]{2,1,0:T(8,128)(2,1)} %get-tuple-element.29.refs_0_), custom_call_target="tpu_custom_call" | custom-call | tf_op jit(solution)/shard_map/gather/pallas_call | solution.py:283
  638.9 24.8 %natural.1 = (bf16[2,896,2560]{2,1,0:T(8,128)(2,1)}, bf16[2,896,2560]{2,1,0:T(8,128)(2,1)}, bf16[2,2560,896]{2,1,0:T(8,128)(2,1)}) custom-call(bf16[64,280,128]{2,1,0:T(8,128)(2,1)} %bitcast.110, bf16[64,280,128]{2,1,0:T(8,128)(2,1)} %bitcast.111, bf16[64,280,128]{2,1,0:T(8,128)(2,1)} %bitcast.112, bf16[64,280,128]{2,1,0:T(8,128)(2,1)} %bitcast.113, ...), custom_call_target="tpu_custom_call" | custom-call | tf_op jit(solution)/shard_map/natural/pallas_call | solution.py:353
  (60 shorter events, 31.9 us)
Async XLA Ops:
  9.6 18.3 %copy-start.16 = (f32[2048]{0:T(1024)}, f32[2048]{0:T(1024)S(1)}, u32[]{:S(2)}) copy-start(f32[2048]{0:T(1024)S(1)} %add_rsqrt_fusion) | copy-start | bytes 24580
  9.6 18.3 %copy-start.1 = (bf16[1,2048,896]{2,1,0:T(8,128)(2,1)S(1)}, bf16[1,2048,896]{2,1,0:T(8,128)(2,1)}, u32[]{:S(2)}) copy-start(bf16[1,2048,896]{2,1,0:T(8,128)(2,1)} %param.11) | copy-start | bytes 11010052
  27.9 24.6 %copy-start = (bf16[1,2048,896]{1,2,0:T(8,128)(2,1)S(1)}, bf16[1,2048,896]{1,2,0:T(8,128)(2,1)}, u32[]{:S(2)}) copy-start(bf16[1,2048,896]{1,2,0:T(8,128)(2,1)} %copy.34) | copy-start | bytes 11010052
  67.3 18.4 %copy-start.3 = (bf16[2048,896]{0,1:T(8,128)(2,1)}, bf16[2048,896]{0,1:T(8,128)(2,1)S(1)}, u32[]{:S(2)}) copy-start(bf16[2048,896]{0,1:T(8,128)(2,1)S(1)} %get-tuple-element.72) | copy-start | bytes 11010052
  67.3 18.4 %copy-start.14 = (f32[2048]{0:T(1024)}, f32[2048]{0:T(1024)S(1)}, u32[]{:S(2)}) copy-start(f32[2048]{0:T(1024)S(1)} %get-tuple-element.71) | copy-start | bytes 24580
  67.4 18.4 %copy-start.2 = (bf16[1,2048,896]{2,1,0:T(8,128)(2,1)S(1)}, bf16[1,2048,896]{2,1,0:T(8,128)(2,1)}, u32[]{:S(2)}) copy-start(bf16[1,2048,896]{2,1,0:T(8,128)(2,1)} %param.12) | copy-start | bytes 11010052
  173.6 17.1 %copy-start.15 = (f32[2048]{0:T(1024)S(1)}, f32[2048]{0:T(1024)}, u32[]{:S(2)}) copy-start(f32[2048]{0:T(1024)} %copy-done.14) | copy-start | bytes 24580
  196.7 22.2 %slice-start = ((s8[4587520]{0:T(1024)(128)(4,1)}), s8[393216]{0:T(1024)(128)(4,1)S(1)}, s32[]{:S(2)}) async-start(s8[4587520]{0:T(1024)(128)(4,1)} %bitcast.108), calls=%async_computation | async-start | bytes 786432
  203.6 15.3 %copy-start.5 = (bf16[2048,896]{0,1:T(8,128)(2,1)}, bf16[2048,896]{0,1:T(8,128)(2,1)S(1)}, u32[]{:S(2)}) copy-start(bf16[2048,896]{0,1:T(8,128)(2,1)S(1)} %fusion.64) | copy-start | bytes 11010052
  203.6 15.3 %slice-start.1 = ((s8[4587520]{0:T(1024)(128)(4,1)}), s8[4194304]{0:T(1024)(128)(4,1)S(1)}, s32[]{:S(2)}) async-start(s8[4587520]{0:T(1024)(128)(4,1)} %bitcast.108), calls=%async_computation.1 | async-start | bytes 8388608
  241.8 16.4 %copy-start.17 = (f32[2048]{0:T(1024)S(1)}, f32[2048]{0:T(1024)}, u32[]{:S(2)}) copy-start(f32[2048]{0:T(1024)} %copy-done.16) | copy-start | bytes 24580
  311.4 9.0 %copy-start.4 = (bf16[2048,896]{0,1:T(8,128)(2,1)S(1)}, bf16[2048,896]{0,1:T(8,128)(2,1)}, u32[]{:S(2)}) copy-start(bf16[2048,896]{0,1:T(8,128)(2,1)} %copy-done.3) | copy-start | bytes 11010052
  402.5 128.3 %copy-start.10 = (f32[2,14,2560]{2,0,1:T(2,128)S(1)}, f32[2,14,2560]{2,0,1:T(2,128)}, u32[]{:S(2)}) copy-start(f32[2,14,2560]{2,0,1:T(2,128)} %param.16) | copy-start | bytes 860164
  402.5 129.1 %copy-start.11 = (f32[2,14,2560]{2,0,1:T(2,128)S(1)}, f32[2,14,2560]{2,0,1:T(2,128)}, u32[]{:S(2)}) copy-start(f32[2,14,2560]{2,0,1:T(2,128)} %param.17) | copy-start | bytes 860164
  402.5 129.9 %copy-start.12 = (f32[2,14,2560]{2,0,1:T(2,128)S(1)}, f32[2,14,2560]{2,0,1:T(2,128)}, u32[]{:S(2)}) copy-start(f32[2,14,2560]{2,0,1:T(2,128)} %param.19) | copy-start | bytes 860164
  402.5 130.7 %copy-start.13 = (f32[2,14,2560]{2,0,1:T(2,128)S(1)}, f32[2,14,2560]{2,0,1:T(2,128)}, u32[]{:S(2)}) copy-start(f32[2,14,2560]{2,0,1:T(2,128)} %param.20) | copy-start | bytes 860164
  638.8 24.8 %copy-start.9 = (f32[2,14,2560]{2,1,0:T(8,128)S(1)}, f32[2,14,2560]{2,1,0:T(8,128)}, u32[]{:S(2)}) copy-start(f32[2,14,2560]{2,1,0:T(8,128)} %get-tuple-element.57) | copy-start | bytes 860164
  638.8 25.8 %copy-start.8 = (f32[2,14,2560]{2,1,0:T(8,128)S(1)}, f32[2,14,2560]{2,1,0:T(8,128)}, u32[]{:S(2)}) copy-start(f32[2,14,2560]{2,1,0:T(8,128)} %get-tuple-element.58) | copy-start | bytes 860164
  638.9 26.7 %copy-start.7 = (f32[2,14,2560]{2,1,0:T(8,128)S(1)}, f32[2,14,2560]{2,1,0:T(8,128)}, u32[]{:S(2)}) copy-start(f32[2,14,2560]{2,1,0:T(8,128)} %get-tuple-element.60) | copy-start | bytes 860164
  638.9 27.6 %copy-start.6 = (f32[2,14,2560]{2,1,0:T(8,128)S(1)}, f32[2,14,2560]{2,1,0:T(8,128)}, u32[]{:S(2)}) copy-start(f32[2,14,2560]{2,1,0:T(8,128)} %get-tuple-element.61) | copy-start | bytes 860164

commit v2 on v1

--- a/solution.py
+++ b/solution.py
@@ -10,6 +10,7 @@
 STRIDE = (16, 4, 1)
 ORDERS = ((0, 1, 2), (0, 1, 2), (1, 2, 0), (1, 2, 0), (2, 0, 1), (2, 0, 1))
 SIGNS = (1, -1, 1, -1, 1, -1)
+TAKEN = (3, 0, 4, 1, 5, 2)
 
 
 def place():
@@ -47,7 +48,7 @@
 
 
 def rs_kernel(*refs):
-    terms, (out, squares), scratch = refs[:6], refs[6:8], refs[8:]
+    terms, (out, squares), scratch = [refs[0].at[m] for m in TAKEN], refs[1:3], refs[3:]
     r1, r2, r3, own, f1, f2, sums, send1, send2, send3, recv1, recv2, recv3, load, send4, recv4 = scratch
     at = place()
     enter(at)
@@ -149,13 +150,13 @@
 
 
 def reduce_scatter(terms):
-    rows = terms[0].shape[3]
+    rows = terms.shape[4]
     bf16, f32 = jnp.bfloat16, jnp.float32
     dma = pltpu.SemaphoreType.DMA
     return pl.pallas_call(
         rs_kernel,
         out_shape=(jax.ShapeDtypeStruct((6, rows, 128), bf16), jax.ShapeDtypeStruct((8, 128), f32)),
-        in_specs=[pl.BlockSpec(memory_space=pl.ANY)] * 6,
+        in_specs=[pl.BlockSpec(memory_space=pl.ANY)],
         out_specs=(pl.BlockSpec(memory_space=pltpu.VMEM), pl.BlockSpec(memory_space=pltpu.VMEM)),
         scratch_shapes=[
             pltpu.VMEM((6, 3, 4, 4, rows, 128), bf16),
@@ -172,7 +173,7 @@
         ],
         compiler_params=pltpu.CompilerParams(collective_id=0, has_side_effects=True, vmem_limit_bytes=60 * 1024 * 1024),
         name="scatter",
-    )(*terms)
+    )(terms)
 
 
 def ag_order(latency=1.8):
@@ -361,35 +362,174 @@
     )(*blocks)
 
 
-def matmul(a, w):
-    return jnp.dot(a, w, preferred_element_type=jnp.float32).astype(jnp.bfloat16)
-
-
-def normed(h):
-    wide = h.astype(jnp.float32)
-    scale = lax.rsqrt(jnp.mean(wide**2, -1, keepdims=True) + 1e-6)
-    return (wide * scale).astype(jnp.bfloat16)
-
-
-def layer(h, w):
-    a = normed(h)
-    gate = jnp.dot(a, w["w_gate"], preferred_element_type=jnp.float32)
-    up = jnp.dot(a, w["w_up"], preferred_element_type=jnp.float32)
-    return h + matmul((jax.nn.silu(gate) * up).astype(jnp.bfloat16), w["w_down"])
-
-
-def stack(weights, h):
-    for number in range(2):
-        h = layer(h, {name: w[number] for name, w in weights.items()})
-    return h
-
-
-def in_blocks(t, g):
-    if t < 2:
-        g = g.reshape(64, 14, 20, LANES).transpose(0, 2, 1, 3)
-    else:
-        g = g.reshape(64, 5, 8, 7, LANES).transpose(0, 1, 3, 2, 4)
-    return g.reshape(4, 4, 4, 280, LANES)
+D, FF, TOKENS = 896, 2560, 2048
+ROWS, CHUNK, TILE = 256, 512, 512
+NT = (((1,), (1,)), ((), ()))
+
+
+def dot(a, b):
+    return jnp.dot(a, b, preferred_element_type=jnp.float32)
+
+
+def dot_t(a, b):
+    return lax.dot_general(a, b, NT, preferred_element_type=jnp.float32)
+
+
+def scale_of(wide):
+    return lax.rsqrt(jnp.mean(wide * wide, -1, keepdims=True) + 1e-6)
+
+
+def rows_kernel(x, dy, *refs):
+    hbm, left, right, weights, (g0, u0, sems) = refs[:3], refs[3], refs[4], refs[5:11], refs[11:]
+    wg0, wu0, wd0, wg1, wu1, wd1 = weights
+    first = pl.program_id(0) == 0
+
+    def fetch(k):
+        return pltpu.make_async_copy(hbm[k % 3].at[k // 3], weights[k], sems.at[k])
+
+    @pl.when(first)
+    def _():
+        for k in range(6):
+            fetch(k).start()
+
+    def ready(*ks):
+        @pl.when(first)
+        def _():
+            for k in ks:
+                fetch(k).wait()
+
+    bf16, f32 = jnp.bfloat16, jnp.float32
+    a = (x[...].astype(f32) * scale_of(x[...].astype(f32))).astype(bf16)
+    left[2] = a.T
+    left[1] = dy[...].T
+    ready(0, 1)
+    for j in range(FF // CHUNK):
+        ch = pl.ds(j * CHUNK, CHUNK)
+        gate, up = dot(a, wg0[:, ch]), dot(a, wu0[:, ch])
+        g0[:, ch], u0[:, ch] = gate, up
+        right[5, :, ch] = (gate * jax.nn.sigmoid(gate) * up).astype(bf16)
+    ready(2)
+    h = x[...] + dot(right[5], wd0[...]).astype(bf16)
+    wide = h.astype(f32)
+    scale = scale_of(wide)
+    a = (wide * scale).astype(bf16)
+    left[0] = a.T
+    ready(3, 4, 5)
+    for j in range(FF // CHUNK):
+        ch = pl.ds(j * CHUNK, CHUNK)
+        gate, up = dot(a, wg1[:, ch]), dot(a, wu1[:, ch])
+        dz = dot_t(dy[...], wd1[ch, :]).astype(bf16).astype(f32)
+        s = jax.nn.sigmoid(gate)
+        silu = gate * s
+        right[2, :, ch] = (silu * up).astype(bf16)
+        right[1, :, ch] = (dz * silu).astype(bf16)
+        right[0, :, ch] = (dz * up * (s * (1 + gate * (1 - s)))).astype(bf16)
+    da = dot_t(right[0], wg1[...]).astype(bf16) + dot_t(right[1], wu1[...]).astype(bf16)
+    da = da.astype(f32)
+    dwide = scale * (da - wide * (scale * scale * jnp.mean(da * wide, -1, keepdims=True)))
+    dh = dy[...] + dwide.astype(bf16)
+    left[3] = dh.T
+    for j in range(FF // CHUNK):
+        ch = pl.ds(j * CHUNK, CHUNK)
+        dz = dot_t(dh, wd0[ch, :]).astype(bf16).astype(f32)
+        gate, up = g0[:, ch], u0[:, ch]
+        s = jax.nn.sigmoid(gate)
+        right[4, :, ch] = (dz * (gate * s)).astype(bf16)
+        right[3, :, ch] = (dz * up * (s * (1 + gate * (1 - s)))).astype(bf16)
+
+
+def by_rows(x, dy, weights):
+    bf16 = jnp.bfloat16
+    state = pl.BlockSpec((ROWS, D), lambda i: (i, 0))
+    return pl.pallas_call(
+        rows_kernel,
+        grid=(TOKENS // ROWS,),
+        out_shape=(jax.ShapeDtypeStruct((4, D, TOKENS), bf16), jax.ShapeDtypeStruct((6, TOKENS, FF), bf16)),
+        in_specs=[state, state] + [pl.BlockSpec(memory_space=pl.ANY)] * 3,
+        out_specs=(pl.BlockSpec((4, D, ROWS), lambda i: (0, 0, i)), pl.BlockSpec((6, ROWS, FF), lambda i: (0, i, 0))),
+        scratch_shapes=[*[pltpu.VMEM(w.shape[1:], bf16) for w in weights * 2], pltpu.VMEM((ROWS, FF), jnp.float32), pltpu.VMEM((ROWS, FF), jnp.float32), pltpu.SemaphoreType.DMA((6,))],
+        compiler_params=pltpu.CompilerParams(vmem_limit_bytes=62 * 1024 * 1024),
+        name="rows",
+    )(x, dy, *weights)
+
+
+def gate_block(acc, stage, wide):
+    def group(i, _):
+        rows = pl.ds(pl.multiple_of(i * 56, 8), 56)
+        for c in range(4):
+            piece = acc[rows, pl.ds(c * LANES, LANES)]
+            for z in range(4):
+                wide[z, pl.ds(14 * c, 14), :] = piece[14 * z : 14 * z + 14]
+        for z in range(4):
+            stage[4 * i + z] = wide[z].astype(jnp.bfloat16)
+        return 0
+
+    lax.fori_loop(0, 16, group, 0)
+
+
+def down_block(acc, stage, turned):
+    turned[...] = acc[...].T
+
+    def group(i, _):
+        rows = turned[pl.ds(pl.multiple_of(i * 8, 8), 8), :]
+        stage[i] = jnp.concatenate([rows[:, c * LANES : (c + 1) * LANES] for c in range(7)], 0).astype(jnp.bfloat16)
+        return 0
+
+    lax.fori_loop(0, 64, group, 0)
+
+
+def gradients_kernel(left, right, out, acc, stage, wide, turned, sem):
+    m, h = pl.program_id(0), pl.program_id(1)
+    acc[...] = dot(left[...], right[...])
+
+    whole = out.at[m, :, pl.ds(pl.multiple_of(56 * h, 8), 56)]
+
+    @pl.when(m + h > 0)
+    def _():
+        pltpu.make_async_copy(stage, whole, sem).wait()
+
+    @pl.when(m % 3 < 2)
+    def _():
+        gate_block(acc, stage, wide)
+        pltpu.make_async_copy(stage, whole, sem).start()
+
+    @pl.when(m % 3 == 2)
+    def _():
+        down_block(acc, stage, turned)
+
+        def put(k, _):
+            i = 64 * h + k
+            pltpu.make_async_copy(stage.at[k], out.at[m, i // 5, pl.ds(pl.multiple_of(i % 5 * 56, 8), 56)], sem).start()
+            return 0
+
+        lax.fori_loop(0, 64, put, 0)
+
+    @pl.when(m + h == 9)
+    def _():
+        pltpu.make_async_copy(stage, whole, sem).wait()
+
+
+def gradients(left, right):
+    bf16, f32 = jnp.bfloat16, jnp.float32
+    return pl.pallas_call(
+        gradients_kernel,
+        grid=(6, FF // TILE),
+        out_shape=jax.ShapeDtypeStruct((6, 64, 280, LANES), bf16),
+        in_specs=[
+            pl.BlockSpec((None, D, TOKENS), lambda m, h: (m // 3 * 2 + m % 3 // 2, 0, 0)),
+            pl.BlockSpec((None, TOKENS, TILE), lambda m, h: (m, 0, h)),
+        ],
+        out_specs=pl.BlockSpec(memory_space=pl.ANY),
+        scratch_shapes=[
+            pltpu.VMEM((D, TILE), f32),
+            pltpu.VMEM((64, 56, LANES), bf16),
+            pltpu.VMEM((4, 56, LANES), f32),
+            pltpu.VMEM((TILE, D), f32),
+            pltpu.SemaphoreType.DMA,
+        ],
+        compiler_params=pltpu.CompilerParams(vmem_limit_bytes=62 * 1024 * 1024),
+        name="gradients",
+    )(left, right)
 
 
 def solution(mesh):
@@ -397,10 +537,8 @@
 
     def step(x, dy, *arrays):
         weights, m, v = (arrays[i : i + 3] for i in (0, 3, 6))
-        _, back = jax.vjp(lambda w: stack(w, x[0]), dict(zip(NAMES, weights, strict=True)))
-        by_weights = back(dy[0])[0]
-        terms = [in_blocks(t, by_weights[NAMES[t]][l]) for t in range(3) for l in range(2)]
-        g, total = reduce_scatter(terms)
+        left, right = by_rows(x[0], dy[0], weights)
+        g, total = reduce_scatter(gradients(left, right).reshape(6, 4, 4, 4, 280, LANES))
         me = lax.axis_index(dp)
         mine = [lax.dynamic_slice_in_dim(w, me * b.shape[1], b.shape[1], 1) for w, b in zip(weights, m, strict=True)]
         new, new_m, new_v = adam(sum(w.size for w in weights), g, total, mine, m, v)

time: 676 us -> 487 us (0.72); the launches traced: 668 us -> 486 us
  matrix products: 289 us -> 0 us
  Pallas kernels: 254 us -> 475 us
  local copies, waits for them, and re-layouts: 93.4 us -> 10.4 us
  other arithmetic: 29.8 us -> 0 us
    dot_general x15 -> x0, matrix products: 289 us -> none  [the longest x5 106 us: layer(): gate = jnp.dot(a, w['w_gate'], preferred_element_type=jnp.float32)]
    pallas_call x0 -> x2, Pallas kernels: none -> 221 us  [the longest x1 125 us: by_rows(): pl.pallas_call(rows_kernel, grid=(TOKENS // ROWS,), out_shape=(jax.ShapeD...]
    another operation x4 -> x0, local copies, waits for them, and re-layouts: 35.2 us -> none  [in_blocks(): g = g.reshape(64, 14, 20, LANES).transpose(0, 2, 1, 3)]
    add_any x4 -> x0, other arithmetic: 26.9 us -> none  [the longest x3 20 us: stack(): h = layer(h, {name: w[number] for name, w in weights.items()})]
    reshape x4 -> x0, local copies, waits for them, and re-layouts: 20.3 us -> none  [in_blocks(): return g.reshape(4, 4, 4, 280, LANES)]
    transpose x4 -> x0, local copies, waits for them, and re-layouts: 15.3 us -> none  [in_blocks(): g = g.reshape(64, 14, 20, LANES).transpose(0, 2, 1, 3)]
    unnamed x50 -> x24, local copies, waits for them, and re-layouts: 19.1 us -> 6.92 us
where the time goes in v2:
time: 487 us; the launch traced here: 486 us
  Pallas kernels  475 us (98%)
  local copies, waits for them, and re-layouts  10.4 us (2%)
    pallas_call x1, Pallas kernels, by_rows(): pl.pallas_call(rows_kernel, grid=(TOKENS // ROWS,), out_shape=(jax.ShapeD...  125 us
    pallas_call x1, Pallas kernels, reduce_scatter(): pl.pallas_call(rs_kernel, out_shape=(jax.ShapeDtypeStruct((6, rows, 128),...  125 us
    pallas_call x1, Pallas kernels, all_gather(): pl.pallas_call(ag_kernel, out_shape=tuple((jax.ShapeDtypeStruct((4, 4, 4,...  102 us
    pallas_call x1, Pallas kernels, gradients(): pl.pallas_call(gradients_kernel, grid=(6, FF // TILE), out_shape=jax.Shap...  96.1 us
    pallas_call x1, Pallas kernels, natural(): pl.pallas_call(natural_kernel, grid=(16,), out_shape=tuple((jax.ShapeDtyp...  24.8 us

profile of v2, /device:TPU:0, one launch (start us, length us, event | category | flops | bytes accessed | tf_op | source)
XLA Modules:
  0.0 486.5 jit_solution(13825907184077747254)
XLA Ops:
  0.6 124.8 %rows.1 = (bf16[4,896,2048]{2,1,0:T(8,128)(2,1)}, bf16[6,2048,2560]{2,1,0:T(8,128)(2,1)}) custom-call(bf16[2048,896]{1,0:T(8,128)(2,1)} %bitcast.16, bf16[2048,896]{1,0:T(8,128)(2,1)} %bitcast.17, bf16[2,896,2560]{2,1,0:T(8,128)(2,1)} %refs_0_.1, bf16[2,896,2560]{2,1,0:T(8,128)(2,1)} %refs_1_.1, bf16[2,2560,896]{2,1,0:T(8,128)(2,1)} %refs_2_.1), custom_call_target="tpu_custom_call" | custom-call | tf_op jit(solution)/shard_map/rows/pallas_call | solution.py:444
  125.5 96.1 %gradients.1 = bf16[6,64,280,128]{3,2,1,0:T(8,128)(2,1)} custom-call(bf16[4,896,2048]{2,1,0:T(8,128)(2,1)} %get-tuple-element.29.left, bf16[6,2048,2560]{2,1,0:T(8,128)(2,1)} %get-tuple-element.30.right), custom_call_target="tpu_custom_call" | custom-call | tf_op jit(solution)/shard_map/gradients/pallas_call | solution.py:514
  221.6 0.0 copy-start.4
  221.6 0.0 copy-start.5
  221.6 0.0 copy-start.6
  221.6 0.0 copy-start.7
  221.6 124.6 %scatter.1 = (bf16[6,280,128]{2,1,0:T(8,128)(2,1)}, f32[8,128]{1,0:T(8,128)}) custom-call(bf16[6,4,4,4,280,128]{5,4,3,2,1,0:T(8,128)(2,1)} %bitcast.9), custom_call_target="tpu_custom_call" | custom-call | tf_op jit(solution)/shard_map/scatter/pallas_call | solution.py:156
  346.2 1.9 constant_dynamic-slice_fusion.1
  348.1 1.6 constant_dynamic-slice_fusion.refs_2_
  349.7 0.0 copy-done.4
  349.7 0.8 copy.20.refs_3_
  350.5 0.0 copy-done.5
  350.5 0.8 copy.21.refs_4_
  351.3 0.0 copy-done.6
  351.3 0.8 copy.22.refs_6_
  352.1 0.0 copy-done.7
  352.1 0.8 copy.23.refs_7_
  352.9 3.4 adam.1
  356.3 101.6 %gather.1 = (bf16[4,4,4,280,128]{4,3,2,1,0:T(8,128)(2,1)}, bf16[4,4,4,280,128]{4,3,2,1,0:T(8,128)(2,1)}, bf16[4,4,4,280,128]{4,3,2,1,0:T(8,128)(2,1)}, bf16[4,4,...) custom-call(bf16[6,280,128]{2,1,0:T(8,128)(2,1)} %get-tuple-element.33.refs_0_), custom_call_target="tpu_custom_call" | custom-call | tf_op jit(solution)/shard_map/gather/pallas_call | solution.py:284
  457.9 0.0 copy-start.3
  457.9 0.0 copy-start.2
  457.9 0.0 copy-start.1
  457.9 0.0 copy-start
  457.9 24.8 %natural.1 = (bf16[2,896,2560]{2,1,0:T(8,128)(2,1)}, bf16[2,896,2560]{2,1,0:T(8,128)(2,1)}, bf16[2,2560,896]{2,1,0:T(8,128)(2,1)}) custom-call(bf16[64,280,128]{2,1,0:T(8,128)(2,1)} %bitcast.10, bf16[64,280,128]{2,1,0:T(8,128)(2,1)} %bitcast.11, bf16[64,280,128]{2,1,0:T(8,128)(2,1)} %bitcast.12, bf16[64,280,128]{2,1,0:T(8,128)(2,1)} %bitcast.13, ...), custom_call_target="tpu_custom_call" | custom-call | tf_op jit(solution)/shard_map/natural/pallas_call | solution.py:354
  482.7 0.0 copy-done.3
  482.7 0.9 copy.24
  483.7 0.0 copy-done.2
  483.7 0.9 copy.25
  484.6 0.0 copy-done.1
  484.6 0.9 copy.26
  485.5 0.0 copy-done
  485.5 0.9 copy.27
Async XLA Ops:
  221.6 128.1 %copy-start.4 = (f32[2,14,2560]{2,0,1:T(2,128)S(1)}, f32[2,14,2560]{2,0,1:T(2,128)}, u32[]{:S(2)}) copy-start(f32[2,14,2560]{2,0,1:T(2,128)} %param.16) | copy-start | bytes 860164
  221.6 128.9 %copy-start.5 = (f32[2,14,2560]{2,0,1:T(2,128)S(1)}, f32[2,14,2560]{2,0,1:T(2,128)}, u32[]{:S(2)}) copy-start(f32[2,14,2560]{2,0,1:T(2,128)} %param.17) | copy-start | bytes 860164
  221.6 129.7 %copy-start.6 = (f32[2,14,2560]{2,0,1:T(2,128)S(1)}, f32[2,14,2560]{2,0,1:T(2,128)}, u32[]{:S(2)}) copy-start(f32[2,14,2560]{2,0,1:T(2,128)} %param.19) | copy-start | bytes 860164
  221.6 130.4 %copy-start.7 = (f32[2,14,2560]{2,0,1:T(2,128)S(1)}, f32[2,14,2560]{2,0,1:T(2,128)}, u32[]{:S(2)}) copy-start(f32[2,14,2560]{2,0,1:T(2,128)} %param.20) | copy-start | bytes 860164
  457.9 24.8 %copy-start.3 = (f32[2,14,2560]{2,1,0:T(8,128)S(1)}, f32[2,14,2560]{2,1,0:T(8,128)}, u32[]{:S(2)}) copy-start(f32[2,14,2560]{2,1,0:T(8,128)} %get-tuple-element.52) | copy-start | bytes 860164
  457.9 25.8 %copy-start.2 = (f32[2,14,2560]{2,1,0:T(8,128)S(1)}, f32[2,14,2560]{2,1,0:T(8,128)}, u32[]{:S(2)}) copy-start(f32[2,14,2560]{2,1,0:T(8,128)} %get-tuple-element.53) | copy-start | bytes 860164
  457.9 26.7 %copy-start.1 = (f32[2,14,2560]{2,1,0:T(8,128)S(1)}, f32[2,14,2560]{2,1,0:T(8,128)}, u32[]{:S(2)}) copy-start(f32[2,14,2560]{2,1,0:T(8,128)} %get-tuple-element.55) | copy-start | bytes 860164
  457.9 27.6 %copy-start = (f32[2,14,2560]{2,1,0:T(8,128)S(1)}, f32[2,14,2560]{2,1,0:T(8,128)}, u32[]{:S(2)}) copy-start(f32[2,14,2560]{2,1,0:T(8,128)} %get-tuple-element.56) | copy-start | bytes 860164

commit v3 on v0

v3 whole, which is shorter than its diff:
```python
import functools
import jax
import jax.numpy as jnp
from jax import lax
from jax.experimental import pallas as pl
from jax.experimental.pallas import tpu as pltpu
from jax.sharding import PartitionSpec as P

MESH = pl.DeviceIdType.MESH
WAYS, AXES, SIDE = 6, 3, 4
STEPS = SIDE - 1
MATRICES, LAYERS, DEVICES, PLANE = 6, 2, 64, 16
LANES, SUBLANES, BLOCK = 128, 8, 280
BF16, F32 = jnp.bfloat16, jnp.float32
HBM, VMEM = pl.BlockSpec(memory_space=pl.ANY), pl.BlockSpec(memory_space=pltpu.VMEM)
DMA = pltpu.SemaphoreType.DMA
MOST_VMEM = 62 * 1024 * 1024
ORDERS = tuple(tuple((way // 2 + i) % AXES for i in range(AXES)) for way in range(WAYS))
SIGNS = (1, -1) * AXES
TAKEN = (3, 0, 4, 1, 5, 2)


def place():
    me = lax.axis_index("dp")
    return (me // PLANE, me // SIDE % SIDE, me % SIDE)


def wrap(i):
    return (i + 3 * SIDE) % SIDE


def neighbour(at, axis, step):
    there = [c for c in at]
    there[axis] = wrap(at[axis] + step)
    return {"dp": (there[0] * SIDE + there[1]) * SIDE + there[2]}


def remote(src, dst, send, recv, to):
    return pltpu.make_async_remote_copy(src_ref=src, dst_ref=dst, send_sem=send, recv_sem=recv, device_id=to, device_id_type=MESH)


def enter(at):
    barrier = pltpu.get_barrier_semaphore()
    for axis in range(AXES):
        for step in range(STEPS):
            pl.semaphore_signal(barrier, inc=1, device_id=neighbour(at, axis, step + 1), device_id_type=MESH)
    pl.semaphore_wait(barrier, AXES * STEPS)


def norm_exchange(at, buf, send, recv, total):
    for axis in range(AXES):
        buf[axis, STEPS] = total
        copies = [
            remote(buf.at[axis, STEPS], buf.at[axis, k], send.at[axis], recv.at[axis, k], neighbour(at, axis, k + 1)) for k in range(STEPS)
        ]
        for copy in copies:
            copy.start()
        for k, copy in enumerate(copies):
            copy.wait_recv()
            total = total + buf[axis, k]
    return total


def passed_on(seen, c, phase, key):
    d1, d2, d3 = key
    if phase == 0 and d3 < STEPS:
        yield 0, (0, 0, d3 + 1)
    if phase < 2 and d2 < STEPS:
        yield 1, (0, d2 + 1, d3)
    if phase == 1 and d2 > 0:
        seen.append((c, d2))
        if seen.count((c, d2)) < SIDE:
            return
        d3 = None
    if d1 < STEPS:
        yield 2, (d1 + 1, d2, d3)


def ag_order(latency=1.8):
    import heapq

    free, out, seen, heap = {}, [], [], []

    def hold(t, c, phase, key):
        for phase, key in passed_on(seen, c, phase, key):
            link = ORDERS[c][2 - phase]
            size = SIDE if key[2] is None else 1
            free[link] = max(t, free.get(link, 0)) + size
            heapq.heappush(heap, (free[link] + latency, len(out) * WAYS + len(heap), c, phase, key))

    for c in range(0, WAYS, 2):
        hold(0, c, 0, (0, 0, 0))
    while heap:
        t, _, *arrival = heapq.heappop(heap)
        out.append(arrival)
        hold(t, *arrival)
    return out


def ag_kernel(*refs):
    mine, outs, (sends, recv1, recv2, recv3, recv4, local) = refs[0], refs[1 : 1 + WAYS], refs[1 + WAYS :]
    at = place()
    enter(at)

    def where(c, key):
        index = [None] * AXES
        for axis, d in zip(ORDERS[c], key, strict=True):
            index[axis] = slice(None) if d is None else wrap(at[axis] - SIGNS[c] * d)
        return outs[c].at[tuple(index)]

    def copy(c, phase, key, of_receiver):
        d1, d2, d3 = key
        back = list(key)
        if not of_receiver:
            back[2 - phase] -= 1
        there = where(c, back)
        src = mine.at[c] if not of_receiver and not any(back) and d3 is not None else there
        if phase == 0:
            recv = recv1.at[c, d3]
        elif phase == 1:
            recv = recv2.at[c, d2, d3]
        elif d3 is not None:
            recv = recv3.at[c, d1, d3]
        else:
            recv = recv4.at[c, d1, d2]
        return remote(src, there, sends.at[c, phase], recv, neighbour(at, ORDERS[c][2 - phase], SIGNS[c]))

    seen = []

    def hold(*held):
        for phase, key in passed_on(seen, *held):
            copy(held[0], phase, key, False).start()

    own = [pltpu.make_async_copy(mine.at[c], where(c, (0, 0, 0)), local.at[c]) for c in range(WAYS)]
    for c in range(WAYS):
        hold(c, 0, (0, 0, 0))
    for copied in own:
        copied.start()
    for even, phase, key in ag_order():
        for c in (even, even + 1):
            copy(c, phase, key, True).wait_recv()
            hold(c, phase, key)
    for c in range(WAYS):
        own[c].wait()
        sent = outs[c].at[pl.ds(0, STEPS)]
        for phase in (2, 1, 0):
            pltpu.make_async_copy(sent, sent, sends.at[c, phase]).wait()
            sent = outs[c].at[(0,) * (AXES - phase) + (pl.ds(0, STEPS),)]


def all_gather(mine):
    return pl.pallas_call(
        ag_kernel,
        out_shape=tuple(jax.ShapeDtypeStruct((SIDE, SIDE, SIDE, *mine.shape[1:]), BF16) for _ in range(WAYS)),
        in_specs=[VMEM],
        out_specs=(HBM,) * WAYS,
        scratch_shapes=[DMA((WAYS, AXES)), DMA((WAYS, SIDE)), *[DMA((WAYS, SIDE, SIDE))] * 3, DMA((WAYS,))],
        compiler_params=pltpu.CompilerParams(collective_id=1, has_side_effects=True),
        name="gather",
    )(mine)


def tiles_of(t, rows, columns):
    n = columns // LANES
    if t < 2:
        return [(0, rows, j * LANES, j * rows) for j in range(n)]
    return [(8 * i, 8, j * LANES, (i * n + j) * 8) for i in range(rows // 8) for j in range(n)]


def adam_kernel(count, g, total, *refs):
    ws, ms, vs, new, new_m, new_v, wide_g, wide_w = refs[0:3], refs[3:6], refs[6:9], refs[9], refs[10:13], refs[13:16], refs[16], refs[17]
    factor = jnp.minimum(1.0, 0.5 * lax.rsqrt(jnp.full((1, 1), jnp.sum(total[...])) / count + 1e-30))
    for t in range(3):
        for l in range(2):
            c = 2 * t + l
            wide_g[...] = g[TAKEN[c]].astype(F32) * factor
            for row, rows, column, at in tiles_of(t, *ms[t].shape[1:]):
                here = (l, pl.ds(row, rows), pl.ds(column, LANES))
                grad = wide_g[pl.ds(at, rows), :]
                m = 0.9 * ms[t][here] + 0.1 * grad
                v = 0.95 * vs[t][here] + 0.05 * grad * grad
                w = ws[t][here].astype(F32)
                new_m[t][here] = m
                new_v[t][here] = v
                wide_w[pl.ds(at, rows), :] = w - 0.02 * (m * lax.rsqrt(v + 1e-8) + 0.1 * w)
            new[c] = wide_w[...].astype(BF16)


def adam(count, g, total, ws, ms, vs):
    like = [jax.ShapeDtypeStruct(m.shape, F32) for m in ms]
    out = pl.pallas_call(
        functools.partial(adam_kernel, count),
        out_shape=(jax.ShapeDtypeStruct(g.shape, BF16), *like, *like),
        in_specs=[VMEM] * 11,
        out_specs=(VMEM,) * 7,
        scratch_shapes=[pltpu.VMEM(g.shape[1:], F32)] * 2,
        name="adam",
    )(g, total, *ws, *ms, *vs)
    return out[0], out[1:4], out[4:7]


def natural_kernel(*refs):
    blocks, outs, wide = refs[:6], refs[6:9], refs[9:]
    for t in range(3):
        for l in range(2):
            for z in range(4):
                block = blocks[2 * t + l][z].astype(F32)
                rows = outs[t].shape[1] // 4
                for row, n, column, at in tiles_of(t, rows, outs[t].shape[2]):
                    wide[t][pl.ds(z * rows + row, n), pl.ds(column, LANES)] = block[at : at + n]
            outs[t][l] = wide[t][...].astype(BF16)


def natural(blocks):
    blocks = [b.reshape(64, *b.shape[3:]) for b in blocks]
    shapes = ((2, 896, 2560), (2, 896, 2560), (2, 2560, 896))
    return pl.pallas_call(
        natural_kernel,
        grid=(16,),
        out_shape=tuple(jax.ShapeDtypeStruct(s, BF16) for s in shapes),
        in_specs=[pl.BlockSpec((4, 280, 128), lambda i: (i, 0, 0))] * 6,
        out_specs=tuple(pl.BlockSpec((2, s[1] // 16, s[2]), lambda i: (0, i, 0)) for s in shapes),
        scratch_shapes=[pltpu.VMEM((s[1] // 16, s[2]), F32) for s in shapes],
        name="natural",
    )(*blocks)


D, FF, TOKENS = 896, 2560, 2048
ROWS, CHUNK, TILE = 256, 512, 512
TILES, PIECE, PLANE_ROWS = FF // TILE, BLOCK * TILE // FF, FF // SIDE
NT = (((1,), (1,)), ((), ()))


def dot(a, b):
    return jnp.dot(a, b, preferred_element_type=F32)


def dot_t(a, b):
    return lax.dot_general(a, b, NT, preferred_element_type=F32)


def scale_of(wide):
    return lax.rsqrt(jnp.mean(wide * wide, -1, keepdims=True) + 1e-6)


def rows_kernel(x, dy, *refs):
    hbm, (tall, wide, turned, deep), weights, (g0, u0, z0, sems) = refs[:3], refs[3:7], refs[7:13], refs[13:]
    wg0, wu0, wd0, wg1, wu1, wd1 = weights
    first = pl.program_id(0) == 0

    def fetch(k):
        return pltpu.make_async_copy(hbm[k % 3].at[k // 3], weights[k], sems.at[k])

    @pl.when(first)
    def _():
        for k in range(6):
            fetch(k).start()

    def ready(*ks):
        @pl.when(first)
        def _():
            for k in ks:
                fetch(k).wait()

    a = (x[...].astype(F32) * scale_of(x[...].astype(F32))).astype(BF16)
    tall[1] = a.T
    deep[0] = dy[...]
    ready(0, 1)
    for j in range(FF // CHUNK):
        ch = pl.ds(j * CHUNK, CHUNK)
        gate, up = dot(a, wg0[:, ch]), dot(a, wu0[:, ch])
        g0[:, ch], u0[:, ch] = gate, up
        z0[:, ch] = (gate * jax.nn.sigmoid(gate) * up).astype(BF16)
        turned[1, ch, :] = z0[:, ch].T
    ready(2)
    h = x[...] + dot(z0[...], wd0[...]).astype(BF16)
    h = h.astype(F32)
    scale = scale_of(h)
    a = (h * scale).astype(BF16)
    tall[0] = a.T
    ready(3, 4, 5)
    for j in range(FF // CHUNK):
        ch = pl.ds(j * CHUNK, CHUNK)
        gate, up = dot(a, wg1[:, ch]), dot(a, wu1[:, ch])
        dz = dot_t(dy[...], wd1[ch, :]).astype(BF16).astype(F32)
        s = jax.nn.sigmoid(gate)
        silu = gate * s
        turned[0, ch, :] = (silu * up).astype(BF16).T
        wide[1, :, ch] = (dz * silu).astype(BF16)
        wide[0, :, ch] = (dz * up * (s * (1 + gate * (1 - s)))).astype(BF16)
    da = dot_t(wide[0], wg1[...]).astype(BF16) + dot_t(wide[1], wu1[...]).astype(BF16)
    da = da.astype(F32)
    dwide = scale * (da - h * (scale * scale * jnp.mean(da * h, -1, keepdims=True)))
    dh = dy[...] + dwide.astype(BF16)
    deep[1] = dh
    for j in range(FF // CHUNK):
        ch = pl.ds(j * CHUNK, CHUNK)
        dz = dot_t(dh, wd0[ch, :]).astype(BF16).astype(F32)
        gate, up = g0[:, ch], u0[:, ch]
        s = jax.nn.sigmoid(gate)
        wide[3, :, ch] = (dz * (gate * s)).astype(BF16)
        wide[2, :, ch] = (dz * up * (s * (1 + gate * (1 - s)))).astype(BF16)


def by_rows(x, dy, weights):
    state = pl.BlockSpec((ROWS, D), lambda i: (i, 0))
    return pl.pallas_call(
        rows_kernel,
        grid=(TOKENS // ROWS,),
        out_shape=tuple(jax.ShapeDtypeStruct(s, BF16) for s in ((2, D, TOKENS), (4, TOKENS, FF), (2, FF, TOKENS), (2, TOKENS, D))),
        in_specs=[state, state] + [HBM] * 3,
        out_specs=(
            pl.BlockSpec((2, D, ROWS), lambda i: (0, 0, i)),
            pl.BlockSpec((4, ROWS, FF), lambda i: (0, i, 0)),
            pl.BlockSpec((2, FF, ROWS), lambda i: (0, 0, i)),
            pl.BlockSpec((2, ROWS, D), lambda i: (0, i, 0)),
        ),
        scratch_shapes=[*[pltpu.VMEM(w.shape[1:], BF16) for w in weights * 2], pltpu.VMEM((ROWS, FF), F32), pltpu.VMEM((ROWS, FF), F32), pltpu.VMEM((ROWS, FF), BF16), pltpu.SemaphoreType.DMA((6,))],
        compiler_params=pltpu.CompilerParams(vmem_limit_bytes=MOST_VMEM),
        name="rows",
    )(x, dy, *weights)


STARTS = (0, 48, 96, 144, 192, 232)
PART = 48


def gate_block(acc, stage, wide):
    def group(i, _):
        rows = pl.ds(pl.multiple_of(i * 56, 8), 56)
        for c in range(4):
            piece = acc[rows, pl.ds(c * LANES, LANES)]
            for z in range(4):
                wide[z, pl.ds(14 * c, 14), :] = piece[14 * z : 14 * z + 14]
        for z in range(4):
            stage[i // 4, i % 4, z] = wide[z].astype(BF16)
        return 0

    lax.fori_loop(0, 16, group, 0)


def down_block(acc, stage):
    def group(i, _):
        for t in range(5):
            rows = acc[pl.ds(pl.multiple_of(i * 40, 8) + 8 * t, 8), :]
            piece = jnp.concatenate([rows[:, c * LANES : (c + 1) * LANES] for c in range(7)], 0)
            stage[i // 4, i % 4, pl.ds(56 * t, 56)] = piece.astype(BF16)
        return 0

    lax.fori_loop(0, 16, group, 0)


def gradients_kernel(*refs):
    (tall, wide, turned, deep), (out, squares, terms), scratch = refs[:4], refs[4:7], refs[7:]
    (lhs, rhs, zs, dh, acc, acc2, stage, stage2, shift, r1, r2, r3, own, f1, f2, sums) = scratch[:16]
    (in_sem, rhs_sem, zs_sem, put_sem, send1, send2, send3, recv1, recv2, recv3, load, send4, recv4) = scratch[16:]
    at = place()

    def fetch_tall(l):
        return pltpu.make_async_copy(tall.at[l], lhs, in_sem.at[0])

    def fetch_deep(l):
        return pltpu.make_async_copy(deep.at[l], dh, in_sem.at[1])

    def fetch_wide(t):
        columns = pl.ds(pl.multiple_of(t % TILES * TILE, TILE), TILE)
        return pltpu.make_async_copy(wide.at[t // TILES, :, columns], rhs.at[t % 2], rhs_sem.at[t % 2])

    def fetch_turned(t):
        rows = pl.ds(pl.multiple_of(t % SIDE * PLANE_ROWS, LANES), PLANE_ROWS)
        return pltpu.make_async_copy(turned.at[t // SIDE, rows], zs.at[t % 2], zs_sem.at[t % 2])

    def put(m, h):
        return pltpu.make_async_copy(stage, terms.at[m, :, :, :, pl.ds(pl.multiple_of(PIECE * h, SUBLANES), PIECE)], put_sem.at[0])

    def put2(m, h):
        return pltpu.make_async_copy(stage2, terms.at[m, h], put_sem.at[1])

    fetch_tall(0).start()
    fetch_wide(0).start()
    fetch_deep(0).start()
    fetch_turned(0).start()
    enter(at)

    def split(c):
        o, s = ORDERS[c], SIGNS[c]
        return o, s, at[o[0]], at[o[1]], at[o[2]]

    def block(m, c, a, i):
        o = ORDERS[c]
        index = [slice(None)] * 3
        index[o[0]] = a
        if i is not None:
            index[o[1]] = i
        return terms.at[(m, *index, pl.ds(STARTS[c], PART))]

    def first(m, c, step, j, start=False):
        o, s, p1, p2, p3 = split(c)
        if start:
            src = block(m, c, wrap(p1 - s), wrap(p2 - s * (1 + j)))
        else:
            src = r1.at[c, m, (step + 2) % STEPS, j]
        return remote(src, r1.at[c, m, step, j], send1.at[c], recv1.at[c, m, step, j], neighbour(at, o[0], s))

    def loading(m, c, step):
        o, s, p1, p2, p3 = split(c)
        return pltpu.make_async_copy(block(m, c, wrap(p1 - s * (2 + step)), None), own.at[c, step], load.at[c, step])

    def second(m, c, step, start=False):
        o, s, p1, p2, p3 = split(c)
        src = r1.at[c, m, 2, 0] if start else r2.at[c, m, (step + 2) % STEPS]
        return remote(src, r2.at[c, m, step], send2.at[c], recv2.at[c, m, step], neighbour(at, o[1], s))

    def third(m, c, step, start=False):
        o, s, p1, p2, p3 = split(c)
        src = r2.at[c, m, 2, wrap(p3 - s)] if start else r3.at[c, m, (step + 2) % STEPS]
        return remote(src, r3.at[c, m, step], send3.at[c], recv3.at[c, m, step], neighbour(at, o[2], s))

    def launch(m):
        for c in range(WAYS):
            for j in range(SIDE):
                first(m, c, 0, j, True).start()
        for step in range(STEPS):
            for c in range(WAYS):
                loading(m, c, step).start()

    def on_first(m, e):
        step, j = e // SIDE, e % SIDE

        @pl.when(j == 0)
        def _():
            for c in range(WAYS):
                loading(m, c, step).wait()

        for c in range(WAYS):
            o, s, p1, p2, p3 = split(c)
            first(m, c, step, j).wait_recv()
            i = wrap(p2 - s * (1 + j))
            mine = own[c, step, i] if o[1] < o[2] else own[c, step, :, i]
            both = r1[c, m, step, j].astype(F32) + mine.astype(F32)
            r1[c, m, step, j] = both.astype(BF16)

            @pl.when(step == 2)
            def _():
                f1[c, j] = both

            @pl.when(step < 2)
            def _():
                first(m, c, step + 1, j).start()

            @pl.when(e == 8)
            def _():
                second(m, c, 0, True).start()

    def on_second(m, step):
        for c in range(WAYS):
            second(m, c, step).wait_recv()
            both = r2[c, m, step].astype(F32) + f1[c, step + 1]
            r2[c, m, step] = both.astype(BF16)

            @pl.when(step == 2)
            def _():
                f2[c] = both
                third(m, c, 0, True).start()

            @pl.when(step < 2)
            def _():
                second(m, c, step + 1).start()

    def on_third(m, step):
        for c in range(WAYS):
            o, s, p1, p2, p3 = split(c)
            third(m, c, step).wait_recv()
            both = (r3[c, m, step].astype(F32) + f2[c, wrap(p3 - s * (2 + step))]).astype(BF16)

            @pl.when(step < 2)
            def _():
                r3[c, m, step] = both
                third(m, c, step + 1).start()

            @pl.when(step == 2)
            def _():
                out[m, pl.ds(STARTS[c], PART)] = both

    def tile(i, _):
        m, h = i // TILES, i % TILES
        kind, l = m % AXES, m // AXES

        @pl.when((h == 0) & (m > 0) & (m < MATRICES + 1))
        def _():
            @pl.when(kind > 0)
            def _():
                put(0, 0).wait()

            @pl.when(kind == 0)
            def _():
                put2(0, 0).wait()

            launch(m - 1)

        @pl.when((m < MATRICES) & (kind < 2))
        def _():
            t = (2 * l + kind) * TILES + h

            @pl.when((kind == 0) & (h == 0))
            def _():
                fetch_tall(l).wait()

                @pl.when(l == 1)
                def _():
                    fetch_deep(1).start()

            fetch_wide(t).wait()

            @pl.when(t < 19)
            def _():
                fetch_wide(t + 1).start()

            acc[...] = dot(lhs[...], rhs[t % 2])

            @pl.when(h > 0)
            def _():
                put(m, h).wait()

            gate_block(acc, stage, shift)
            put(m, h).start()

        @pl.when((m < MATRICES) & (kind == 2) & (h < SIDE))
        def _():
            t = SIDE * l + h

            @pl.when(h == 0)
            def _():
                fetch_deep(l).wait()

                @pl.when(l == 0)
                def _():
                    fetch_tall(1).start()

            fetch_turned(t).wait()

            @pl.when(t < 7)
            def _():
                fetch_turned(t + 1).start()

            acc2[...] = dot(zs[t % 2], dh[...])

            @pl.when(h > 0)
            def _():
                put2(m, h).wait()

            down_block(acc2, stage2)
            put2(m, h).start()

        @pl.when((h > 0) & (h < SIDE) & (m > 2))
        def _():
            on_third(m - 3, h - 1)

        @pl.when((h > 0) & (h < SIDE) & (m > 1) & (m < MATRICES + 2))
        def _():
            on_second(m - 2, h - 1)

        @pl.when((h < SIDE) & (m > 0) & (m < MATRICES + 1))
        def _():
            lax.fori_loop(0, 3, lambda k, _: (on_first(m - 1, 3 * h + k), 0)[1], 0)

        return 0

    lax.fori_loop(0, (MATRICES + AXES) * TILES, tile, 0)

    total = jnp.zeros((SUBLANES, LANES), F32)
    for m in range(MATRICES):
        g = out[m].astype(F32)
        total = total + jnp.sum((g * g).reshape(-1, SUBLANES, LANES), axis=0)
    squares[...] = norm_exchange(at, sums, send4, recv4, total)
    for c in range(WAYS):
        for r, sem in ((r1, send1), (r2, send2), (r3, send3)):
            pltpu.make_async_copy(r.at[c], r.at[c], sem.at[c]).wait()
    for axis in range(STEPS):
        pltpu.make_async_copy(sums.at[axis, pl.ds(0, STEPS)], sums.at[axis, pl.ds(0, STEPS)], send4.at[axis]).wait()


def gradients(tall, wide, turned, deep):
    g, squares, _ = pl.pallas_call(
        gradients_kernel,
        out_shape=(
            jax.ShapeDtypeStruct((MATRICES, BLOCK, LANES), BF16),
            jax.ShapeDtypeStruct((SUBLANES, LANES), F32),
            jax.ShapeDtypeStruct((MATRICES, SIDE, SIDE, SIDE, BLOCK, LANES), BF16),
        ),
        in_specs=[HBM] * 4,
        out_specs=(VMEM, VMEM, HBM),
        scratch_shapes=[
            pltpu.VMEM((D, TOKENS), BF16),
            pltpu.VMEM((2, TOKENS, TILE), BF16),
            pltpu.VMEM((2, PLANE_ROWS, TOKENS), BF16),
            pltpu.VMEM((TOKENS, D), BF16),
            pltpu.VMEM((D, TILE), F32),
            pltpu.VMEM((PLANE_ROWS, D), F32),
            pltpu.VMEM((SIDE, SIDE, SIDE, PIECE, LANES), BF16),
            pltpu.VMEM((SIDE, SIDE, BLOCK, LANES), BF16),
            pltpu.VMEM((SIDE, PIECE, LANES), F32),
            pltpu.VMEM((WAYS, MATRICES, STEPS, SIDE, SIDE, PART, LANES), BF16),
            pltpu.VMEM((WAYS, MATRICES, STEPS, SIDE, PART, LANES), BF16),
            pltpu.VMEM((WAYS, MATRICES, STEPS, PART, LANES), BF16),
            pltpu.VMEM((WAYS, STEPS, SIDE, SIDE, PART, LANES), BF16),
            pltpu.VMEM((WAYS, SIDE, SIDE, PART, LANES), F32),
            pltpu.VMEM((WAYS, SIDE, PART, LANES), F32),
            pltpu.VMEM((AXES, SIDE, SUBLANES, LANES), F32),
            *[DMA((2,))] * 4,
            *[DMA((WAYS,))] * AXES,
            DMA((WAYS, MATRICES, STEPS, SIDE)), *[DMA((WAYS, MATRICES, STEPS))] * 2,
            DMA((WAYS, STEPS)),
            DMA((AXES,)), DMA((AXES, STEPS)),
        ],
        compiler_params=pltpu.CompilerParams(collective_id=0, has_side_effects=True, vmem_limit_bytes=MOST_VMEM),
        name="gradients",
    )(tall, wide, turned, deep)
    return g, squares


def solution(mesh):
    rep, dp = mesh.axis_names

    def step(x, dy, *arrays):
        weights, m, v = (arrays[i : i + 3] for i in (0, 3, 6))
        g, total = gradients(*by_rows(x[0], dy[0], weights))
        me = lax.axis_index(dp)
        mine = [lax.dynamic_slice_in_dim(w, me * b.shape[1], b.shape[1], 1) for w, b in zip(weights, m, strict=True)]
        new, new_m, new_v = adam(sum(w.size for w in weights), g, total, mine, m, v)
        return (*natural(all_gather(new)), *new_m, *new_v)

    whole, rows, sequences = P(None, None, None), P(None, dp, None), P((rep, dp), None, None)
    return jax.shard_map(
        step,
        mesh=mesh,
        in_specs=(sequences, sequences, *[whole] * 3, *[rows] * 6),
        out_specs=(*[P(rep, None, None)] * 3, *[P(rep, dp, None)] * 6),
        check_vma=False,
    )
```

time: 1630 us -> 438 us (0.27)
  blocking collectives: 863 us -> 0 us
  Pallas kernels: 0 us -> 426 us
  matrix products: 275 us -> 0 us
  waiting for transfers between devices: 226 us -> 0 us
  starting transfers between devices: 102 us -> 0 us
  local copies, waits for them, and re-layouts: 76.1 us -> 10.4 us
  other arithmetic: 56.6 us -> 0 us
  between operations: 19.1 us -> 0.75 us
    unnamed x1 -> x0, blocking collectives: 690 us -> none
    pallas_call x0 -> x5, Pallas kernels: none -> 426 us  [the longest x1 178 us: gradients(): pl.pallas_call(gradients_kernel, out_shape=(jax.ShapeDtypeStruct((MATRICE...]
    dot_general x15 -> x0, matrix products: 275 us -> none  [the longest x5 99.4 us: layer(): up = jnp.dot(a, w['w_up'], preferred_element_type=jnp.float32)]
    reshape x3 -> x0, waiting for transfers between devices: 226 us -> none  [step(): t.reshape(-1, *t.shape[2:])]
    reduce_sum x1 -> x0, blocking collectives: 173 us -> none  [of_a_group(): jnp.sum(g * g)]
    unnamed x34 -> x0, starting transfers between devices: 102 us -> none
    unnamed x81 -> x24, local copies, waits for them, and re-layouts: 72.8 us -> 6.9 us
    unnamed x8 -> x0, other arithmetic: 45.1 us -> none
  transfers between devices with their start and end apart: 37 -> 0, of which waited for: 3 -> 0; matrix products, arithmetic and copies ran while one was open for 53% -> 0% of each run, Pallas kernels for 0% -> 0%
where the time goes in v3:
time: 438 us
  Pallas kernels  426 us (97%)
  local copies, waits for them, and re-layouts  10.4 us (2%)
    pallas_call x1, Pallas kernels, gradients(): pl.pallas_call(gradients_kernel, out_shape=(jax.ShapeDtypeStruct((MATRICE...  178 us
    pallas_call x1, Pallas kernels, by_rows(): pl.pallas_call(rows_kernel, grid=(TOKENS // ROWS,), out_shape=tuple((jax....  127 us
    pallas_call x1, Pallas kernels, all_gather(): pl.pallas_call(ag_kernel, out_shape=tuple((jax.ShapeDtypeStruct((SIDE, SI...  93.9 us
    pallas_call x1, Pallas kernels, natural(): pl.pallas_call(natural_kernel, grid=(16,), out_shape=tuple((jax.ShapeDtyp...  24.8 us

profile of v3, /device:TPU:0, one launch (start us, length us, event | category | flops | bytes accessed | tf_op | source)
XLA Modules:
  0.0 437.5 jit_solution(4419149919115754592)
XLA Ops:
  0.6 126.7 %rows.1 = (bf16[2,896,2048]{2,1,0:T(8,128)(2,1)}, bf16[4,2048,2560]{2,1,0:T(8,128)(2,1)}, bf16[2,2560,2048]{2,1,0:T(8,128)(2,1)}, bf16[2,2048,896]{2,1,0:T(8,128)(2,1)}) custom-call(bf16[2048,896]{1,0:T(8,128)(2,1)} %bitcast.14, bf16[2048,896]{1,0:T(8,128)(2,1)} %bitcast.15, bf16[2,896,2560]{2,1,0:T(8,128)(2,1)} %refs_0_.1, bf16[2,896,2560]{2,1,0:T(8,128)(2,1)} %refs_1_.1, ...), custom_call_target="tpu_custom_call" | custom-call | tf_op jit(solution)/shard_map/rows/pallas_call | solution.py:307
  127.3 0.0 copy-start.4
  127.3 0.0 copy-start.5
  127.3 0.0 copy-start.6
  127.3 0.0 copy-start.7
  127.4 177.7 %gradients.1 = (bf16[6,280,128]{2,1,0:T(8,128)(2,1)}, f32[8,128]{1,0:T(8,128)}, bf16[6,4,4,4,280,128]{5,4,3,2,1,0:T(8,128)(2,1)}) custom-call(bf16[2,896,2048]{2,1,0:T(8,128)(2,1)} %get-tuple-element.31.refs_0_, bf16[4,2048,2560]{2,1,0:T(8,128)(2,1)} %get-tuple-element.32.refs_1_, bf16[2,2560,2048]{2,1,0:T(8,128)(2,1)} %get-tuple-element.33.refs_2_, ...), custom_call_target="tpu_custom_call" | custom-call | tf_op jit(solution)/shard_map/gradients/pallas_call | solution.py:584
  305.1 1.9 constant_dynamic-slice_fusion.1
  306.9 1.6 constant_dynamic-slice_fusion.refs_2_
  308.5 0.0 copy-done.4
  308.5 0.8 copy.20.refs_3_
  309.3 0.0 copy-done.5
  309.3 0.8 copy.21.refs_4_
  310.1 0.0 copy-done.6
  310.1 0.8 copy.22.refs_6_
  310.9 0.0 copy-done.7
  310.9 0.8 copy.23.refs_7_
  311.7 3.4 adam.1
  315.1 93.9 %gather.1 = (bf16[4,4,4,280,128]{4,3,2,1,0:T(8,128)(2,1)}, bf16[4,4,4,280,128]{4,3,2,1,0:T(8,128)(2,1)}, bf16[4,4,4,280,128]{4,3,2,1,0:T(8,128)(2,1)}, bf16[4,4,...) custom-call(bf16[6,280,128]{2,1,0:T(8,128)(2,1)} %get-tuple-element.37.refs_0_), custom_call_target="tpu_custom_call" | custom-call | tf_op jit(solution)/shard_map/gather/pallas_call | solution.py:152
  408.9 0.0 copy-start.3
  408.9 0.0 copy-start.2
  409.0 0.0 copy-start.1
  409.0 0.0 copy-start
  409.0 24.8 %natural.1 = (bf16[2,896,2560]{2,1,0:T(8,128)(2,1)}, bf16[2,896,2560]{2,1,0:T(8,128)(2,1)}, bf16[2,2560,896]{2,1,0:T(8,128)(2,1)}) custom-call(bf16[64,280,128]{2,1,0:T(8,128)(2,1)} %bitcast.8, bf16[64,280,128]{2,1,0:T(8,128)(2,1)} %bitcast.9, bf16[64,280,128]{2,1,0:T(8,128)(2,1)} %bitcast.10, bf16[64,280,128]{2,1,0:T(8,128)(2,1)} %bitcast.11, ...), custom_call_target="tpu_custom_call" | custom-call | tf_op jit(solution)/shard_map/natural/pallas_call | solution.py:217
  433.8 0.0 copy-done.3
  433.8 0.9 copy.24
  434.7 0.0 copy-done.2
  434.7 0.9 copy.25
  435.7 0.0 copy-done.1
  435.7 0.9 copy.26
  436.6 0.0 copy-done
  436.6 0.9 copy.27
Async XLA Ops:
  127.3 181.2 %copy-start.4 = (f32[2,14,2560]{2,0,1:T(2,128)S(1)}, f32[2,14,2560]{2,0,1:T(2,128)}, u32[]{:S(2)}) copy-start(f32[2,14,2560]{2,0,1:T(2,128)} %param.16) | copy-start | bytes 860164
  127.3 182.0 %copy-start.5 = (f32[2,14,2560]{2,0,1:T(2,128)S(1)}, f32[2,14,2560]{2,0,1:T(2,128)}, u32[]{:S(2)}) copy-start(f32[2,14,2560]{2,0,1:T(2,128)} %param.17) | copy-start | bytes 860164
  127.3 182.8 %copy-start.6 = (f32[2,14,2560]{2,0,1:T(2,128)S(1)}, f32[2,14,2560]{2,0,1:T(2,128)}, u32[]{:S(2)}) copy-start(f32[2,14,2560]{2,0,1:T(2,128)} %param.19) | copy-start | bytes 860164
  127.3 183.5 %copy-start.7 = (f32[2,14,2560]{2,0,1:T(2,128)S(1)}, f32[2,14,2560]{2,0,1:T(2,128)}, u32[]{:S(2)}) copy-start(f32[2,14,2560]{2,0,1:T(2,128)} %param.20) | copy-start | bytes 860164
  408.9 24.8 %copy-start.3 = (f32[2,14,2560]{2,1,0:T(8,128)S(1)}, f32[2,14,2560]{2,1,0:T(8,128)}, u32[]{:S(2)}) copy-start(f32[2,14,2560]{2,1,0:T(8,128)} %get-tuple-element.56) | copy-start | bytes 860164
  408.9 25.8 %copy-start.2 = (f32[2,14,2560]{2,1,0:T(8,128)S(1)}, f32[2,14,2560]{2,1,0:T(8,128)}, u32[]{:S(2)}) copy-start(f32[2,14,2560]{2,1,0:T(8,128)} %get-tuple-element.57) | copy-start | bytes 860164
  409.0 26.7 %copy-start.1 = (f32[2,14,2560]{2,1,0:T(8,128)S(1)}, f32[2,14,2560]{2,1,0:T(8,128)}, u32[]{:S(2)}) copy-start(f32[2,14,2560]{2,1,0:T(8,128)} %get-tuple-element.59) | copy-start | bytes 860164
  409.0 27.6 %copy-start = (f32[2,14,2560]{2,1,0:T(8,128)S(1)}, f32[2,14,2560]{2,1,0:T(8,128)}, u32[]{:S(2)}) copy-start(f32[2,14,2560]{2,1,0:T(8,128)} %get-tuple-element.60) | copy-start | bytes 860164

commit v4 on v3

--- a/solution.py
+++ b/solution.py
@@ -151,11 +151,11 @@
 def all_gather(mine):
     return pl.pallas_call(
         ag_kernel,
-        out_shape=tuple(jax.ShapeDtypeStruct((SIDE, SIDE, SIDE, *mine.shape[1:]), BF16) for _ in range(WAYS)),
+        out_shape=(pltpu.VMEM((SIDE, SIDE, SIDE, *mine.shape[1:]), BF16),) * WAYS,
         in_specs=[VMEM],
-        out_specs=(HBM,) * WAYS,
+        out_specs=(VMEM,) * WAYS,
         scratch_shapes=[DMA((WAYS, AXES)), DMA((WAYS, SIDE)), *[DMA((WAYS, SIDE, SIDE))] * 3, DMA((WAYS,))],
-        compiler_params=pltpu.CompilerParams(collective_id=1, has_side_effects=True),
+        compiler_params=pltpu.CompilerParams(collective_id=1, has_side_effects=True, vmem_limit_bytes=MOST_VMEM // SUBLANES),
         name="gather",
     )(mine)
 
@@ -200,32 +200,34 @@
 
 
 def natural_kernel(*refs):
-    blocks, outs, wide = refs[:6], refs[6:9], refs[9:]
-    for t in range(3):
-        for l in range(2):
-            for z in range(4):
-                block = blocks[2 * t + l][z].astype(F32)
-                rows = outs[t].shape[1] // 4
+    gathered, outs, wide = refs[:MATRICES], refs[MATRICES:-AXES], refs[-AXES:]
+    first = pl.program_id(0) * SIDE
+    for t in range(AXES):
+        for l in range(LAYERS):
+            for z in range(SIDE):
+                block = gathered[LAYERS * t + l][first + z].astype(F32)
+                rows = outs[t].shape[1] // SIDE
                 for row, n, column, at in tiles_of(t, rows, outs[t].shape[2]):
                     wide[t][pl.ds(z * rows + row, n), pl.ds(column, LANES)] = block[at : at + n]
             outs[t][l] = wide[t][...].astype(BF16)
 
 
-def natural(blocks):
-    blocks = [b.reshape(64, *b.shape[3:]) for b in blocks]
-    shapes = ((2, 896, 2560), (2, 896, 2560), (2, 2560, 896))
+def natural(gathered):
+    shapes = (GATE, GATE, DOWN)
     return pl.pallas_call(
         natural_kernel,
-        grid=(16,),
-        out_shape=tuple(jax.ShapeDtypeStruct(s, BF16) for s in shapes),
-        in_specs=[pl.BlockSpec((4, 280, 128), lambda i: (i, 0, 0))] * 6,
-        out_specs=tuple(pl.BlockSpec((2, s[1] // 16, s[2]), lambda i: (0, i, 0)) for s in shapes),
-        scratch_shapes=[pltpu.VMEM((s[1] // 16, s[2]), F32) for s in shapes],
+        grid=(PLANE,),
+        out_shape=tuple(jax.ShapeDtypeStruct((LAYERS, *s), BF16) for s in shapes),
+        in_specs=[VMEM] * MATRICES,
+        out_specs=tuple(pl.BlockSpec((LAYERS, s[0] // PLANE, s[1]), lambda i: (0, i, 0)) for s in shapes),
+        scratch_shapes=[pltpu.VMEM((s[0] // PLANE, s[1]), F32) for s in shapes],
+        compiler_params=pltpu.CompilerParams(vmem_limit_bytes=MOST_VMEM // SIDE),
         name="natural",
-    )(*blocks)
+    )(*[g.reshape(DEVICES, BLOCK, LANES) for g in gathered])
 
 
 D, FF, TOKENS = 896, 2560, 2048
+GATE, DOWN = (D, FF), (FF, D)
 ROWS, CHUNK, TILE = 256, 512, 512
 TILES, PIECE, PLANE_ROWS = FF // TILE, BLOCK * TILE // FF, FF // SIDE
 NT = (((1,), (1,)), ((), ()))
@@ -411,15 +413,15 @@
         src = r1.at[c, m, 2, 0] if start else r2.at[c, m, (step + 2) % STEPS]
         return remote(src, r2.at[c, m, step], send2.at[c], recv2.at[c, m, step], neighbour(at, o[1], s))
 
-    def third(m, c, step, start=False):
+    def third(m, c, k):
         o, s, p1, p2, p3 = split(c)
-        src = r2.at[c, m, 2, wrap(p3 - s)] if start else r3.at[c, m, (step + 2) % STEPS]
-        return remote(src, r3.at[c, m, step], send3.at[c], recv3.at[c, m, step], neighbour(at, o[2], s))
+        return remote(r2.at[c, m, 2, wrap(p3 + k + 1)], r3.at[c, m, k], send3.at[c], recv3.at[c, m, k], neighbour(at, o[2], k + 1))
 
     def launch(m):
         for c in range(WAYS):
             for j in range(SIDE):
                 first(m, c, 0, j, True).start()
+    def load_own(m):
         for step in range(STEPS):
             for c in range(WAYS):
                 loading(m, c, step).start()
@@ -461,26 +463,21 @@
             @pl.when(step == 2)
             def _():
                 f2[c] = both
-                third(m, c, 0, True).start()
+                for k in range(STEPS):
+                    third(m, c, k).start()
 
             @pl.when(step < 2)
             def _():
                 second(m, c, step + 1).start()
 
-    def on_third(m, step):
+    def on_third(m):
         for c in range(WAYS):
             o, s, p1, p2, p3 = split(c)
-            third(m, c, step).wait_recv()
-            both = (r3[c, m, step].astype(F32) + f2[c, wrap(p3 - s * (2 + step))]).astype(BF16)
-
-            @pl.when(step < 2)
-            def _():
-                r3[c, m, step] = both
-                third(m, c, step + 1).start()
-
-            @pl.when(step == 2)
-            def _():
-                out[m, pl.ds(STARTS[c], PART)] = both
+            total = f2[c, p3]
+            for k in range(STEPS):
+                third(m, c, k).wait_recv()
+                total = total + r3[c, m, k].astype(F32)
+            out[m, pl.ds(STARTS[c], PART)] = total.astype(BF16)
 
     def tile(i, _):
         m, h = i // TILES, i % TILES
@@ -552,21 +549,27 @@
             down_block(acc2, stage2)
             put2(m, h).start()
 
-        @pl.when((h > 0) & (h < SIDE) & (m > 2))
-        def _():
-            on_third(m - 3, h - 1)
-
-        @pl.when((h > 0) & (h < SIDE) & (m > 1) & (m < MATRICES + 2))
-        def _():
-            on_second(m - 2, h - 1)
-
-        @pl.when((h < SIDE) & (m > 0) & (m < MATRICES + 1))
-        def _():
-            lax.fori_loop(0, 3, lambda k, _: (on_first(m - 1, 3 * h + k), 0)[1], 0)
+        @pl.when((h == SIDE) & (m > 1))
+        def _():
+            on_third(m - 2)
+
+        @pl.when((h != 1) & (h != SIDE) & (m > 1) & (m < MATRICES + 2))
+        def _():
+            on_second(m - 2, (h + 1) // 2)
+
+        ring, turn = (i - 1) // TILES - 1, (i - 1) % TILES
+
+        @pl.when((ring >= 0) & (ring < MATRICES))
+        def _():
+            lax.fori_loop(TILES * turn // 2, TILES * (turn + 1) // 2, lambda e, _: (on_first(ring, e), 0)[1], 0)
+
+        @pl.when((h == 0) & (m > 0) & (m < MATRICES + 1))
+        def _():
+            load_own(m - 1)
 
         return 0
 
-    lax.fori_loop(0, (MATRICES + AXES) * TILES, tile, 0)
+    lax.fori_loop(0, (MATRICES + 2) * TILES, tile, 0)
 
     total = jnp.zeros((SUBLANES, LANES), F32)
     for m in range(MATRICES):

time: 438 us -> 420 us (0.959)
  Pallas kernels: 426 us -> 408 us
    pallas_call x2, Pallas kernels: 119 us -> 107 us  [the longest x1 94.7 us: all_gather(): pl.pallas_call(ag_kernel, out_shape=(pltpu.VMEM((SIDE, SIDE, SIDE, *mine....]
    pallas_call x1, Pallas kernels: 178 us -> 171 us  [gradients(): pl.pallas_call(gradients_kernel, out_shape=(jax.ShapeDtypeStruct((MATRICE...]
where the time goes in v4:
time: 420 us
  Pallas kernels  408 us (97%)
  local copies, waits for them, and re-layouts  11.4 us (3%)
    pallas_call x1, Pallas kernels, gradients(): pl.pallas_call(gradients_kernel, out_shape=(jax.ShapeDtypeStruct((MATRICE...  171 us
    pallas_call x1, Pallas kernels, by_rows(): pl.pallas_call(rows_kernel, grid=(TOKENS // ROWS,), out_shape=tuple((jax....  127 us
    pallas_call x1, Pallas kernels, all_gather(): pl.pallas_call(ag_kernel, out_shape=(pltpu.VMEM((SIDE, SIDE, SIDE, *mine....  94.7 us
    pallas_call x1, Pallas kernels, natural(): pl.pallas_call(natural_kernel, grid=(PLANE,), out_shape=tuple((jax.ShapeD...  12.7 us

profile of v4, /device:TPU:0, one launch (start us, length us, event | category | flops | bytes accessed | tf_op | source)
XLA Modules:
  0.0 420.1 jit_solution(2244075279506872222)
XLA Ops:
  0.6 126.7 %rows.1 = (bf16[2,896,2048]{2,1,0:T(8,128)(2,1)}, bf16[4,2048,2560]{2,1,0:T(8,128)(2,1)}, bf16[2,2560,2048]{2,1,0:T(8,128)(2,1)}, bf16[2,2048,896]{2,1,0:T(8,128)(2,1)}) custom-call(bf16[2048,896]{1,0:T(8,128)(2,1)} %bitcast.14, bf16[2048,896]{1,0:T(8,128)(2,1)} %bitcast.15, bf16[2,896,2560]{2,1,0:T(8,128)(2,1)} %refs_0_.1, bf16[2,896,2560]{2,1,0:T(8,128)(2,1)} %refs_1_.1, ...), custom_call_target="tpu_custom_call" | custom-call | tf_op jit(solution)/shard_map/rows/pallas_call | solution.py:309
  127.3 0.0 copy-start.5
  127.3 0.0 copy-start.6
  127.3 0.0 copy-start.7
  127.3 0.0 copy-start.8
  127.4 170.6 %gradients.1 = (bf16[6,280,128]{2,1,0:T(8,128)(2,1)}, f32[8,128]{1,0:T(8,128)}, bf16[6,4,4,4,280,128]{5,4,3,2,1,0:T(8,128)(2,1)}) custom-call(bf16[2,896,2048]{2,1,0:T(8,128)(2,1)} %get-tuple-element.31.refs_0_, bf16[4,2048,2560]{2,1,0:T(8,128)(2,1)} %get-tuple-element.32.refs_1_, bf16[2,2560,2048]{2,1,0:T(8,128)(2,1)} %get-tuple-element.33.refs_2_, ...), custom_call_target="tpu_custom_call" | custom-call | tf_op jit(solution)/shard_map/gradients/pallas_call | solution.py:587
  298.0 1.9 constant_dynamic-slice_fusion.1
  299.8 1.6 constant_dynamic-slice_fusion.refs_2_
  301.4 0.0 copy-done.5
  301.4 0.8 copy.20.refs_3_
  302.2 0.0 copy-done.6
  302.2 0.8 copy.21.refs_4_
  303.0 0.0 copy-done.7
  303.0 0.8 copy.22.refs_6_
  303.8 0.0 copy-done.8
  303.8 0.8 copy.23.refs_7_
  304.6 3.4 adam.1
  308.0 1.0 copy-done
  309.0 94.7 %gather.1 = (bf16[4,4,4,280,128]{4,3,2,1,0:T(8,128)(2,1)S(1)}, bf16[4,4,4,280,128]{4,3,2,1,0:T(8,128)(2,1)S(1)}, bf16[4,4,4,280,128]{4,3,2,1,0:T(8,128)(2,1)S(1)...) custom-call(bf16[6,280,128]{2,1,0:T(8,128)(2,1)S(1)} %copy-done), custom_call_target="tpu_custom_call" | custom-call | tf_op jit(solution)/shard_map/gather/pallas_call | solution.py:152
  403.7 0.0 copy-start.4
  403.7 0.0 copy-start.3
  403.7 0.0 copy-start.2
  403.7 0.0 copy-start.1
  403.7 12.7 %natural.1 = (bf16[2,896,2560]{2,1,0:T(8,128)(2,1)}, bf16[2,896,2560]{2,1,0:T(8,128)(2,1)}, bf16[2,2560,896]{2,1,0:T(8,128)(2,1)}) custom-call(bf16[64,280,128]{2,1,0:T(8,128)(2,1)S(1)} %bitcast.8, bf16[64,280,128]{2,1,0:T(8,128)(2,1)S(1)} %bitcast.9, bf16[64,280,128]{2,1,0:T(8,128)(2,1)S(1)} %bitcast.10, bf16[64,280,128]{2,1,0:T(8,128)(2,1)S(1)} %bitcast.11, ...), custom_call_target="tpu_custom_call" | custom-call | tf_op jit(solution)/shard_map/natural/pallas_call | solution.py:217
  416.4 0.0 copy-done.4
  416.4 0.9 copy.24
  417.3 0.0 copy-done.3
  417.3 0.9 copy.25
  418.2 0.0 copy-done.2
  418.2 0.9 copy.26
  419.2 0.0 copy-done.1
  419.2 0.9 copy.27
  (1 shorter events, 0.0 us)
Async XLA Ops:
  127.3 174.1 %copy-start.5 = (f32[2,14,2560]{2,0,1:T(2,128)S(1)}, f32[2,14,2560]{2,0,1:T(2,128)}, u32[]{:S(2)}) copy-start(f32[2,14,2560]{2,0,1:T(2,128)} %param.16) | copy-start | bytes 860164
  127.3 174.9 %copy-start.6 = (f32[2,14,2560]{2,0,1:T(2,128)S(1)}, f32[2,14,2560]{2,0,1:T(2,128)}, u32[]{:S(2)}) copy-start(f32[2,14,2560]{2,0,1:T(2,128)} %param.17) | copy-start | bytes 860164
  127.3 175.7 %copy-start.7 = (f32[2,14,2560]{2,0,1:T(2,128)S(1)}, f32[2,14,2560]{2,0,1:T(2,128)}, u32[]{:S(2)}) copy-start(f32[2,14,2560]{2,0,1:T(2,128)} %param.19) | copy-start | bytes 860164
  127.3 176.4 %copy-start.8 = (f32[2,14,2560]{2,0,1:T(2,128)S(1)}, f32[2,14,2560]{2,0,1:T(2,128)}, u32[]{:S(2)}) copy-start(f32[2,14,2560]{2,0,1:T(2,128)} %param.20) | copy-start | bytes 860164
  308.0 1.0 copy-start
  403.7 12.7 %copy-start.4 = (f32[2,14,2560]{2,1,0:T(8,128)S(1)}, f32[2,14,2560]{2,1,0:T(8,128)}, u32[]{:S(2)}) copy-start(f32[2,14,2560]{2,1,0:T(8,128)} %get-tuple-element.56) | copy-start | bytes 860164
  403.7 13.6 %copy-start.3 = (f32[2,14,2560]{2,1,0:T(8,128)S(1)}, f32[2,14,2560]{2,1,0:T(8,128)}, u32[]{:S(2)}) copy-start(f32[2,14,2560]{2,1,0:T(8,128)} %get-tuple-element.57) | copy-start | bytes 860164
  403.7 14.6 %copy-start.2 = (f32[2,14,2560]{2,1,0:T(8,128)S(1)}, f32[2,14,2560]{2,1,0:T(8,128)}, u32[]{:S(2)}) copy-start(f32[2,14,2560]{2,1,0:T(8,128)} %get-tuple-element.59) | copy-start | bytes 860164
  403.7 15.5 %copy-start.1 = (f32[2,14,2560]{2,1,0:T(8,128)S(1)}, f32[2,14,2560]{2,1,0:T(8,128)}, u32[]{:S(2)}) copy-start(f32[2,14,2560]{2,1,0:T(8,128)} %get-tuple-element.60) | copy-start | bytes 860164

commit v5 on v4

--- a/solution.py
+++ b/solution.py
@@ -168,35 +168,64 @@
 
 
 def adam_kernel(count, g, total, *refs):
-    ws, ms, vs, new, new_m, new_v, wide_g, wide_w = refs[0:3], refs[3:6], refs[6:9], refs[9], refs[10:13], refs[13:16], refs[16], refs[17]
+    refs = list(refs)
+    ws, ms, vs = (refs[AXES * k : AXES * (k + 1)] for k in range(3))
+    new, *refs = refs[3 * AXES :]
+    new_m, new_v, windows, owns = (refs[AXES * k : AXES * (k + 1)] for k in range(4))
+    wide_g, wide_w, sems = refs[4 * AXES :]
+    me = lax.axis_index("dp")
+    taken = []
+    for t in range(AXES):
+        rows = windows[t].shape[1]
+        first = pl.multiple_of((me // SIDE if t < 2 else me) * rows, SUBLANES)
+        taken.append(pltpu.make_async_copy(ws[t].at[:, pl.ds(first, rows)], windows[t], sems.at[t]))
+    for copy in taken:
+        copy.start()
     factor = jnp.minimum(1.0, 0.5 * lax.rsqrt(jnp.full((1, 1), jnp.sum(total[...])) / count + 1e-30))
-    for t in range(3):
-        for l in range(2):
-            c = 2 * t + l
-            wide_g[...] = g[TAKEN[c]].astype(F32) * factor
-            for row, rows, column, at in tiles_of(t, *ms[t].shape[1:]):
-                here = (l, pl.ds(row, rows), pl.ds(column, LANES))
-                grad = wide_g[pl.ds(at, rows), :]
+    for t in range(AXES):
+        taken[t].wait()
+        rows, columns = owns[t].shape[1:]
+        if t < 2:
+            for z in range(SIDE):
+
+                @pl.when(me % SIDE == z)
+                def _():
+                    for l in range(LAYERS):
+                        owns[t][l] = windows[t][l].astype(F32)[z * rows : (z + 1) * rows]
+
+        for l in range(LAYERS):
+            wide_g[...] = g[TAKEN[LAYERS * t + l]].astype(F32) * factor
+            for row, n, column, at in tiles_of(t, rows, columns):
+                lanes = pl.ds(column, LANES)
+                here = (slice(None), l, lanes) if t < 2 else (l, pl.ds(row, n), lanes)
+                grad = wide_g[pl.ds(at, n), :]
                 m = 0.9 * ms[t][here] + 0.1 * grad
                 v = 0.95 * vs[t][here] + 0.05 * grad * grad
-                w = ws[t][here].astype(F32)
+                w = (owns if t < 2 else windows)[t][l, pl.ds(row, n), lanes].astype(F32)
                 new_m[t][here] = m
                 new_v[t][here] = v
-                wide_w[pl.ds(at, rows), :] = w - 0.02 * (m * lax.rsqrt(v + 1e-8) + 0.1 * w)
-            new[c] = wide_w[...].astype(BF16)
+                wide_w[pl.ds(at, n), :] = w - 0.02 * (m * lax.rsqrt(v + 1e-8) + 0.1 * w)
+            new[LAYERS * t + l] = wide_w[...].astype(BF16)
 
 
 def adam(count, g, total, ws, ms, vs):
+    ms, vs = ([*(jnp.swapaxes(a, 0, 1) for a in arrays[:2]), arrays[2]] for arrays in (ms, vs))
     like = [jax.ShapeDtypeStruct(m.shape, F32) for m in ms]
-    out = pl.pallas_call(
+    new, *moments = pl.pallas_call(
         functools.partial(adam_kernel, count),
-        out_shape=(jax.ShapeDtypeStruct(g.shape, BF16), *like, *like),
-        in_specs=[VMEM] * 11,
-        out_specs=(VMEM,) * 7,
-        scratch_shapes=[pltpu.VMEM(g.shape[1:], F32)] * 2,
+        out_shape=(pltpu.VMEM(g.shape, BF16), *like, *like),
+        in_specs=[VMEM] * 2 + [HBM] * AXES + [VMEM] * AXES * 2,
+        out_specs=(VMEM,) * (1 + AXES * 2),
+        scratch_shapes=[
+            *[pltpu.VMEM((LAYERS, w.shape[1] // n, w.shape[2]), BF16) for w, n in zip(ws, (PLANE, PLANE, DEVICES), strict=True)],
+            *[pltpu.VMEM((LAYERS, w.shape[1] // DEVICES, w.shape[2]), F32) for w in ws],
+            *[pltpu.VMEM(g.shape[1:], F32)] * 2,
+            DMA((AXES,)),
+        ],
+        compiler_params=pltpu.CompilerParams(vmem_limit_bytes=MOST_VMEM),
         name="adam",
     )(g, total, *ws, *ms, *vs)
-    return out[0], out[1:4], out[4:7]
+    return new, *([*(jnp.swapaxes(a, 0, 1) for a in part[:2]), part[2]] for part in (moments[:AXES], moments[AXES:]))
 
 
 def natural_kernel(*refs):
@@ -255,7 +284,7 @@
 
     @pl.when(first)
     def _():
-        for k in range(6):
+        for k in range(2):
             fetch(k).start()
 
     def ready(*ks):
@@ -263,6 +292,9 @@
         def _():
             for k in ks:
                 fetch(k).wait()
+            if 0 in ks:
+                for k in range(2, MATRICES):
+                    fetch(k).start()
 
     a = (x[...].astype(F32) * scale_of(x[...].astype(F32))).astype(BF16)
     tall[1] = a.T
@@ -317,7 +349,7 @@
             pl.BlockSpec((2, FF, ROWS), lambda i: (0, 0, i)),
             pl.BlockSpec((2, ROWS, D), lambda i: (0, i, 0)),
         ),
-        scratch_shapes=[*[pltpu.VMEM(w.shape[1:], BF16) for w in weights * 2], pltpu.VMEM((ROWS, FF), F32), pltpu.VMEM((ROWS, FF), F32), pltpu.VMEM((ROWS, FF), BF16), pltpu.SemaphoreType.DMA((6,))],
+        scratch_shapes=[*[pltpu.VMEM(w.shape[1:], BF16) for w in weights * 2], pltpu.VMEM((ROWS, FF), F32), pltpu.VMEM((ROWS, FF), F32), pltpu.VMEM((ROWS, FF), BF16), DMA((MATRICES,))],
         compiler_params=pltpu.CompilerParams(vmem_limit_bytes=MOST_VMEM),
         name="rows",
     )(x, dy, *weights)
@@ -628,9 +660,7 @@
     def step(x, dy, *arrays):
         weights, m, v = (arrays[i : i + 3] for i in (0, 3, 6))
         g, total = gradients(*by_rows(x[0], dy[0], weights))
-        me = lax.axis_index(dp)
-        mine = [lax.dynamic_slice_in_dim(w, me * b.shape[1], b.shape[1], 1) for w, b in zip(weights, m, strict=True)]
-        new, new_m, new_v = adam(sum(w.size for w in weights), g, total, mine, m, v)
+        new, new_m, new_v = adam(sum(w.size for w in weights), g, total, weights, m, v)
         return (*natural(all_gather(new)), *new_m, *new_v)
 
     whole, rows, sequences = P(None, None, None), P(None, dp, None), P((rep, dp), None, None)

time: 420 us -> 413 us (0.983)
  local copies, waits for them, and re-layouts: 11.4 us -> 0 us
    unnamed x26 -> x0, local copies, waits for them, and re-layouts: 7.92 us -> none
where the time goes in v5:
time: 413 us
  Pallas kernels  412 us (100%)
    pallas_call x1, Pallas kernels, gradients(): pl.pallas_call(gradients_kernel, out_shape=(jax.ShapeDtypeStruct((MATRICE...  171 us
    pallas_call x1, Pallas kernels, by_rows(): pl.pallas_call(rows_kernel, grid=(TOKENS // ROWS,), out_shape=tuple((jax....  128 us
    pallas_call x1, Pallas kernels, all_gather(): pl.pallas_call(ag_kernel, out_shape=(pltpu.VMEM((SIDE, SIDE, SIDE, *mine....  95.1 us
    pallas_call x1, Pallas kernels, natural(): pl.pallas_call(natural_kernel, grid=(PLANE,), out_shape=tuple((jax.ShapeD...  12.7 us

profile of v5, /device:TPU:0, one launch (start us, length us, event | category | flops | bytes accessed | tf_op | source)
XLA Modules:
  0.0 413.1 jit_solution(16663463147562517910)
XLA Ops:
  0.6 127.8 %rows.1 = (bf16[2,896,2048]{2,1,0:T(8,128)(2,1)}, bf16[4,2048,2560]{2,1,0:T(8,128)(2,1)}, bf16[2,2560,2048]{2,1,0:T(8,128)(2,1)}, bf16[2,2048,896]{2,1,0:T(8,128)(2,1)}) custom-call(bf16[2048,896]{1,0:T(8,128)(2,1)} %bitcast.22, bf16[2048,896]{1,0:T(8,128)(2,1)} %bitcast.23, bf16[2,896,2560]{2,1,0:T(8,128)(2,1)} %refs_0_.3, bf16[2,896,2560]{2,1,0:T(8,128)(2,1)} %refs_1_.3, ...), custom_call_target="tpu_custom_call" | custom-call | tf_op jit(solution)/shard_map/rows/pallas_call | solution.py:341
  128.4 170.8 %gradients.1 = (bf16[6,280,128]{2,1,0:T(8,128)(2,1)}, f32[8,128]{1,0:T(8,128)}, bf16[6,4,4,4,280,128]{5,4,3,2,1,0:T(8,128)(2,1)}) custom-call(bf16[2,896,2048]{2,1,0:T(8,128)(2,1)} %get-tuple-element.31.refs_0_, bf16[4,2048,2560]{2,1,0:T(8,128)(2,1)} %get-tuple-element.32.refs_1_, bf16[2,2560,2048]{2,1,0:T(8,128)(2,1)} %get-tuple-element.33.refs_2_, ...), custom_call_target="tpu_custom_call" | custom-call | tf_op jit(solution)/shard_map/gradients/pallas_call | solution.py:619
  299.2 6.1 %adam.1 = (bf16[6,280,128]{2,1,0:T(8,128)(2,1)S(1)}, f32[14,2,2560]{2,1,0:T(2,128)}, f32[14,2,2560]{2,1,0:T(2,128)}, f32[2,40,896]{2,1,0:T(8,128)}, f32[14,2,256...) custom-call(bf16[6,280,128]{2,1,0:T(8,128)(2,1)} %get-tuple-element.35.g, ...), custom_call_target="tpu_custom_call" | custom-call | tf_op jit(solution)/shard_map/adam/pallas_call | solution.py:214
  305.4 95.1 %gather.1 = (bf16[4,4,4,280,128]{4,3,2,1,0:T(8,128)(2,1)S(1)}, bf16[4,4,4,280,128]{4,3,2,1,0:T(8,128)(2,1)S(1)}, bf16[4,4,4,280,128]{4,3,2,1,0:T(8,128)(2,1)S(1)...) custom-call(bf16[6,280,128]{2,1,0:T(8,128)(2,1)S(1)} %get-tuple-elem, ...), custom_call_target="tpu_custom_call" | custom-call | tf_op jit(solution)/shard_map/gather/pallas_call | solution.py:152
  400.4 12.7 %natural.1 = (bf16[2,896,2560]{2,1,0:T(8,128)(2,1)}, bf16[2,896,2560]{2,1,0:T(8,128)(2,1)}, bf16[2,2560,896]{2,1,0:T(8,128)(2,1)}) custom-call(bf16[64,280,128]{2,1,0:T(8,128)(2,1)S(1)} %bitcast.16, bf16[64,280,128]{2,1,0:T(8,128)(2,1)S(1)} %bitcast.17, bf16[64,280,128]{2,1,0:T(8,128)(2,1)S(1)} %bitcast.18, bf16[64,280,128]{2,1,0:T(8,128)(2,1)S(1)} %bitcast.19, ...), custom_call_target="tpu_custom_call" | custom-call | tf_op jit(solution)/shard_map/natural/pallas_call | solution.py:246

commit v6 on v5

--- a/solution.py
+++ b/solution.py
@@ -230,14 +230,14 @@
 
 def natural_kernel(*refs):
     gathered, outs, wide = refs[:MATRICES], refs[MATRICES:-AXES], refs[-AXES:]
-    first = pl.program_id(0) * SIDE
+    first = pl.program_id(0) * SUBLANES
     for t in range(AXES):
         for l in range(LAYERS):
-            for z in range(SIDE):
-                block = gathered[LAYERS * t + l][first + z].astype(F32)
-                rows = outs[t].shape[1] // SIDE
-                for row, n, column, at in tiles_of(t, rows, outs[t].shape[2]):
-                    wide[t][pl.ds(z * rows + row, n), pl.ds(column, LANES)] = block[at : at + n]
+            rows, columns = outs[t].shape[1:]
+            for k in range(SUBLANES):
+                block = gathered[LAYERS * t + l][first + k].astype(F32)
+                for row, n, column, at in tiles_of(t, rows // SUBLANES, columns):
+                    wide[t][pl.ds(k * rows // SUBLANES + row, n), pl.ds(column, LANES)] = block[at : at + n]
             outs[t][l] = wide[t][...].astype(BF16)
 
 
@@ -245,11 +245,11 @@
     shapes = (GATE, GATE, DOWN)
     return pl.pallas_call(
         natural_kernel,
-        grid=(PLANE,),
+        grid=(SUBLANES,),
         out_shape=tuple(jax.ShapeDtypeStruct((LAYERS, *s), BF16) for s in shapes),
         in_specs=[VMEM] * MATRICES,
-        out_specs=tuple(pl.BlockSpec((LAYERS, s[0] // PLANE, s[1]), lambda i: (0, i, 0)) for s in shapes),
-        scratch_shapes=[pltpu.VMEM((s[0] // PLANE, s[1]), F32) for s in shapes],
+        out_specs=tuple(pl.BlockSpec((LAYERS, s[0] // SUBLANES, s[1]), lambda i: (0, i, 0)) for s in shapes),
+        scratch_shapes=[pltpu.VMEM((s[0] // SUBLANES, s[1]), F32) for s in shapes],
         compiler_params=pltpu.CompilerParams(vmem_limit_bytes=MOST_VMEM // SIDE),
         name="natural",
     )(*[g.reshape(DEVICES, BLOCK, LANES) for g in gathered])
@@ -257,7 +257,7 @@
 
 D, FF, TOKENS = 896, 2560, 2048
 GATE, DOWN = (D, FF), (FF, D)
-ROWS, CHUNK, TILE = 256, 512, 512
+ROWS, CHUNK, TILE = 256, 256, 512
 TILES, PIECE, PLANE_ROWS = FF // TILE, BLOCK * TILE // FF, FF // SIDE
 NT = (((1,), (1,)), ((), ()))
 
@@ -275,7 +275,7 @@
 
 
 def rows_kernel(x, dy, *refs):
-    hbm, (tall, wide, turned, deep), weights, (g0, u0, z0, sems) = refs[:3], refs[3:7], refs[7:13], refs[13:]
+    hbm, (tall, wide, turned, deep), weights, (g0, u0, z0, dz1, sems) = refs[:3], refs[3:7], refs[7:13], refs[13:]
     wg0, wu0, wd0, wg1, wu1, wd1 = weights
     first = pl.program_id(0) == 0
 
@@ -299,36 +299,39 @@
     a = (x[...].astype(F32) * scale_of(x[...].astype(F32))).astype(BF16)
     tall[1] = a.T
     deep[0] = dy[...]
+    chunks = [pl.ds(j * CHUNK, CHUNK) for j in range(FF // CHUNK)]
     ready(0, 1)
-    for j in range(FF // CHUNK):
-        ch = pl.ds(j * CHUNK, CHUNK)
+    for ch in chunks:
         gate, up = dot(a, wg0[:, ch]), dot(a, wu0[:, ch])
         g0[:, ch], u0[:, ch] = gate, up
         z0[:, ch] = (gate * jax.nn.sigmoid(gate) * up).astype(BF16)
         turned[1, ch, :] = z0[:, ch].T
-    ready(2)
+    ready(2, 3, 4, 5)
+    for ch in chunks[:SIDE]:
+        dz1[:, ch] = dot_t(dy[...], wd1[ch, :]).astype(BF16)
     h = x[...] + dot(z0[...], wd0[...]).astype(BF16)
+    for ch in chunks[SIDE:]:
+        dz1[:, ch] = dot_t(dy[...], wd1[ch, :]).astype(BF16)
     h = h.astype(F32)
     scale = scale_of(h)
     a = (h * scale).astype(BF16)
     tall[0] = a.T
-    ready(3, 4, 5)
-    for j in range(FF // CHUNK):
-        ch = pl.ds(j * CHUNK, CHUNK)
+    for ch in chunks:
         gate, up = dot(a, wg1[:, ch]), dot(a, wu1[:, ch])
-        dz = dot_t(dy[...], wd1[ch, :]).astype(BF16).astype(F32)
+        dz = dz1[:, ch].astype(F32)
         s = jax.nn.sigmoid(gate)
         silu = gate * s
         turned[0, ch, :] = (silu * up).astype(BF16).T
         wide[1, :, ch] = (dz * silu).astype(BF16)
         wide[0, :, ch] = (dz * up * (s * (1 + gate * (1 - s)))).astype(BF16)
-    da = dot_t(wide[0], wg1[...]).astype(BF16) + dot_t(wide[1], wu1[...]).astype(BF16)
-    da = da.astype(F32)
+    most, rest = pl.ds(0, FF - CHUNK), chunks[-1]
+    da_gate, da_up = dot_t(wide[0, :, most], wg1[:, most]), dot_t(wide[1, :, most], wu1[:, most])
+    da_gate, da_up = da_gate + dot_t(wide[0, :, rest], wg1[:, rest]), da_up + dot_t(wide[1, :, rest], wu1[:, rest])
+    da = (da_gate.astype(BF16) + da_up.astype(BF16)).astype(F32)
     dwide = scale * (da - h * (scale * scale * jnp.mean(da * h, -1, keepdims=True)))
     dh = dy[...] + dwide.astype(BF16)
     deep[1] = dh
-    for j in range(FF // CHUNK):
-        ch = pl.ds(j * CHUNK, CHUNK)
+    for ch in chunks:
         dz = dot_t(dh, wd0[ch, :]).astype(BF16).astype(F32)
         gate, up = g0[:, ch], u0[:, ch]
         s = jax.nn.sigmoid(gate)
@@ -349,7 +352,7 @@
             pl.BlockSpec((2, FF, ROWS), lambda i: (0, 0, i)),
             pl.BlockSpec((2, ROWS, D), lambda i: (0, i, 0)),
         ),
-        scratch_shapes=[*[pltpu.VMEM(w.shape[1:], BF16) for w in weights * 2], pltpu.VMEM((ROWS, FF), F32), pltpu.VMEM((ROWS, FF), F32), pltpu.VMEM((ROWS, FF), BF16), DMA((MATRICES,))],
+        scratch_shapes=[*[pltpu.VMEM(w.shape[1:], BF16) for w in weights * 2], pltpu.VMEM((ROWS, FF), F32), pltpu.VMEM((ROWS, FF), F32), pltpu.VMEM((ROWS, FF), BF16), pltpu.VMEM((ROWS, FF), BF16), DMA((MATRICES,))],
         compiler_params=pltpu.CompilerParams(vmem_limit_bytes=MOST_VMEM),
         name="rows",
     )(x, dy, *weights)
@@ -581,19 +584,19 @@
             down_block(acc2, stage2)
             put2(m, h).start()
 
-        @pl.when((h == SIDE) & (m > 1))
-        def _():
-            on_third(m - 2)
-
-        @pl.when((h != 1) & (h != SIDE) & (m > 1) & (m < MATRICES + 2))
-        def _():
-            on_second(m - 2, (h + 1) // 2)
+        @pl.when((h == 0) & (m > 2))
+        def _():
+            on_third(m - 3)
+
+        @pl.when((h != 0) & (h != 3) & (m > 1) & (m < MATRICES + 2))
+        def _():
+            on_second(m - 2, h // 2)
 
         ring, turn = (i - 1) // TILES - 1, (i - 1) % TILES
 
         @pl.when((ring >= 0) & (ring < MATRICES))
         def _():
-            lax.fori_loop(TILES * turn // 2, TILES * (turn + 1) // 2, lambda e, _: (on_first(ring, e), 0)[1], 0)
+            lax.fori_loop(2 * turn + 1 - (SIDE - turn) // SIDE, 2 * turn + 3 + turn // SIDE, lambda e, _: (on_first(ring, e), 0)[1], 0)
 
         @pl.when((h == 0) & (m > 0) & (m < MATRICES + 1))
         def _():
@@ -601,7 +604,7 @@
 
         return 0
 
-    lax.fori_loop(0, (MATRICES + 2) * TILES, tile, 0)
+    lax.fori_loop(0, (MATRICES + 2) * TILES + 1, tile, 0)
 
     total = jnp.zeros((SUBLANES, LANES), F32)
     for m in range(MATRICES):

time: 413 us -> 404 us (0.978)
  Pallas kernels: 412 us -> 403 us
    pallas_call x1, Pallas kernels: 171 us -> 162 us  [gradients(): pl.pallas_call(gradients_kernel, out_shape=(jax.ShapeDtypeStruct((MATRICE...]
where the time goes in v6:
time: 404 us
  Pallas kernels  403 us (100%)
    pallas_call x1, Pallas kernels, gradients(): pl.pallas_call(gradients_kernel, out_shape=(jax.ShapeDtypeStruct((MATRICE...  162 us
    pallas_call x1, Pallas kernels, by_rows(): pl.pallas_call(rows_kernel, grid=(TOKENS // ROWS,), out_shape=tuple((jax....  126 us
    pallas_call x1, Pallas kernels, all_gather(): pl.pallas_call(ag_kernel, out_shape=(pltpu.VMEM((SIDE, SIDE, SIDE, *mine....  98.1 us
    pallas_call x1, Pallas kernels, natural(): pl.pallas_call(natural_kernel, grid=(SUBLANES,), out_shape=tuple((jax.Sha...  11 us

profile of v6, /device:TPU:0, one launch (start us, length us, event | category | flops | bytes accessed | tf_op | source)
XLA Modules:
  0.0 403.6 jit_solution(7511776001933468873)
XLA Ops:
  0.6 125.7 %rows.1 = (bf16[2,896,2048]{2,1,0:T(8,128)(2,1)}, bf16[4,2048,2560]{2,1,0:T(8,128)(2,1)}, bf16[2,2560,2048]{2,1,0:T(8,128)(2,1)}, bf16[2,2048,896]{2,1,0:T(8,128)(2,1)}) custom-call(bf16[2048,896]{1,0:T(8,128)(2,1)} %bitcast.22, bf16[2048,896]{1,0:T(8,128)(2,1)} %bitcast.23, bf16[2,896,2560]{2,1,0:T(8,128)(2,1)} %refs_0_.3, bf16[2,896,2560]{2,1,0:T(8,128)(2,1)} %refs_1_.3, ...), custom_call_target="tpu_custom_call" | custom-call | tf_op jit(solution)/shard_map/rows/pallas_call | solution.py:344
  126.3 162.1 %gradients.1 = (bf16[6,280,128]{2,1,0:T(8,128)(2,1)}, f32[8,128]{1,0:T(8,128)}, bf16[6,4,4,4,280,128]{5,4,3,2,1,0:T(8,128)(2,1)}) custom-call(bf16[2,896,2048]{2,1,0:T(8,128)(2,1)} %get-tuple-element.31.refs_0_, bf16[4,2048,2560]{2,1,0:T(8,128)(2,1)} %get-tuple-element.32.refs_1_, bf16[2,2560,2048]{2,1,0:T(8,128)(2,1)} %get-tuple-element.33.refs_2_, ...), custom_call_target="tpu_custom_call" | custom-call | tf_op jit(solution)/shard_map/gradients/pallas_call | solution.py:622
  288.4 6.1 %adam.1 = (bf16[6,280,128]{2,1,0:T(8,128)(2,1)S(1)}, f32[14,2,2560]{2,1,0:T(2,128)}, f32[14,2,2560]{2,1,0:T(2,128)}, f32[2,40,896]{2,1,0:T(8,128)}, f32[14,2,256...) custom-call(bf16[6,280,128]{2,1,0:T(8,128)(2,1)} %get-tuple-element.35.g, ...), custom_call_target="tpu_custom_call" | custom-call | tf_op jit(solution)/shard_map/adam/pallas_call | solution.py:214
  294.6 98.1 %gather.1 = (bf16[4,4,4,280,128]{4,3,2,1,0:T(8,128)(2,1)S(1)}, bf16[4,4,4,280,128]{4,3,2,1,0:T(8,128)(2,1)S(1)}, bf16[4,4,4,280,128]{4,3,2,1,0:T(8,128)(2,1)S(1)...) custom-call(bf16[6,280,128]{2,1,0:T(8,128)(2,1)S(1)} %get-tuple-elem, ...), custom_call_target="tpu_custom_call" | custom-call | tf_op jit(solution)/shard_map/gather/pallas_call | solution.py:152
  392.6 11.0 %natural.1 = (bf16[2,896,2560]{2,1,0:T(8,128)(2,1)}, bf16[2,896,2560]{2,1,0:T(8,128)(2,1)}, bf16[2,2560,896]{2,1,0:T(8,128)(2,1)}) custom-call(bf16[64,280,128]{2,1,0:T(8,128)(2,1)S(1)} %bitcast.16, bf16[64,280,128]{2,1,0:T(8,128)(2,1)S(1)} %bitcast.17, bf16[64,280,128]{2,1,0:T(8,128)(2,1)S(1)} %bitcast.18, bf16[64,280,128]{2,1,0:T(8,128)(2,1)S(1)} %bitcast.19, ...), custom_call_target="tpu_custom_call" | custom-call | tf_op jit(solution)/shard_map/natural/pallas_call | solution.py:246

commit v7 on v6

--- a/solution.py
+++ b/solution.py
@@ -108,28 +108,29 @@
             index[axis] = slice(None) if d is None else wrap(at[axis] - SIGNS[c] * d)
         return outs[c].at[tuple(index)]
 
-    def copy(c, phase, key, of_receiver):
+    def arrived(c, phase, key):
+        d1, d2, d3 = key
+        if phase == 0:
+            return recv1.at[c // 2, d3 - 1]
+        if phase == 1:
+            return recv2.at[c // 2, d2 - 1, d3]
+        if d3 is not None:
+            return recv3.at[c // 2, d1 - 1, d3]
+        return recv4.at[c // 2, d1 - 1, d2 - 1]
+
+    def send_on(c, phase, key):
         d1, d2, d3 = key
         back = list(key)
-        if not of_receiver:
-            back[2 - phase] -= 1
+        back[2 - phase] -= 1
         there = where(c, back)
-        src = mine.at[c] if not of_receiver and not any(back) and d3 is not None else there
-        if phase == 0:
-            recv = recv1.at[c, d3]
-        elif phase == 1:
-            recv = recv2.at[c, d2, d3]
-        elif d3 is not None:
-            recv = recv3.at[c, d1, d3]
-        else:
-            recv = recv4.at[c, d1, d2]
-        return remote(src, there, sends.at[c, phase], recv, neighbour(at, ORDERS[c][2 - phase], SIGNS[c]))
+        src = there if any(d != 0 for d in back) else mine.at[c]
+        remote(src, there, sends.at[c, phase], arrived(c, phase, key), neighbour(at, ORDERS[c][2 - phase], SIGNS[c])).start()
 
     seen = []
 
     def hold(*held):
         for phase, key in passed_on(seen, *held):
-            copy(held[0], phase, key, False).start()
+            send_on(held[0], phase, key)
 
     own = [pltpu.make_async_copy(mine.at[c], where(c, (0, 0, 0)), local.at[c]) for c in range(WAYS)]
     for c in range(WAYS):
@@ -137,8 +138,9 @@
     for copied in own:
         copied.start()
     for even, phase, key in ag_order():
+        two = outs[even].at[0, pl.ds(0, 2)] if key[2] is None else outs[even].at[0, 0, pl.ds(0, 2)]
+        pltpu.make_async_copy(two, two, arrived(even, phase, key)).wait()
         for c in (even, even + 1):
-            copy(c, phase, key, True).wait_recv()
             hold(c, phase, key)
     for c in range(WAYS):
         own[c].wait()
@@ -154,7 +156,7 @@
         out_shape=(pltpu.VMEM((SIDE, SIDE, SIDE, *mine.shape[1:]), BF16),) * WAYS,
         in_specs=[VMEM],
         out_specs=(VMEM,) * WAYS,
-        scratch_shapes=[DMA((WAYS, AXES)), DMA((WAYS, SIDE)), *[DMA((WAYS, SIDE, SIDE))] * 3, DMA((WAYS,))],
+        scratch_shapes=[DMA((WAYS, AXES)), DMA((AXES, STEPS)), *[DMA((AXES, STEPS, SIDE))] * 2, DMA((AXES, STEPS, STEPS)), DMA((WAYS,))],
         compiler_params=pltpu.CompilerParams(collective_id=1, has_side_effects=True, vmem_limit_bytes=MOST_VMEM // SUBLANES),
         name="gather",
     )(mine)
@@ -274,39 +276,84 @@
     return lax.rsqrt(jnp.mean(wide * wide, -1, keepdims=True) + 1e-6)
 
 
-def rows_kernel(x, dy, *refs):
-    hbm, (tall, wide, turned, deep), weights, (g0, u0, z0, dz1, sems) = refs[:3], refs[3:7], refs[7:13], refs[13:]
+def rows_kernel(x_hbm, dy_hbm, *refs):
+    hbm, results, weights, rest = refs[:3], refs[3:7], refs[7:13], refs[13:]
+    buffers, (xs, dys, g0, u0, z0, dz1, sems, part_sems, in_sems, out_sems) = rest[:4], rest[4:]
     wg0, wu0, wd0, wg1, wu1, wd1 = weights
-    first = pl.program_id(0) == 0
+    i, slot = pl.program_id(0), pl.program_id(0) % 2
+    first = i == 0
+    chunks = [pl.ds(j * CHUNK, CHUNK) for j in range(FF // CHUNK)]
 
     def fetch(k):
         return pltpu.make_async_copy(hbm[k % 3].at[k // 3], weights[k], sems.at[k])
 
+    def fetch_part(k, j):
+        return pltpu.make_async_copy(hbm[k].at[0, :, chunks[j]], weights[k].at[:, chunks[j]], part_sems.at[k, j])
+
+    def take(i):
+        rows = pl.ds(pl.multiple_of(i * ROWS, ROWS), ROWS)
+        for k, (source, there) in enumerate(((x_hbm, xs), (dy_hbm, dys))):
+            yield pltpu.make_async_copy(source.at[rows], there.at[i % 2], in_sems.at[i % 2, k])
+
+    def put(k, part):
+        rows = pl.ds(pl.multiple_of(i * ROWS, ROWS), ROWS)
+        there = results[k].at[part, rows] if k % 2 else results[k].at[part, :, rows]
+        return pltpu.make_async_copy(buffers[k].at[slot, part], there, out_sems.at[slot, k, part])
+
+    def outs():
+        return [put(k, part) for k in range(4) for part in range(results[k].shape[0])]
+
     @pl.when(first)
     def _():
-        for k in range(2):
-            fetch(k).start()
-
-    def ready(*ks):
-        @pl.when(first)
-        def _():
-            for k in ks:
-                fetch(k).wait()
-            if 0 in ks:
-                for k in range(2, MATRICES):
-                    fetch(k).start()
-
-    a = (x[...].astype(F32) * scale_of(x[...].astype(F32))).astype(BF16)
-    tall[1] = a.T
-    deep[0] = dy[...]
-    chunks = [pl.ds(j * CHUNK, CHUNK) for j in range(FF // CHUNK)]
-    ready(0, 1)
-    for ch in chunks:
-        gate, up = dot(a, wg0[:, ch]), dot(a, wu0[:, ch])
-        g0[:, ch], u0[:, ch] = gate, up
-        z0[:, ch] = (gate * jax.nn.sigmoid(gate) * up).astype(BF16)
-        turned[1, ch, :] = z0[:, ch].T
-    ready(2, 3, 4, 5)
+        for copy in take(0):
+            copy.start()
+        for j in range(len(chunks)):
+            for k in range(2):
+                fetch_part(k, j).start()
+
+    for copy in take(i):
+        copy.wait()
+
+    @pl.when(i + 1 < pl.num_programs(0))
+    def _():
+        for copy in take(i + 1):
+            copy.start()
+
+    @pl.when(i > 1)
+    def _():
+        for copy in outs():
+            copy.wait()
+
+    tall, wide, turned, deep = (b.at[slot] for b in buffers)
+    x, dy = xs.at[slot], dys.at[slot]
+
+    def forward(coming):
+        a = (x[...].astype(F32) * scale_of(x[...].astype(F32))).astype(BF16)
+        tall[1] = a.T
+        deep[0] = dy[...]
+        for j, ch in enumerate(chunks):
+            if coming:
+                for k in range(2):
+                    fetch_part(k, j).wait()
+                if 0 < j < 5:
+                    fetch(j + 1).start()
+            gate, up = dot(a, wg0[:, ch]), dot(a, wu0[:, ch])
+            g0[:, ch], u0[:, ch] = gate, up
+            z0[:, ch] = (gate * jax.nn.sigmoid(gate) * up).astype(BF16)
+            turned[1, ch, :] = z0[:, ch].T
+
+    @pl.when(first)
+    def _():
+        forward(True)
+        for k in range(2, MATRICES):
+            fetch(k).wait()
+
+    @pl.when(i > 0)
+    def _():
+        forward(False)
+
+    for k, part in ((0, 1), (3, 0), (2, 1)):
+        put(k, part).start()
     for ch in chunks[:SIDE]:
         dz1[:, ch] = dot_t(dy[...], wd1[ch, :]).astype(BF16)
     h = x[...] + dot(z0[...], wd0[...]).astype(BF16)
@@ -316,6 +363,7 @@
     scale = scale_of(h)
     a = (h * scale).astype(BF16)
     tall[0] = a.T
+    put(0, 0).start()
     for ch in chunks:
         gate, up = dot(a, wg1[:, ch]), dot(a, wu1[:, ch])
         dz = dz1[:, ch].astype(F32)
@@ -324,6 +372,8 @@
         turned[0, ch, :] = (silu * up).astype(BF16).T
         wide[1, :, ch] = (dz * silu).astype(BF16)
         wide[0, :, ch] = (dz * up * (s * (1 + gate * (1 - s)))).astype(BF16)
+    for k, part in ((2, 0), (1, 0), (1, 1)):
+        put(k, part).start()
     most, rest = pl.ds(0, FF - CHUNK), chunks[-1]
     da_gate, da_up = dot_t(wide[0, :, most], wg1[:, most]), dot_t(wide[1, :, most], wu1[:, most])
     da_gate, da_up = da_gate + dot_t(wide[0, :, rest], wg1[:, rest]), da_up + dot_t(wide[1, :, rest], wu1[:, rest])
@@ -331,28 +381,45 @@
     dwide = scale * (da - h * (scale * scale * jnp.mean(da * h, -1, keepdims=True)))
     dh = dy[...] + dwide.astype(BF16)
     deep[1] = dh
+    put(3, 1).start()
     for ch in chunks:
         dz = dot_t(dh, wd0[ch, :]).astype(BF16).astype(F32)
         gate, up = g0[:, ch], u0[:, ch]
         s = jax.nn.sigmoid(gate)
         wide[3, :, ch] = (dz * (gate * s)).astype(BF16)
         wide[2, :, ch] = (dz * up * (s * (1 + gate * (1 - s)))).astype(BF16)
+    put(1, 2).start()
+    put(1, 3).start()
+
+    @pl.when(i + 1 == pl.num_programs(0))
+    def _():
+        for copy in outs():
+            copy.wait()
+
+    @pl.when(i + 1 == pl.num_programs(0))
+    def _():
+        for k in range(4):
+            for part in range(results[k].shape[0]):
+                pltpu.make_async_copy(buffers[k].at[1 - slot, part], buffers[k].at[1 - slot, part], out_sems.at[1 - slot, k, part]).wait()
 
 
 def by_rows(x, dy, weights):
-    state = pl.BlockSpec((ROWS, D), lambda i: (i, 0))
+    shapes = ((2, D, TOKENS), (4, TOKENS, FF), (2, FF, TOKENS), (2, TOKENS, D))
+    buffers = ((2, D, ROWS), (4, ROWS, FF), (2, FF, ROWS), (2, ROWS, D))
     return pl.pallas_call(
         rows_kernel,
         grid=(TOKENS // ROWS,),
-        out_shape=tuple(jax.ShapeDtypeStruct(s, BF16) for s in ((2, D, TOKENS), (4, TOKENS, FF), (2, FF, TOKENS), (2, TOKENS, D))),
-        in_specs=[state, state] + [HBM] * 3,
-        out_specs=(
-            pl.BlockSpec((2, D, ROWS), lambda i: (0, 0, i)),
-            pl.BlockSpec((4, ROWS, FF), lambda i: (0, i, 0)),
-            pl.BlockSpec((2, FF, ROWS), lambda i: (0, 0, i)),
-            pl.BlockSpec((2, ROWS, D), lambda i: (0, i, 0)),
-        ),
-        scratch_shapes=[*[pltpu.VMEM(w.shape[1:], BF16) for w in weights * 2], pltpu.VMEM((ROWS, FF), F32), pltpu.VMEM((ROWS, FF), F32), pltpu.VMEM((ROWS, FF), BF16), pltpu.VMEM((ROWS, FF), BF16), DMA((MATRICES,))],
+        out_shape=tuple(jax.ShapeDtypeStruct(s, BF16) for s in shapes),
+        in_specs=[HBM] * 5,
+        out_specs=(HBM,) * 4,
+        scratch_shapes=[
+            *[pltpu.VMEM(w.shape[1:], BF16) for w in weights * 2],
+            *[pltpu.VMEM((2, *b), BF16) for b in buffers],
+            *[pltpu.VMEM((2, ROWS, D), BF16)] * 2,
+            *[pltpu.VMEM((ROWS, FF), F32)] * 2,
+            *[pltpu.VMEM((ROWS, FF), BF16)] * 2,
+            DMA((MATRICES,)), DMA((2, FF // CHUNK)), DMA((2, 2)), DMA((2, 4, 4)),
+        ],
         compiler_params=pltpu.CompilerParams(vmem_limit_bytes=MOST_VMEM),
         name="rows",
     )(x, dy, *weights)
@@ -437,20 +504,23 @@
             src = block(m, c, wrap(p1 - s), wrap(p2 - s * (1 + j)))
         else:
             src = r1.at[c, m, (step + 2) % STEPS, j]
-        return remote(src, r1.at[c, m, step, j], send1.at[c], recv1.at[c, m, step, j], neighbour(at, o[0], s))
+        return remote(src, r1.at[c, m, step, j], send1, recv1.at[m, step, j], neighbour(at, o[0], s))
 
     def loading(m, c, step):
         o, s, p1, p2, p3 = split(c)
-        return pltpu.make_async_copy(block(m, c, wrap(p1 - s * (2 + step)), None), own.at[c, step], load.at[c, step])
+        return pltpu.make_async_copy(block(m, c, wrap(p1 - s * (2 + step)), None), own.at[c, step], load.at[step])
 
     def second(m, c, step, start=False):
         o, s, p1, p2, p3 = split(c)
         src = r1.at[c, m, 2, 0] if start else r2.at[c, m, (step + 2) % STEPS]
-        return remote(src, r2.at[c, m, step], send2.at[c], recv2.at[c, m, step], neighbour(at, o[1], s))
+        return remote(src, r2.at[c, m, step], send2, recv2.at[m, step], neighbour(at, o[1], s))
 
     def third(m, c, k):
         o, s, p1, p2, p3 = split(c)
-        return remote(r2.at[c, m, 2, wrap(p3 + k + 1)], r3.at[c, m, k], send3.at[c], recv3.at[c, m, k], neighbour(at, o[2], k + 1))
+        return remote(r2.at[c, m, 2, wrap(p3 + k + 1)], r3.at[c, m, k], send3, recv3.at[m], neighbour(at, o[2], k + 1))
+
+    def whole(ref, sem):
+        pltpu.make_async_copy(ref, ref, sem).wait()
 
     def launch(m):
         for c in range(WAYS):
@@ -466,51 +536,60 @@
 
         @pl.when(j == 0)
         def _():
-            for c in range(WAYS):
-                loading(m, c, step).wait()
-
-        for c in range(WAYS):
+            whole(own.at[:, step], load.at[step])
+
+        whole(r1.at[:, m, step, j], recv1.at[m, step, j])
+
+        def both(c):
             o, s, p1, p2, p3 = split(c)
-            first(m, c, step, j).wait_recv()
             i = wrap(p2 - s * (1 + j))
             mine = own[c, step, i] if o[1] < o[2] else own[c, step, :, i]
-            both = r1[c, m, step, j].astype(F32) + mine.astype(F32)
-            r1[c, m, step, j] = both.astype(BF16)
-
-            @pl.when(step == 2)
-            def _():
-                f1[c, j] = both
-
-            @pl.when(step < 2)
-            def _():
+            return r1[c, m, step, j].astype(F32) + mine.astype(F32)
+
+        @pl.when(step < 2)
+        def _():
+            for c in range(WAYS):
+                r1[c, m, step, j] = both(c).astype(BF16)
                 first(m, c, step + 1, j).start()
 
-            @pl.when(e == 8)
-            def _():
-                second(m, c, 0, True).start()
+        @pl.when(step == 2)
+        def _():
+            for c in range(WAYS):
+                total = both(c)
+                f1[c, j] = total
+
+                @pl.when(j == 0)
+                def _():
+                    r1[c, m, 2, 0] = total.astype(BF16)
+                    second(m, c, 0, True).start()
 
     def on_second(m, step):
-        for c in range(WAYS):
-            second(m, c, step).wait_recv()
-            both = r2[c, m, step].astype(F32) + f1[c, step + 1]
-            r2[c, m, step] = both.astype(BF16)
-
-            @pl.when(step == 2)
-            def _():
-                f2[c] = both
+        whole(r2.at[:, m, step], recv2.at[m, step])
+
+        def both(c):
+            return r2[c, m, step].astype(F32) + f1[c, step + 1]
+
+        @pl.when(step < 2)
+        def _():
+            for c in range(WAYS):
+                r2[c, m, step] = both(c).astype(BF16)
+                second(m, c, step + 1).start()
+
+        @pl.when(step == 2)
+        def _():
+            for c in range(WAYS):
+                total = both(c)
+                f2[c] = total
+                r2[c, m, 2] = total.astype(BF16)
                 for k in range(STEPS):
                     third(m, c, k).start()
 
-            @pl.when(step < 2)
-            def _():
-                second(m, c, step + 1).start()
-
     def on_third(m):
+        whole(r3.at[:, m], recv3.at[m])
         for c in range(WAYS):
             o, s, p1, p2, p3 = split(c)
             total = f2[c, p3]
             for k in range(STEPS):
-                third(m, c, k).wait_recv()
                 total = total + r3[c, m, k].astype(F32)
             out[m, pl.ds(STARTS[c], PART)] = total.astype(BF16)
 
@@ -611,11 +690,10 @@
         g = out[m].astype(F32)
         total = total + jnp.sum((g * g).reshape(-1, SUBLANES, LANES), axis=0)
     squares[...] = norm_exchange(at, sums, send4, recv4, total)
-    for c in range(WAYS):
-        for r, sem in ((r1, send1), (r2, send2), (r3, send3)):
-            pltpu.make_async_copy(r.at[c], r.at[c], sem.at[c]).wait()
-    for axis in range(STEPS):
-        pltpu.make_async_copy(sums.at[axis, pl.ds(0, STEPS)], sums.at[axis, pl.ds(0, STEPS)], send4.at[axis]).wait()
+    for r, sem in ((r1, send1), (r2, send2), (r3, send3)):
+        whole(r, sem)
+    for axis in range(AXES):
+        whole(sums.at[axis, pl.ds(0, STEPS)], send4.at[axis])
 
 
 def gradients(tall, wide, turned, deep):
@@ -646,9 +724,9 @@
             pltpu.VMEM((WAYS, SIDE, PART, LANES), F32),
             pltpu.VMEM((AXES, SIDE, SUBLANES, LANES), F32),
             *[DMA((2,))] * 4,
-            *[DMA((WAYS,))] * AXES,
-            DMA((WAYS, MATRICES, STEPS, SIDE)), *[DMA((WAYS, MATRICES, STEPS))] * 2,
-            DMA((WAYS, STEPS)),
+            *[DMA] * AXES,
+            DMA((MATRICES, STEPS, SIDE)), DMA((MATRICES, STEPS)), DMA((MATRICES,)),
+            DMA((STEPS,)),
             DMA((AXES,)), DMA((AXES, STEPS)),
         ],
         compiler_params=pltpu.CompilerParams(collective_id=0, has_side_effects=True, vmem_limit_bytes=MOST_VMEM),

time: 404 us -> 392 us (0.970)
  Pallas kernels: 403 us -> 391 us
    pallas_call x1, Pallas kernels: 162 us -> 152 us  [gradients(): pl.pallas_call(gradients_kernel, out_shape=(jax.ShapeDtypeStruct((MATRICE...]
where the time goes in v7:
time: 392 us
  Pallas kernels  391 us (100%)
    pallas_call x1, Pallas kernels, gradients(): pl.pallas_call(gradients_kernel, out_shape=(jax.ShapeDtypeStruct((MATRICE...  152 us
    pallas_call x1, Pallas kernels, by_rows(): pl.pallas_call(rows_kernel, grid=(TOKENS // ROWS,), out_shape=tuple((jax....  124 us
    pallas_call x1, Pallas kernels, all_gather(): pl.pallas_call(ag_kernel, out_shape=(pltpu.VMEM((SIDE, SIDE, SIDE, *mine....  97.4 us
    pallas_call x1, Pallas kernels, natural(): pl.pallas_call(natural_kernel, grid=(SUBLANES,), out_shape=tuple((jax.Sha...  11 us

profile of v7, /device:TPU:0, one launch (start us, length us, event | category | flops | bytes accessed | tf_op | source)
XLA Modules:
  0.0 391.6 jit_solution(13485355747865125025)
XLA Ops:
  0.6 124.3 %rows.1 = (bf16[2,896,2048]{2,1,0:T(8,128)(2,1)}, bf16[4,2048,2560]{2,1,0:T(8,128)(2,1)}, bf16[2,2560,2048]{2,1,0:T(8,128)(2,1)}, bf16[2,2048,896]{2,1,0:T(8,128)(2,1)}) custom-call(bf16[2048,896]{1,0:T(8,128)(2,1)} %bitcast.22, bf16[2048,896]{1,0:T(8,128)(2,1)} %bitcast.23, bf16[2,896,2560]{2,1,0:T(8,128)(2,1)} %refs_0_.3, bf16[2,896,2560]{2,1,0:T(8,128)(2,1)} %refs_1_.3, ...), custom_call_target="tpu_custom_call" | custom-call | tf_op jit(solution)/shard_map/rows/pallas_call | solution.py:409
  125.0 152.1 %gradients.1 = (bf16[6,280,128]{2,1,0:T(8,128)(2,1)}, f32[8,128]{1,0:T(8,128)}, bf16[6,4,4,4,280,128]{5,4,3,2,1,0:T(8,128)(2,1)}) custom-call(bf16[2,896,2048]{2,1,0:T(8,128)(2,1)} %get-tuple-element.31.refs_0_, bf16[4,2048,2560]{2,1,0:T(8,128)(2,1)} %get-tuple-element.32.refs_1_, bf16[2,2560,2048]{2,1,0:T(8,128)(2,1)} %get-tuple-element.33.refs_2_, ...), custom_call_target="tpu_custom_call" | custom-call | tf_op jit(solution)/shard_map/gradients/pallas_call | solution.py:700
  277.0 6.1 %adam.1 = (bf16[6,280,128]{2,1,0:T(8,128)(2,1)S(1)}, f32[14,2,2560]{2,1,0:T(2,128)}, f32[14,2,2560]{2,1,0:T(2,128)}, f32[2,40,896]{2,1,0:T(8,128)}, f32[14,2,256...) custom-call(bf16[6,280,128]{2,1,0:T(8,128)(2,1)} %get-tuple-element.35.g, ...), custom_call_target="tpu_custom_call" | custom-call | tf_op jit(solution)/shard_map/adam/pallas_call | solution.py:216
  283.2 97.4 %gather.1 = (bf16[4,4,4,280,128]{4,3,2,1,0:T(8,128)(2,1)S(1)}, bf16[4,4,4,280,128]{4,3,2,1,0:T(8,128)(2,1)S(1)}, bf16[4,4,4,280,128]{4,3,2,1,0:T(8,128)(2,1)S(1)...) custom-call(bf16[6,280,128]{2,1,0:T(8,128)(2,1)S(1)} %get-tuple-elem, ...), custom_call_target="tpu_custom_call" | custom-call | tf_op jit(solution)/shard_map/gather/pallas_call | solution.py:154
  380.6 11.0 %natural.1 = (bf16[2,896,2560]{2,1,0:T(8,128)(2,1)}, bf16[2,896,2560]{2,1,0:T(8,128)(2,1)}, bf16[2,2560,896]{2,1,0:T(8,128)(2,1)}) custom-call(bf16[64,280,128]{2,1,0:T(8,128)(2,1)S(1)} %bitcast.16, bf16[64,280,128]{2,1,0:T(8,128)(2,1)S(1)} %bitcast.17, bf16[64,280,128]{2,1,0:T(8,128)(2,1)S(1)} %bitcast.18, bf16[64,280,128]{2,1,0:T(8,128)(2,1)S(1)} %bitcast.19, ...), custom_call_target="tpu_custom_call" | custom-call | tf_op jit(solution)/shard_map/natural/pallas_call | solution.py:248

commit v8 on v7

--- a/solution.py
+++ b/solution.py
@@ -14,7 +14,8 @@
 BF16, F32 = jnp.bfloat16, jnp.float32
 HBM, VMEM = pl.BlockSpec(memory_space=pl.ANY), pl.BlockSpec(memory_space=pltpu.VMEM)
 DMA = pltpu.SemaphoreType.DMA
-MOST_VMEM = 62 * 1024 * 1024
+MIB = 1 << 20
+MOST_VMEM, SPARE_VMEM = 62 * MIB, 2 * MIB
 ORDERS = tuple(tuple((way // 2 + i) % AXES for i in range(AXES)) for way in range(WAYS))
 SIGNS = (1, -1) * AXES
 TAKEN = (3, 0, 4, 1, 5, 2)
@@ -39,25 +40,34 @@
     return pltpu.make_async_remote_copy(src_ref=src, dst_ref=dst, send_sem=send, recv_sem=recv, device_id=to, device_id_type=MESH)
 
 
-def enter(at):
+def moved(at, steps):
+    x, y, z = (wrap(a + step) for a, step in zip(at, steps, strict=True))
+    return {"dp": (x * SIDE + y) * SIDE + z}
+
+
+LINES = tuple(tuple(k * (axis == line) for axis in range(AXES)) for line in range(AXES) for k in range(1, SIDE))
+PLANE_PEERS = tuple((0, k // SIDE, k % SIDE) for k in range(1, PLANE))
+LINE_PEERS = LINES[:STEPS]
+
+
+def enter(at, peers):
     barrier = pltpu.get_barrier_semaphore()
-    for axis in range(AXES):
-        for step in range(STEPS):
-            pl.semaphore_signal(barrier, inc=1, device_id=neighbour(at, axis, step + 1), device_id_type=MESH)
-    pl.semaphore_wait(barrier, AXES * STEPS)
+    for steps in peers:
+        pl.semaphore_signal(barrier, inc=1, device_id=moved(at, steps), device_id_type=MESH)
+    pl.semaphore_wait(barrier, len(peers))
 
 
 def norm_exchange(at, buf, send, recv, total):
-    for axis in range(AXES):
-        buf[axis, STEPS] = total
-        copies = [
-            remote(buf.at[axis, STEPS], buf.at[axis, k], send.at[axis], recv.at[axis, k], neighbour(at, axis, k + 1)) for k in range(STEPS)
-        ]
-        for copy in copies:
-            copy.start()
-        for k, copy in enumerate(copies):
-            copy.wait_recv()
-            total = total + buf[axis, k]
+    first = 0
+    for stage, peers in enumerate((PLANE_PEERS, LINE_PEERS)):
+        own, others = buf.at[first], buf.at[pl.ds(first + 1, len(peers))]
+        own[...] = total
+        for k, steps in enumerate(peers):
+            remote(own, others.at[k], send.at[stage], recv.at[stage], moved(at, steps)).start()
+        pltpu.make_async_copy(others, others, recv.at[stage]).wait()
+        total = total + jnp.sum(others[...], axis=0)
+        pltpu.make_async_copy(others, others, send.at[stage]).wait()
+        first += 1 + len(peers)
     return total
 
 
@@ -76,7 +86,7 @@
         yield 2, (d1 + 1, d2, d3)
 
 
-def ag_order(latency=1.8):
+def ag_order(latency=2):
     import heapq
 
     free, out, seen, heap = {}, [], [], []
@@ -100,7 +110,7 @@
 def ag_kernel(*refs):
     mine, outs, (sends, recv1, recv2, recv3, recv4, local) = refs[0], refs[1 : 1 + WAYS], refs[1 + WAYS :]
     at = place()
-    enter(at)
+    enter(at, LINES)
 
     def where(c, key):
         index = [None] * AXES
@@ -170,31 +180,13 @@
 
 
 def adam_kernel(count, g, total, *refs):
-    refs = list(refs)
     ws, ms, vs = (refs[AXES * k : AXES * (k + 1)] for k in range(3))
     new, *refs = refs[3 * AXES :]
-    new_m, new_v, windows, owns = (refs[AXES * k : AXES * (k + 1)] for k in range(4))
-    wide_g, wide_w, sems = refs[4 * AXES :]
-    me = lax.axis_index("dp")
-    taken = []
-    for t in range(AXES):
-        rows = windows[t].shape[1]
-        first = pl.multiple_of((me // SIDE if t < 2 else me) * rows, SUBLANES)
-        taken.append(pltpu.make_async_copy(ws[t].at[:, pl.ds(first, rows)], windows[t], sems.at[t]))
-    for copy in taken:
-        copy.start()
+    *moments, wide_g, wide_w = refs
+    new_m, new_v = moments[:AXES], moments[AXES:]
     factor = jnp.minimum(1.0, 0.5 * lax.rsqrt(jnp.full((1, 1), jnp.sum(total[...])) / count + 1e-30))
     for t in range(AXES):
-        taken[t].wait()
-        rows, columns = owns[t].shape[1:]
-        if t < 2:
-            for z in range(SIDE):
-
-                @pl.when(me % SIDE == z)
-                def _():
-                    for l in range(LAYERS):
-                        owns[t][l] = windows[t][l].astype(F32)[z * rows : (z + 1) * rows]
-
+        rows, columns = ws[t].shape[1:]
         for l in range(LAYERS):
             wide_g[...] = g[TAKEN[LAYERS * t + l]].astype(F32) * factor
             for row, n, column, at in tiles_of(t, rows, columns):
@@ -203,7 +195,7 @@
                 grad = wide_g[pl.ds(at, n), :]
                 m = 0.9 * ms[t][here] + 0.1 * grad
                 v = 0.95 * vs[t][here] + 0.05 * grad * grad
-                w = (owns if t < 2 else windows)[t][l, pl.ds(row, n), lanes].astype(F32)
+                w = ws[t][l, pl.ds(row, n), lanes]
                 new_m[t][here] = m
                 new_v[t][here] = v
                 wide_w[pl.ds(at, n), :] = w - 0.02 * (m * lax.rsqrt(v + 1e-8) + 0.1 * w)
@@ -216,15 +208,10 @@
     new, *moments = pl.pallas_call(
         functools.partial(adam_kernel, count),
         out_shape=(pltpu.VMEM(g.shape, BF16), *like, *like),
-        in_specs=[VMEM] * 2 + [HBM] * AXES + [VMEM] * AXES * 2,
+        in_specs=[VMEM] * (2 + AXES * 3),
         out_specs=(VMEM,) * (1 + AXES * 2),
-        scratch_shapes=[
-            *[pltpu.VMEM((LAYERS, w.shape[1] // n, w.shape[2]), BF16) for w, n in zip(ws, (PLANE, PLANE, DEVICES), strict=True)],
-            *[pltpu.VMEM((LAYERS, w.shape[1] // DEVICES, w.shape[2]), F32) for w in ws],
-            *[pltpu.VMEM(g.shape[1:], F32)] * 2,
-            DMA((AXES,)),
-        ],
-        compiler_params=pltpu.CompilerParams(vmem_limit_bytes=MOST_VMEM),
+        scratch_shapes=[pltpu.VMEM(g.shape[1:], F32)] * 2,
+        compiler_params=pltpu.CompilerParams(vmem_limit_bytes=MOST_VMEM // SIDE),
         name="adam",
     )(g, total, *ws, *ms, *vs)
     return new, *([*(jnp.swapaxes(a, 0, 1) for a in part[:2]), part[2]] for part in (moments[:AXES], moments[AXES:]))
@@ -454,10 +441,32 @@
     lax.fori_loop(0, 16, group, 0)
 
 
+def own_rows(ws, windows, owns, sems):
+    me = lax.axis_index("dp")
+    taken = []
+    for t in range(AXES):
+        rows = windows[t].shape[1]
+        first = pl.multiple_of((me // SIDE if t < 2 else me) * rows, SUBLANES)
+        taken.append(pltpu.make_async_copy(ws[t].at[:, pl.ds(first, rows)], windows[t], sems.at[t]))
+        taken[t].start()
+    for t in range(AXES):
+        taken[t].wait()
+        rows = owns[t].shape[1]
+        if t == 2:
+            owns[t][...] = windows[t][...].astype(F32)
+        for z in range(SIDE if t < 2 else 0):
+
+            @pl.when(me % SIDE == z)
+            def _():
+                for l in range(LAYERS):
+                    owns[t][l] = windows[t][l].astype(F32)[z * rows : (z + 1) * rows]
+
+
 def gradients_kernel(*refs):
-    (tall, wide, turned, deep), (out, squares, terms), scratch = refs[:4], refs[4:7], refs[7:]
+    (tall, wide, turned, deep), ws, (out, squares, terms), owns, scratch = refs[:4], refs[4:7], refs[7:10], refs[10:13], refs[13:]
     (lhs, rhs, zs, dh, acc, acc2, stage, stage2, shift, r1, r2, r3, own, f1, f2, sums) = scratch[:16]
-    (in_sem, rhs_sem, zs_sem, put_sem, send1, send2, send3, recv1, recv2, recv3, load, send4, recv4) = scratch[16:]
+    *windows, window_sem = scratch[16:20]
+    (in_sem, rhs_sem, zs_sem, put_sem, send1, send2, send3, recv1, recv2, recv3, load, send4, recv4) = scratch[20:]
     at = place()
 
     def fetch_tall(l):
@@ -484,7 +493,7 @@
     fetch_wide(0).start()
     fetch_deep(0).start()
     fetch_turned(0).start()
-    enter(at)
+    enter(at, sorted({*LINES, *PLANE_PEERS}))
 
     def split(c):
         o, s = ORDERS[c], SIGNS[c]
@@ -665,7 +674,7 @@
 
         @pl.when((h == 0) & (m > 2))
         def _():
-            on_third(m - 3)
+            on_third(m - AXES)
 
         @pl.when((h != 0) & (h != 3) & (m > 1) & (m < MATRICES + 2))
         def _():
@@ -683,7 +692,9 @@
 
         return 0
 
-    lax.fori_loop(0, (MATRICES + 2) * TILES + 1, tile, 0)
+    lax.fori_loop(0, (MATRICES + 2) * TILES, tile, 0)
+    own_rows(ws, windows, owns, window_sem)
+    on_third(MATRICES - 1)
 
     total = jnp.zeros((SUBLANES, LANES), F32)
     for m in range(MATRICES):
@@ -692,20 +703,19 @@
     squares[...] = norm_exchange(at, sums, send4, recv4, total)
     for r, sem in ((r1, send1), (r2, send2), (r3, send3)):
         whole(r, sem)
-    for axis in range(AXES):
-        whole(sums.at[axis, pl.ds(0, STEPS)], send4.at[axis])
-
-
-def gradients(tall, wide, turned, deep):
-    g, squares, _ = pl.pallas_call(
+
+
+def gradients(tall, wide, turned, deep, weights):
+    g, squares, _, *owns = pl.pallas_call(
         gradients_kernel,
         out_shape=(
-            jax.ShapeDtypeStruct((MATRICES, BLOCK, LANES), BF16),
-            jax.ShapeDtypeStruct((SUBLANES, LANES), F32),
+            pltpu.VMEM((MATRICES, BLOCK, LANES), BF16),
+            pltpu.VMEM((SUBLANES, LANES), F32),
             jax.ShapeDtypeStruct((MATRICES, SIDE, SIDE, SIDE, BLOCK, LANES), BF16),
+            *[pltpu.VMEM((LAYERS, w.shape[1] // DEVICES, w.shape[2]), F32) for w in weights],
         ),
-        in_specs=[HBM] * 4,
-        out_specs=(VMEM, VMEM, HBM),
+        in_specs=[HBM] * (4 + AXES),
+        out_specs=(VMEM, VMEM, HBM, *[VMEM] * AXES),
         scratch_shapes=[
             pltpu.VMEM((D, TOKENS), BF16),
             pltpu.VMEM((2, TOKENS, TILE), BF16),
@@ -722,17 +732,19 @@
             pltpu.VMEM((WAYS, STEPS, SIDE, SIDE, PART, LANES), BF16),
             pltpu.VMEM((WAYS, SIDE, SIDE, PART, LANES), F32),
             pltpu.VMEM((WAYS, SIDE, PART, LANES), F32),
-            pltpu.VMEM((AXES, SIDE, SUBLANES, LANES), F32),
+            pltpu.VMEM((PLANE + SIDE, SUBLANES, LANES), F32),
+            *[pltpu.VMEM((LAYERS, w.shape[1] // n, w.shape[2]), BF16) for w, n in zip(weights, (PLANE, PLANE, DEVICES), strict=True)],
+            DMA((AXES,)),
             *[DMA((2,))] * 4,
             *[DMA] * AXES,
             DMA((MATRICES, STEPS, SIDE)), DMA((MATRICES, STEPS)), DMA((MATRICES,)),
             DMA((STEPS,)),
-            DMA((AXES,)), DMA((AXES, STEPS)),
+            DMA((2,)), DMA((2,)),
         ],
-        compiler_params=pltpu.CompilerParams(collective_id=0, has_side_effects=True, vmem_limit_bytes=MOST_VMEM),
+        compiler_params=pltpu.CompilerParams(collective_id=0, has_side_effects=True, vmem_limit_bytes=MOST_VMEM - SPARE_VMEM),
         name="gradients",
-    )(tall, wide, turned, deep)
-    return g, squares
+    )(tall, wide, turned, deep, *weights)
+    return g, squares, owns
 
 
 def solution(mesh):
@@ -740,8 +752,8 @@
 
     def step(x, dy, *arrays):
         weights, m, v = (arrays[i : i + 3] for i in (0, 3, 6))
-        g, total = gradients(*by_rows(x[0], dy[0], weights))
-        new, new_m, new_v = adam(sum(w.size for w in weights), g, total, weights, m, v)
+        g, total, owns = gradients(*by_rows(x[0], dy[0], weights), weights)
+        new, new_m, new_v = adam(MATRICES * D * FF, g, total, owns, m, v)
         return (*natural(all_gather(new)), *new_m, *new_v)
 
     whole, rows, sequences = P(None, None, None), P(None, dp, None), P((rep, dp), None, None)

time: 392 us -> 387 us (0.987)
  Pallas kernels: 391 us -> 386 us
where the time goes in v8:
time: 387 us
  Pallas kernels  386 us (100%)
    pallas_call x1, Pallas kernels, gradients(): pl.pallas_call(gradients_kernel, out_shape=(pltpu.VMEM((MATRICES, BLOCK,...  149 us
    pallas_call x1, Pallas kernels, by_rows(): pl.pallas_call(rows_kernel, grid=(TOKENS // ROWS,), out_shape=tuple((jax....  124 us
    pallas_call x1, Pallas kernels, all_gather(): pl.pallas_call(ag_kernel, out_shape=(pltpu.VMEM((SIDE, SIDE, SIDE, *mine....  97.9 us
    pallas_call x1, Pallas kernels, natural(): pl.pallas_call(natural_kernel, grid=(SUBLANES,), out_shape=tuple((jax.Sha...  11 us

profile of v8, /device:TPU:0, one launch (start us, length us, event | category | flops | bytes accessed | tf_op | source)
XLA Modules:
  0.0 386.7 jit_solution(4599391013977451122)
XLA Ops:
  0.6 124.3 %rows.1 = (bf16[2,896,2048]{2,1,0:T(8,128)(2,1)}, bf16[4,2048,2560]{2,1,0:T(8,128)(2,1)}, bf16[2,2560,2048]{2,1,0:T(8,128)(2,1)}, bf16[2,2048,896]{2,1,0:T(8,128)(2,1)}) custom-call(bf16[2048,896]{1,0:T(8,128)(2,1)} %bitcast.26, bf16[2048,896]{1,0:T(8,128)(2,1)} %bitcast.27, bf16[2,896,2560]{2,1,0:T(8,128)(2,1)} %refs_4_.1, bf16[2,896,2560]{2,1,0:T(8,128)(2,1)} %refs_5_.2, ...), custom_call_target="tpu_custom_call" | custom-call | tf_op jit(solution)/shard_map/rows/pallas_call | solution.py:396
  125.0 0.0 copy-start
  125.0 0.0 copy-start.1
  125.0 0.0 copy-start.2
  125.0 0.0 copy-start.3
  125.0 0.0 copy-start.4
  125.0 0.0 copy-start.5
  125.0 149.4 %gradients.1 = (bf16[6,280,128]{2,1,0:T(8,128)(2,1)S(1)}, f32[8,128]{1,0:T(8,128)S(1)}, bf16[6,4,4,4,280,128]{5,4,3,2,1,0:T(8,128)(2,1)}, f32[2,14,2560]{2,1,0:T...) custom-call(bf16[2,896,2048]{2,1,0:T(8,128)(2,1)} %get-tuple-element.34.refs_0_, ...), custom_call_target="tpu_custom_call" | custom-call | tf_op jit(solution)/shard_map/gradients/pallas_call | solution.py:709
  274.4 0.0 copy-done
  274.4 0.0 copy-done.1
  274.4 0.0 copy-done.2
  274.4 0.0 copy-done.3
  274.4 0.0 copy-done.4
  274.5 0.0 copy-done.5
  274.5 3.4 adam.1
  277.8 97.9 %gather.1 = (bf16[4,4,4,280,128]{4,3,2,1,0:T(8,128)(2,1)S(1)}, bf16[4,4,4,280,128]{4,3,2,1,0:T(8,128)(2,1)S(1)}, bf16[4,4,4,280,128]{4,3,2,1,0:T(8,128)(2,1)S(1)...) custom-call(bf16[6,280,128]{2,1,0:T(8,128)(2,1)S(1)} %get-tuple-elem, ...), custom_call_target="tpu_custom_call" | custom-call | tf_op jit(solution)/shard_map/gather/pallas_call | solution.py:164
  375.8 11.0 %natural.1 = (bf16[2,896,2560]{2,1,0:T(8,128)(2,1)}, bf16[2,896,2560]{2,1,0:T(8,128)(2,1)}, bf16[2,2560,896]{2,1,0:T(8,128)(2,1)}) custom-call(bf16[64,280,128]{2,1,0:T(8,128)(2,1)S(1)} %bitcast.16, bf16[64,280,128]{2,1,0:T(8,128)(2,1)S(1)} %bitcast.17, bf16[64,280,128]{2,1,0:T(8,128)(2,1)S(1)} %bitcast.18, bf16[64,280,128]{2,1,0:T(8,128)(2,1)S(1)} %bitcast.19, ...), custom_call_target="tpu_custom_call" | custom-call | tf_op jit(solution)/shard_map/natural/pallas_call | solution.py:235
Async XLA Ops:
  125.0 149.4 %copy-start = (f32[2,14,2560]{2,0,1:T(2,128)S(1)}, f32[2,14,2560]{2,0,1:T(2,128)}, u32[]{:S(2)}) copy-start(f32[2,14,2560]{2,0,1:T(2,128)} %param.16) | copy-start | bytes 860164
  125.0 149.4 %copy-start.1 = (f32[2,14,2560]{2,0,1:T(2,128)S(1)}, f32[2,14,2560]{2,0,1:T(2,128)}, u32[]{:S(2)}) copy-start(f32[2,14,2560]{2,0,1:T(2,128)} %param.17) | copy-start | bytes 860164
  125.0 149.4 %copy-start.2 = (f32[2,40,896]{2,1,0:T(8,128)S(1)}, f32[2,40,896]{2,1,0:T(8,128)}, u32[]{:S(2)}) copy-start(f32[2,40,896]{2,1,0:T(8,128)} %refs_5_.3) | copy-start | bytes 860164
  125.0 149.4 %copy-start.3 = (f32[2,14,2560]{2,0,1:T(2,128)S(1)}, f32[2,14,2560]{2,0,1:T(2,128)}, u32[]{:S(2)}) copy-start(f32[2,14,2560]{2,0,1:T(2,128)} %param.19) | copy-start | bytes 860164
  125.0 149.4 %copy-start.4 = (f32[2,14,2560]{2,0,1:T(2,128)S(1)}, f32[2,14,2560]{2,0,1:T(2,128)}, u32[]{:S(2)}) copy-start(f32[2,14,2560]{2,0,1:T(2,128)} %param.20) | copy-start | bytes 860164
  125.0 149.4 %copy-start.5 = (f32[2,40,896]{2,1,0:T(8,128)S(1)}, f32[2,40,896]{2,1,0:T(8,128)}, u32[]{:S(2)}) copy-start(f32[2,40,896]{2,1,0:T(8,128)} %refs_8_.1) | copy-start | bytes 860164

commit v9 on v8

--- a/solution.py
+++ b/solution.py
@@ -412,33 +412,34 @@
     )(x, dy, *weights)
 
 
+GATE_ROWS, DOWN_ROWS = D // DEVICES, FF // DEVICES
 STARTS = (0, 48, 96, 144, 192, 232)
 PART = 48
 
 
 def gate_block(acc, stage, wide):
     def group(i, _):
-        rows = pl.ds(pl.multiple_of(i * 56, 8), 56)
-        for c in range(4):
+        rows = pl.ds(pl.multiple_of(i * PIECE, SUBLANES), PIECE)
+        for c in range(SIDE):
             piece = acc[rows, pl.ds(c * LANES, LANES)]
-            for z in range(4):
-                wide[z, pl.ds(14 * c, 14), :] = piece[14 * z : 14 * z + 14]
-        for z in range(4):
-            stage[i // 4, i % 4, z] = wide[z].astype(BF16)
+            for z in range(SIDE):
+                wide[z, pl.ds(GATE_ROWS * c, GATE_ROWS), :] = piece[GATE_ROWS * z : GATE_ROWS * (z + 1)]
+        for z in range(SIDE):
+            stage[i // SIDE, i % SIDE, z] = wide[z].astype(BF16)
         return 0
 
-    lax.fori_loop(0, 16, group, 0)
+    lax.fori_loop(0, PLANE, group, 0)
 
 
 def down_block(acc, stage):
     def group(i, _):
-        for t in range(5):
-            rows = acc[pl.ds(pl.multiple_of(i * 40, 8) + 8 * t, 8), :]
-            piece = jnp.concatenate([rows[:, c * LANES : (c + 1) * LANES] for c in range(7)], 0)
-            stage[i // 4, i % 4, pl.ds(56 * t, 56)] = piece.astype(BF16)
+        for t in range(DOWN_ROWS // SUBLANES):
+            rows = acc[pl.ds(pl.multiple_of(i * DOWN_ROWS, SUBLANES) + SUBLANES * t, SUBLANES), :]
+            piece = jnp.concatenate([rows[:, c * LANES : (c + 1) * LANES] for c in range(D // LANES)], 0)
+            stage[i // SIDE, i % SIDE, pl.ds(PIECE * t, PIECE)] = piece.astype(BF16)
         return 0
 
-    lax.fori_loop(0, 16, group, 0)
+    lax.fori_loop(0, PLANE, group, 0)
 
 
 def own_rows(ws, windows, owns, sems):
@@ -464,9 +465,9 @@
 
 def gradients_kernel(*refs):
     (tall, wide, turned, deep), ws, (out, squares, terms), owns, scratch = refs[:4], refs[4:7], refs[7:10], refs[10:13], refs[13:]
-    (lhs, rhs, zs, dh, acc, acc2, stage, stage2, shift, r1, r2, r3, own, f1, f2, sums) = scratch[:16]
-    *windows, window_sem = scratch[16:20]
-    (in_sem, rhs_sem, zs_sem, put_sem, send1, send2, send3, recv1, recv2, recv3, load, send4, recv4) = scratch[20:]
+    (lhs, rhs, zs, dh, acc, acc2, stage, stage2, shift, ra, rf, qa, qf, r3, own, f1, f2, sums) = scratch[:18]
+    *windows, window_sem = scratch[18:22]
+    (in_sem, rhs_sem, zs_sem, put_sem, sent, first_a, first_f, second_a, second_f, recv3, load, send4, recv4) = scratch[22:]
     at = place()
 
     def fetch_tall(l):
@@ -507,91 +508,73 @@
             index[o[1]] = i
         return terms.at[(m, *index, pl.ds(STARTS[c], PART))]
 
-    def first(m, c, step, j, start=False):
-        o, s, p1, p2, p3 = split(c)
-        if start:
-            src = block(m, c, wrap(p1 - s), wrap(p2 - s * (1 + j)))
-        else:
-            src = r1.at[c, m, (step + 2) % STEPS, j]
-        return remote(src, r1.at[c, m, step, j], send1, recv1.at[m, step, j], neighbour(at, o[0], s))
-
-    def loading(m, c, step):
-        o, s, p1, p2, p3 = split(c)
-        return pltpu.make_async_copy(block(m, c, wrap(p1 - s * (2 + step)), None), own.at[c, step], load.at[step])
-
-    def second(m, c, step, start=False):
-        o, s, p1, p2, p3 = split(c)
-        src = r1.at[c, m, 2, 0] if start else r2.at[c, m, (step + 2) % STEPS]
-        return remote(src, r2.at[c, m, step], send2, recv2.at[m, step], neighbour(at, o[1], s))
-
-    def third(m, c, k):
-        o, s, p1, p2, p3 = split(c)
-        return remote(r2.at[c, m, 2, wrap(p3 + k + 1)], r3.at[c, m, k], send3, recv3.at[m], neighbour(at, o[2], k + 1))
+    def piece(c, j):
+        return wrap(split(c)[3] + SIGNS[c] * (2 + j - j // 2 * (2 * j - 1)))
+
+    def along(c, axis, src, there, sem, recv, steps=1):
+        return remote(src, there, sent.at[sem], recv, neighbour(at, ORDERS[c][axis], SIGNS[c] * steps))
+
+    def launch(m):
+        for j in range(SIDE):
+            for c in range(WAYS):
+                src = block(m, c, wrap(split(c)[2] + 2 * SIGNS[c]), piece(c, j))
+                along(c, 0, src, ra.at[c, m, j], 0, first_a.at[m, j]).start()
+        for j in range(SIDE):
+            for c in range(WAYS):
+                src = block(m, c, wrap(split(c)[2] - SIGNS[c]), piece(c, j))
+                along(c, 0, src, rf.at[c, m, 1, j], 1, first_f.at[m, j], -1).start()
+
+    def load_own(m):
+        for k in range(2):
+            for c in range(WAYS):
+                mine = block(m, c, wrap(split(c)[2] + SIGNS[c] * (1 - k)), None)
+                pltpu.make_async_copy(mine, own.at[c, k], load.at[k]).start()
 
     def whole(ref, sem):
         pltpu.make_async_copy(ref, ref, sem).wait()
 
-    def launch(m):
+    def term(c, k, j):
+        i = piece(c, j)
+        mine = own[c, k, i] if ORDERS[c][1] < ORDERS[c][2] else own[c, k, :, i]
+        return mine.astype(F32)
+
+    def on_first_a(m, j):
+        whole(ra.at[:, m, j], first_a.at[m, j])
         for c in range(WAYS):
-            for j in range(SIDE):
-                first(m, c, 0, j, True).start()
-    def load_own(m):
-        for step in range(STEPS):
-            for c in range(WAYS):
-                loading(m, c, step).start()
-
-    def on_first(m, e):
-        step, j = e // SIDE, e % SIDE
-
-        @pl.when(j == 0)
-        def _():
-            whole(own.at[:, step], load.at[step])
-
-        whole(r1.at[:, m, step, j], recv1.at[m, step, j])
-
-        def both(c):
-            o, s, p1, p2, p3 = split(c)
-            i = wrap(p2 - s * (1 + j))
-            mine = own[c, step, i] if o[1] < o[2] else own[c, step, :, i]
-            return r1[c, m, step, j].astype(F32) + mine.astype(F32)
-
-        @pl.when(step < 2)
-        def _():
-            for c in range(WAYS):
-                r1[c, m, step, j] = both(c).astype(BF16)
-                first(m, c, step + 1, j).start()
-
-        @pl.when(step == 2)
-        def _():
-            for c in range(WAYS):
-                total = both(c)
-                f1[c, j] = total
-
-                @pl.when(j == 0)
-                def _():
-                    r1[c, m, 2, 0] = total.astype(BF16)
-                    second(m, c, 0, True).start()
-
-    def on_second(m, step):
-        whole(r2.at[:, m, step], recv2.at[m, step])
-
-        def both(c):
-            return r2[c, m, step].astype(F32) + f1[c, step + 1]
-
-        @pl.when(step < 2)
-        def _():
-            for c in range(WAYS):
-                r2[c, m, step] = both(c).astype(BF16)
-                second(m, c, step + 1).start()
-
-        @pl.when(step == 2)
-        def _():
-            for c in range(WAYS):
-                total = both(c)
-                f2[c] = total
-                r2[c, m, 2] = total.astype(BF16)
-                for k in range(STEPS):
-                    third(m, c, k).start()
+            ra[c, m, j] = (ra[c, m, j].astype(F32) + term(c, 0, j)).astype(BF16)
+            along(c, 0, ra.at[c, m, j], rf.at[c, m, 0, j], 1, first_f.at[m, j]).start()
+
+    def on_first_f(m, j):
+        whole(rf.at[:, m, :, j], first_f.at[m, j])
+        for c in range(WAYS):
+            total = rf[c, m, 0, j].astype(F32) + rf[c, m, 1, j].astype(F32) + term(c, 1, j)
+            if j < 2:
+                rf[c, m, 1, j] = total.astype(BF16)
+            else:
+                f1[c, j - 2] = total
+            if j == 0:
+                along(c, 1, rf.at[c, m, 1, j], qa.at[c, m], 2, second_a.at[m]).start()
+            if j == 1:
+                along(c, 1, rf.at[c, m, 1, j], qf.at[c, m, 1], 3, second_f.at[m], -1).start()
+
+    def on_second_a(m):
+        whole(qa.at[:, m], second_a.at[m])
+        for c in range(WAYS):
+            qa[c, m] = (qa[c, m].astype(F32) + f1[c, 0]).astype(BF16)
+            along(c, 1, qa.at[c, m], qf.at[c, m, 0], 3, second_f.at[m]).start()
+
+    def third(m, c, k):
+        src = qf.at[c, m, 1, wrap(split(c)[4] + k + 1)]
+        return remote(src, r3.at[c, m, k], sent.at[4], recv3.at[m], neighbour(at, ORDERS[c][2], k + 1))
+
+    def on_second_f(m):
+        whole(qf.at[:, m], second_f.at[m])
+        for c in range(WAYS):
+            total = qf[c, m, 0].astype(F32) + qf[c, m, 1].astype(F32) + f1[c, 1]
+            f2[c] = total
+            qf[c, m, 1] = total.astype(BF16)
+            for k in range(STEPS):
+                third(m, c, k).start()
 
     def on_third(m):
         whole(r3.at[:, m], recv3.at[m])
@@ -676,15 +659,32 @@
         def _():
             on_third(m - AXES)
 
-        @pl.when((h != 0) & (h != 3) & (m > 1) & (m < MATRICES + 2))
-        def _():
-            on_second(m - 2, h // 2)
-
-        ring, turn = (i - 1) // TILES - 1, (i - 1) % TILES
-
-        @pl.when((ring >= 0) & (ring < MATRICES))
-        def _():
-            lax.fori_loop(2 * turn + 1 - (SIDE - turn) // SIDE, 2 * turn + 3 + turn // SIDE, lambda e, _: (on_first(ring, e), 0)[1], 0)
+        @pl.when((h == 2) & (m > 1))
+        def _():
+            on_second_a(m - 2)
+
+        @pl.when((h == SIDE) & (m > 1))
+        def _():
+            on_second_f(m - 2)
+
+        @pl.when((h == SIDE) & (m > 0) & (m < MATRICES + 1))
+        def _():
+            whole(own.at[:, 1], load.at[1])
+            for j in range(2):
+                on_first_f(m - 1, j)
+
+        @pl.when((h == 0) & (m > 1))
+        def _():
+            for j in range(2, SIDE):
+                on_first_f(m - 2, j)
+
+        @pl.when(((h == 1) | (h == 2)) & (m > 0) & (m < MATRICES + 1))
+        def _():
+            @pl.when(h == 1)
+            def _():
+                whole(own.at[:, 0], load.at[0])
+
+            lax.fori_loop(h - 1, AXES * h - 2, lambda j, _: (on_first_a(m - 1, j), 0)[1], 0)
 
         @pl.when((h == 0) & (m > 0) & (m < MATRICES + 1))
         def _():
@@ -701,8 +701,8 @@
         g = out[m].astype(F32)
         total = total + jnp.sum((g * g).reshape(-1, SUBLANES, LANES), axis=0)
     squares[...] = norm_exchange(at, sums, send4, recv4, total)
-    for r, sem in ((r1, send1), (r2, send2), (r3, send3)):
-        whole(r, sem)
+    for k, buffer in enumerate((ra, rf, qa, qf, r3)):
+        whole(buffer, sent.at[k])
 
 
 def gradients(tall, wide, turned, deep, weights):
@@ -726,19 +726,21 @@
             pltpu.VMEM((SIDE, SIDE, SIDE, PIECE, LANES), BF16),
             pltpu.VMEM((SIDE, SIDE, BLOCK, LANES), BF16),
             pltpu.VMEM((SIDE, PIECE, LANES), F32),
-            pltpu.VMEM((WAYS, MATRICES, STEPS, SIDE, SIDE, PART, LANES), BF16),
-            pltpu.VMEM((WAYS, MATRICES, STEPS, SIDE, PART, LANES), BF16),
+            pltpu.VMEM((WAYS, MATRICES, SIDE, SIDE, PART, LANES), BF16),
+            pltpu.VMEM((WAYS, MATRICES, 2, SIDE, SIDE, PART, LANES), BF16),
+            pltpu.VMEM((WAYS, MATRICES, SIDE, PART, LANES), BF16),
+            pltpu.VMEM((WAYS, MATRICES, 2, SIDE, PART, LANES), BF16),
             pltpu.VMEM((WAYS, MATRICES, STEPS, PART, LANES), BF16),
-            pltpu.VMEM((WAYS, STEPS, SIDE, SIDE, PART, LANES), BF16),
-            pltpu.VMEM((WAYS, SIDE, SIDE, PART, LANES), F32),
+            pltpu.VMEM((WAYS, 2, SIDE, SIDE, PART, LANES), BF16),
+            pltpu.VMEM((WAYS, 2, SIDE, PART, LANES), F32),
             pltpu.VMEM((WAYS, SIDE, PART, LANES), F32),
             pltpu.VMEM((PLANE + SIDE, SUBLANES, LANES), F32),
             *[pltpu.VMEM((LAYERS, w.shape[1] // n, w.shape[2]), BF16) for w, n in zip(weights, (PLANE, PLANE, DEVICES), strict=True)],
             DMA((AXES,)),
             *[DMA((2,))] * 4,
-            *[DMA] * AXES,
-            DMA((MATRICES, STEPS, SIDE)), DMA((MATRICES, STEPS)), DMA((MATRICES,)),
-            DMA((STEPS,)),
+            DMA((TILES,)),
+            *[DMA((MATRICES, SIDE))] * 2, *[DMA((MATRICES,))] * 3,
+            DMA((2,)),
             DMA((2,)), DMA((2,)),
         ],
         compiler_params=pltpu.CompilerParams(collective_id=0, has_side_effects=True, vmem_limit_bytes=MOST_VMEM - SPARE_VMEM),
@@ -756,11 +758,11 @@
         new, new_m, new_v = adam(MATRICES * D * FF, g, total, owns, m, v)
         return (*natural(all_gather(new)), *new_m, *new_v)
 
-    whole, rows, sequences = P(None, None, None), P(None, dp, None), P((rep, dp), None, None)
+    whole, rows, sequences = P(), P(None, dp), P((rep, dp))
     return jax.shard_map(
         step,
         mesh=mesh,
-        in_specs=(sequences, sequences, *[whole] * 3, *[rows] * 6),
-        out_specs=(*[P(rep, None, None)] * 3, *[P(rep, dp, None)] * 6),
+        in_specs=(sequences, sequences, *[whole] * AXES, *[rows] * MATRICES),
+        out_specs=(*[P(rep)] * AXES, *[P(rep, dp)] * MATRICES),
         check_vma=False,
     )

time: 387 us -> 381 us (0.984)
  Pallas kernels: 386 us -> 380 us
    pallas_call x1, Pallas kernels: 149 us -> 139 us  [gradients(): pl.pallas_call(gradients_kernel, out_shape=(pltpu.VMEM((MATRICES, BLOCK,...]
    pallas_call x1, Pallas kernels: 97.9 us -> 102 us  [all_gather(): pl.pallas_call(ag_kernel, out_shape=(pltpu.VMEM((SIDE, SIDE, SIDE, *mine....]
where the time goes in v9:
time: 381 us
  Pallas kernels  380 us (100%)
    pallas_call x1, Pallas kernels, gradients(): pl.pallas_call(gradients_kernel, out_shape=(pltpu.VMEM((MATRICES, BLOCK,...  139 us
    pallas_call x1, Pallas kernels, by_rows(): pl.pallas_call(rows_kernel, grid=(TOKENS // ROWS,), out_shape=tuple((jax....  124 us
    pallas_call x1, Pallas kernels, all_gather(): pl.pallas_call(ag_kernel, out_shape=(pltpu.VMEM((SIDE, SIDE, SIDE, *mine....  102 us
    pallas_call x1, Pallas kernels, natural(): pl.pallas_call(natural_kernel, grid=(SUBLANES,), out_shape=tuple((jax.Sha...  11 us

profile of v9, /device:TPU:0, one launch (start us, length us, event | category | flops | bytes accessed | tf_op | source)
XLA Modules:
  0.0 380.9 jit_solution(7274526807487558471)
XLA Ops:
  0.6 124.3 %rows.1 = (bf16[2,896,2048]{2,1,0:T(8,128)(2,1)}, bf16[4,2048,2560]{2,1,0:T(8,128)(2,1)}, bf16[2,2560,2048]{2,1,0:T(8,128)(2,1)}, bf16[2,2048,896]{2,1,0:T(8,128)(2,1)}) custom-call(bf16[2048,896]{1,0:T(8,128)(2,1)} %bitcast.26, bf16[2048,896]{1,0:T(8,128)(2,1)} %bitcast.27, bf16[2,896,2560]{2,1,0:T(8,128)(2,1)} %refs_4_.1, bf16[2,896,2560]{2,1,0:T(8,128)(2,1)} %refs_5_.2, ...), custom_call_target="tpu_custom_call" | custom-call | tf_op jit(solution)/shard_map/rows/pallas_call | solution.py:396
  125.0 0.0 copy-start
  125.0 0.0 copy-start.1
  125.0 0.0 copy-start.2
  125.0 0.0 copy-start.3
  125.0 0.0 copy-start.4
  125.0 0.0 copy-start.5
  125.0 139.5 %gradients.1 = (bf16[6,280,128]{2,1,0:T(8,128)(2,1)S(1)}, f32[8,128]{1,0:T(8,128)S(1)}, bf16[6,4,4,4,280,128]{5,4,3,2,1,0:T(8,128)(2,1)}, f32[2,14,2560]{2,1,0:T...) custom-call(bf16[2,896,2048]{2,1,0:T(8,128)(2,1)} %get-tuple-element.34.refs_0_, ...), custom_call_target="tpu_custom_call" | custom-call | tf_op jit(solution)/shard_map/gradients/pallas_call | solution.py:709
  264.5 0.0 copy-done
  264.5 0.0 copy-done.1
  264.5 0.0 copy-done.2
  264.5 0.0 copy-done.3
  264.6 0.0 copy-done.4
  264.6 0.0 copy-done.5
  264.6 3.4 adam.1
  268.0 102.0 %gather.1 = (bf16[4,4,4,280,128]{4,3,2,1,0:T(8,128)(2,1)S(1)}, bf16[4,4,4,280,128]{4,3,2,1,0:T(8,128)(2,1)S(1)}, bf16[4,4,4,280,128]{4,3,2,1,0:T(8,128)(2,1)S(1)...) custom-call(bf16[6,280,128]{2,1,0:T(8,128)(2,1)S(1)} %get-tuple-elem, ...), custom_call_target="tpu_custom_call" | custom-call | tf_op jit(solution)/shard_map/gather/pallas_call | solution.py:164
  369.9 11.0 %natural.1 = (bf16[2,896,2560]{2,1,0:T(8,128)(2,1)}, bf16[2,896,2560]{2,1,0:T(8,128)(2,1)}, bf16[2,2560,896]{2,1,0:T(8,128)(2,1)}) custom-call(bf16[64,280,128]{2,1,0:T(8,128)(2,1)S(1)} %bitcast.16, bf16[64,280,128]{2,1,0:T(8,128)(2,1)S(1)} %bitcast.17, bf16[64,280,128]{2,1,0:T(8,128)(2,1)S(1)} %bitcast.18, bf16[64,280,128]{2,1,0:T(8,128)(2,1)S(1)} %bitcast.19, ...), custom_call_target="tpu_custom_call" | custom-call | tf_op jit(solution)/shard_map/natural/pallas_call | solution.py:235
Async XLA Ops:
  125.0 139.6 %copy-start = (f32[2,14,2560]{2,0,1:T(2,128)S(1)}, f32[2,14,2560]{2,0,1:T(2,128)}, u32[]{:S(2)}) copy-start(f32[2,14,2560]{2,0,1:T(2,128)} %param.16) | copy-start | bytes 860164
  125.0 139.6 %copy-start.1 = (f32[2,14,2560]{2,0,1:T(2,128)S(1)}, f32[2,14,2560]{2,0,1:T(2,128)}, u32[]{:S(2)}) copy-start(f32[2,14,2560]{2,0,1:T(2,128)} %param.17) | copy-start | bytes 860164
  125.0 139.5 %copy-start.2 = (f32[2,40,896]{2,1,0:T(8,128)S(1)}, f32[2,40,896]{2,1,0:T(8,128)}, u32[]{:S(2)}) copy-start(f32[2,40,896]{2,1,0:T(8,128)} %refs_5_.3) | copy-start | bytes 860164
  125.0 139.5 %copy-start.3 = (f32[2,14,2560]{2,0,1:T(2,128)S(1)}, f32[2,14,2560]{2,0,1:T(2,128)}, u32[]{:S(2)}) copy-start(f32[2,14,2560]{2,0,1:T(2,128)} %param.19) | copy-start | bytes 860164
  125.0 139.5 %copy-start.4 = (f32[2,14,2560]{2,0,1:T(2,128)S(1)}, f32[2,14,2560]{2,0,1:T(2,128)}, u32[]{:S(2)}) copy-start(f32[2,14,2560]{2,0,1:T(2,128)} %param.20) | copy-start | bytes 860164
  125.0 139.5 %copy-start.5 = (f32[2,40,896]{2,1,0:T(8,128)S(1)}, f32[2,40,896]{2,1,0:T(8,128)}, u32[]{:S(2)}) copy-start(f32[2,40,896]{2,1,0:T(8,128)} %refs_8_.1) | copy-start | bytes 860164

commit v10 on v9

--- a/solution.py
+++ b/solution.py
@@ -247,6 +247,7 @@
 D, FF, TOKENS = 896, 2560, 2048
 GATE, DOWN = (D, FF), (FF, D)
 ROWS, CHUNK, TILE = 256, 256, 512
+SOON, AHEAD, NEXT = 4, 6, 8
 TILES, PIECE, PLANE_ROWS = FF // TILE, BLOCK * TILE // FF, FF // SIDE
 NT = (((1,), (1,)), ((), ()))
 
@@ -268,7 +269,7 @@
     buffers, (xs, dys, g0, u0, z0, dz1, sems, part_sems, in_sems, out_sems) = rest[:4], rest[4:]
     wg0, wu0, wd0, wg1, wu1, wd1 = weights
     i, slot = pl.program_id(0), pl.program_id(0) % 2
-    first = i == 0
+    first, blocks = i == 0, pl.num_programs(0)
     chunks = [pl.ds(j * CHUNK, CHUNK) for j in range(FF // CHUNK)]
 
     def fetch(k):
@@ -277,42 +278,51 @@
     def fetch_part(k, j):
         return pltpu.make_async_copy(hbm[k].at[0, :, chunks[j]], weights[k].at[:, chunks[j]], part_sems.at[k, j])
 
-    def take(i):
+    def take(source, there, i):
         rows = pl.ds(pl.multiple_of(i * ROWS, ROWS), ROWS)
-        for k, (source, there) in enumerate(((x_hbm, xs), (dy_hbm, dys))):
-            yield pltpu.make_async_copy(source.at[rows], there.at[i % 2], in_sems.at[i % 2, k])
-
-    def put(k, part):
+        slot = i % there.shape[0]
+        return pltpu.make_async_copy(source.at[rows], there.at[slot], in_sems.at[there.shape[0] - 2, slot])
+
+    def put(k, part, slot=slot):
         rows = pl.ds(pl.multiple_of(i * ROWS, ROWS), ROWS)
         there = results[k].at[part, rows] if k % 2 else results[k].at[part, :, rows]
         return pltpu.make_async_copy(buffers[k].at[slot, part], there, out_sems.at[slot, k, part])
 
-    def outs():
-        return [put(k, part) for k in range(4) for part in range(results[k].shape[0])]
+    def outs(slot):
+        return [put(k, part, slot) for k, result in enumerate(results) for part in range(result.shape[0])]
 
     @pl.when(first)
     def _():
-        for copy in take(0):
-            copy.start()
+        take(x_hbm, xs, 0).start()
+        take(dy_hbm, dys, 0).start()
         for j in range(len(chunks)):
             for k in range(2):
                 fetch_part(k, j).start()
-
-    for copy in take(i):
-        copy.wait()
-
-    @pl.when(i + 1 < pl.num_programs(0))
+        take(dy_hbm, dys, 1).start()
+        take(dy_hbm, dys, 0).wait()
+
+    take(x_hbm, xs, i).wait()
+
+    @pl.when(i + 1 < blocks)
     def _():
-        for copy in take(i + 1):
-            copy.start()
+        take(x_hbm, xs, i + 1).start()
+        take(dy_hbm, dys, i + 1).wait()
+
+    @pl.when(i + 2 < blocks)
+    def _():
+        take(dy_hbm, dys, i + 2).start()
 
     @pl.when(i > 1)
     def _():
-        for copy in outs():
+        for copy in outs(slot):
             copy.wait()
 
     tall, wide, turned, deep = (b.at[slot] for b in buffers)
-    x, dy = xs.at[slot], dys.at[slot]
+    x, dy, next_dy = xs.at[slot], dys.at[i % AXES], dys.at[(i + 1) % AXES]
+
+    def make_dz1(dy, some):
+        for ch in some:
+            dz1[:, ch] = dot_t(dy[...], wd1[ch, :]).astype(BF16)
 
     def forward(coming):
         a = (x[...].astype(F32) * scale_of(x[...].astype(F32))).astype(BF16)
@@ -334,6 +344,7 @@
         forward(True)
         for k in range(2, MATRICES):
             fetch(k).wait()
+        make_dz1(dy, chunks[:AHEAD])
 
     @pl.when(i > 0)
     def _():
@@ -341,11 +352,9 @@
 
     for k, part in ((0, 1), (3, 0), (2, 1)):
         put(k, part).start()
-    for ch in chunks[:SIDE]:
-        dz1[:, ch] = dot_t(dy[...], wd1[ch, :]).astype(BF16)
+    make_dz1(dy, chunks[AHEAD:NEXT])
     h = x[...] + dot(z0[...], wd0[...]).astype(BF16)
-    for ch in chunks[SIDE:]:
-        dz1[:, ch] = dot_t(dy[...], wd1[ch, :]).astype(BF16)
+    make_dz1(dy, chunks[NEXT:])
     h = h.astype(F32)
     scale = scale_of(h)
     a = (h * scale).astype(BF16)
@@ -358,13 +367,12 @@
         silu = gate * s
         turned[0, ch, :] = (silu * up).astype(BF16).T
         wide[1, :, ch] = (dz * silu).astype(BF16)
-        wide[0, :, ch] = (dz * up * (s * (1 + gate * (1 - s)))).astype(BF16)
+        wide[0, :, ch] = (dz * up * (s + silu * (1 - s))).astype(BF16)
     for k, part in ((2, 0), (1, 0), (1, 1)):
         put(k, part).start()
-    most, rest = pl.ds(0, FF - CHUNK), chunks[-1]
-    da_gate, da_up = dot_t(wide[0, :, most], wg1[:, most]), dot_t(wide[1, :, most], wu1[:, most])
-    da_gate, da_up = da_gate + dot_t(wide[0, :, rest], wg1[:, rest]), da_up + dot_t(wide[1, :, rest], wu1[:, rest])
-    da = (da_gate.astype(BF16) + da_up.astype(BF16)).astype(F32)
+    da_gate, da_up = dot_t(wg1[...], wide[0]), dot_t(wu1[...], wide[1])
+    make_dz1(next_dy, chunks[:SOON])
+    da = (da_gate.astype(BF16) + da_up.astype(BF16)).T.astype(F32)
     dwide = scale * (da - h * (scale * scale * jnp.mean(da * h, -1, keepdims=True)))
     dh = dy[...] + dwide.astype(BF16)
     deep[1] = dh
@@ -373,21 +381,17 @@
         dz = dot_t(dh, wd0[ch, :]).astype(BF16).astype(F32)
         gate, up = g0[:, ch], u0[:, ch]
         s = jax.nn.sigmoid(gate)
-        wide[3, :, ch] = (dz * (gate * s)).astype(BF16)
-        wide[2, :, ch] = (dz * up * (s * (1 + gate * (1 - s)))).astype(BF16)
+        silu = gate * s
+        wide[3, :, ch] = (dz * silu).astype(BF16)
+        wide[2, :, ch] = (dz * up * (s + silu * (1 - s))).astype(BF16)
+    make_dz1(next_dy, chunks[SOON:AHEAD])
     put(1, 2).start()
     put(1, 3).start()
 
-    @pl.when(i + 1 == pl.num_programs(0))
+    @pl.when(i + 1 == blocks)
     def _():
-        for copy in outs():
+        for copy in outs(slot) + outs(1 - slot):
             copy.wait()
-
-    @pl.when(i + 1 == pl.num_programs(0))
-    def _():
-        for k in range(4):
-            for part in range(results[k].shape[0]):
-                pltpu.make_async_copy(buffers[k].at[1 - slot, part], buffers[k].at[1 - slot, part], out_sems.at[1 - slot, k, part]).wait()
 
 
 def by_rows(x, dy, weights):
@@ -402,10 +406,10 @@
         scratch_shapes=[
             *[pltpu.VMEM(w.shape[1:], BF16) for w in weights * 2],
             *[pltpu.VMEM((2, *b), BF16) for b in buffers],
-            *[pltpu.VMEM((2, ROWS, D), BF16)] * 2,
+            *[pltpu.VMEM((n, ROWS, D), BF16) for n in (2, AXES)],
             *[pltpu.VMEM((ROWS, FF), F32)] * 2,
             *[pltpu.VMEM((ROWS, FF), BF16)] * 2,
-            DMA((MATRICES,)), DMA((2, FF // CHUNK)), DMA((2, 2)), DMA((2, 4, 4)),
+            DMA((MATRICES,)), DMA((2, FF // CHUNK)), DMA((2, AXES)), DMA((2, 4, 4)),
         ],
         compiler_params=pltpu.CompilerParams(vmem_limit_bytes=MOST_VMEM),
         name="rows",

time: 381 us -> 373 us (0.979)
  Pallas kernels: 380 us -> 372 us
    pallas_call x1, Pallas kernels: 124 us -> 117 us  [by_rows(): pl.pallas_call(rows_kernel, grid=(TOKENS // ROWS,), out_shape=tuple((jax....]
where the time goes in v10:
time: 373 us
  Pallas kernels  372 us (100%)
    pallas_call x1, Pallas kernels, gradients(): pl.pallas_call(gradients_kernel, out_shape=(pltpu.VMEM((MATRICES, BLOCK,...  139 us
    pallas_call x1, Pallas kernels, by_rows(): pl.pallas_call(rows_kernel, grid=(TOKENS // ROWS,), out_shape=tuple((jax....  117 us
    pallas_call x1, Pallas kernels, all_gather(): pl.pallas_call(ag_kernel, out_shape=(pltpu.VMEM((SIDE, SIDE, SIDE, *mine....  102 us
    pallas_call x1, Pallas kernels, natural(): pl.pallas_call(natural_kernel, grid=(SUBLANES,), out_shape=tuple((jax.Sha...  11 us

profile of v10, /device:TPU:0, one launch (start us, length us, event | category | flops | bytes accessed | tf_op | source)
XLA Modules:
  0.0 373.2 jit_solution(10528918531312598465)
XLA Ops:
  0.6 116.7 %rows.1 = (bf16[2,896,2048]{2,1,0:T(8,128)(2,1)}, bf16[4,2048,2560]{2,1,0:T(8,128)(2,1)}, bf16[2,2560,2048]{2,1,0:T(8,128)(2,1)}, bf16[2,2048,896]{2,1,0:T(8,128)(2,1)}) custom-call(bf16[2048,896]{1,0:T(8,128)(2,1)} %bitcast.26, bf16[2048,896]{1,0:T(8,128)(2,1)} %bitcast.27, bf16[2,896,2560]{2,1,0:T(8,128)(2,1)} %refs_4_.1, bf16[2,896,2560]{2,1,0:T(8,128)(2,1)} %refs_5_.2, ...), custom_call_target="tpu_custom_call" | custom-call | tf_op jit(solution)/shard_map/rows/pallas_call | solution.py:400
  117.3 0.0 copy-start
  117.3 0.0 copy-start.1
  117.4 0.0 copy-start.2
  117.4 0.0 copy-start.3
  117.4 0.0 copy-start.4
  117.4 0.0 copy-start.5
  117.4 139.5 %gradients.1 = (bf16[6,280,128]{2,1,0:T(8,128)(2,1)S(1)}, f32[8,128]{1,0:T(8,128)S(1)}, bf16[6,4,4,4,280,128]{5,4,3,2,1,0:T(8,128)(2,1)}, f32[2,14,2560]{2,1,0:T...) custom-call(bf16[2,896,2048]{2,1,0:T(8,128)(2,1)} %get-tuple-element.34.refs_0_, ...), custom_call_target="tpu_custom_call" | custom-call | tf_op jit(solution)/shard_map/gradients/pallas_call | solution.py:713
  256.9 0.0 copy-done
  256.9 0.0 copy-done.1
  256.9 0.0 copy-done.2
  256.9 0.0 copy-done.3
  256.9 0.0 copy-done.4
  256.9 0.0 copy-done.5
  256.9 3.4 adam.1
  260.3 101.9 %gather.1 = (bf16[4,4,4,280,128]{4,3,2,1,0:T(8,128)(2,1)S(1)}, bf16[4,4,4,280,128]{4,3,2,1,0:T(8,128)(2,1)S(1)}, bf16[4,4,4,280,128]{4,3,2,1,0:T(8,128)(2,1)S(1)...) custom-call(bf16[6,280,128]{2,1,0:T(8,128)(2,1)S(1)} %get-tuple-elem, ...), custom_call_target="tpu_custom_call" | custom-call | tf_op jit(solution)/shard_map/gather/pallas_call | solution.py:164
  362.3 11.0 %natural.1 = (bf16[2,896,2560]{2,1,0:T(8,128)(2,1)}, bf16[2,896,2560]{2,1,0:T(8,128)(2,1)}, bf16[2,2560,896]{2,1,0:T(8,128)(2,1)}) custom-call(bf16[64,280,128]{2,1,0:T(8,128)(2,1)S(1)} %bitcast.16, bf16[64,280,128]{2,1,0:T(8,128)(2,1)S(1)} %bitcast.17, bf16[64,280,128]{2,1,0:T(8,128)(2,1)S(1)} %bitcast.18, bf16[64,280,128]{2,1,0:T(8,128)(2,1)S(1)} %bitcast.19, ...), custom_call_target="tpu_custom_call" | custom-call | tf_op jit(solution)/shard_map/natural/pallas_call | solution.py:235
Async XLA Ops:
  117.3 139.5 %copy-start = (f32[2,14,2560]{2,0,1:T(2,128)S(1)}, f32[2,14,2560]{2,0,1:T(2,128)}, u32[]{:S(2)}) copy-start(f32[2,14,2560]{2,0,1:T(2,128)} %param.16) | copy-start | bytes 860164
  117.3 139.5 %copy-start.1 = (f32[2,14,2560]{2,0,1:T(2,128)S(1)}, f32[2,14,2560]{2,0,1:T(2,128)}, u32[]{:S(2)}) copy-start(f32[2,14,2560]{2,0,1:T(2,128)} %param.17) | copy-start | bytes 860164
  117.4 139.5 %copy-start.2 = (f32[2,40,896]{2,1,0:T(8,128)S(1)}, f32[2,40,896]{2,1,0:T(8,128)}, u32[]{:S(2)}) copy-start(f32[2,40,896]{2,1,0:T(8,128)} %refs_5_.3) | copy-start | bytes 860164
  117.4 139.5 %copy-start.3 = (f32[2,14,2560]{2,0,1:T(2,128)S(1)}, f32[2,14,2560]{2,0,1:T(2,128)}, u32[]{:S(2)}) copy-start(f32[2,14,2560]{2,0,1:T(2,128)} %param.19) | copy-start | bytes 860164
  117.4 139.5 %copy-start.4 = (f32[2,14,2560]{2,0,1:T(2,128)S(1)}, f32[2,14,2560]{2,0,1:T(2,128)}, u32[]{:S(2)}) copy-start(f32[2,14,2560]{2,0,1:T(2,128)} %param.20) | copy-start | bytes 860164
  117.4 139.5 %copy-start.5 = (f32[2,40,896]{2,1,0:T(8,128)S(1)}, f32[2,40,896]{2,1,0:T(8,128)}, u32[]{:S(2)}) copy-start(f32[2,40,896]{2,1,0:T(8,128)} %refs_8_.1) | copy-start | bytes 860164

commit v11 on v10

--- a/solution.py
+++ b/solution.py
@@ -247,6 +247,7 @@
 D, FF, TOKENS = 896, 2560, 2048
 GATE, DOWN = (D, FF), (FF, D)
 ROWS, CHUNK, TILE = 256, 256, 512
+TALL, WIDE, TURNED, DEEP = range(4)
 SOON, AHEAD, NEXT = 4, 6, 8
 TILES, PIECE, PLANE_ROWS = FF // TILE, BLOCK * TILE // FF, FF // SIDE
 NT = (((1,), (1,)), ((), ()))
@@ -350,7 +351,7 @@
     def _():
         forward(False)
 
-    for k, part in ((0, 1), (3, 0), (2, 1)):
+    for k, part in ((TALL, 1), (DEEP, 0), (TURNED, 1)):
         put(k, part).start()
     make_dz1(dy, chunks[AHEAD:NEXT])
     h = x[...] + dot(z0[...], wd0[...]).astype(BF16)
@@ -359,7 +360,7 @@
     scale = scale_of(h)
     a = (h * scale).astype(BF16)
     tall[0] = a.T
-    put(0, 0).start()
+    put(TALL, 0).start()
     for ch in chunks:
         gate, up = dot(a, wg1[:, ch]), dot(a, wu1[:, ch])
         dz = dz1[:, ch].astype(F32)
@@ -368,7 +369,7 @@
         turned[0, ch, :] = (silu * up).astype(BF16).T
         wide[1, :, ch] = (dz * silu).astype(BF16)
         wide[0, :, ch] = (dz * up * (s + silu * (1 - s))).astype(BF16)
-    for k, part in ((2, 0), (1, 0), (1, 1)):
+    for k, part in ((TURNED, 0), (WIDE, 0), (WIDE, 1)):
         put(k, part).start()
     da_gate, da_up = dot_t(wg1[...], wide[0]), dot_t(wu1[...], wide[1])
     make_dz1(next_dy, chunks[:SOON])
@@ -376,7 +377,7 @@
     dwide = scale * (da - h * (scale * scale * jnp.mean(da * h, -1, keepdims=True)))
     dh = dy[...] + dwide.astype(BF16)
     deep[1] = dh
-    put(3, 1).start()
+    put(DEEP, 1).start()
     for ch in chunks:
         dz = dot_t(dh, wd0[ch, :]).astype(BF16).astype(F32)
         gate, up = g0[:, ch], u0[:, ch]
@@ -385,8 +386,8 @@
         wide[3, :, ch] = (dz * silu).astype(BF16)
         wide[2, :, ch] = (dz * up * (s + silu * (1 - s))).astype(BF16)
     make_dz1(next_dy, chunks[SOON:AHEAD])
-    put(1, 2).start()
-    put(1, 3).start()
+    put(WIDE, 2).start()
+    put(WIDE, 3).start()
 
     @pl.when(i + 1 == blocks)
     def _():
@@ -422,17 +423,14 @@
 
 
 def gate_block(acc, stage, wide):
-    def group(i, _):
-        rows = pl.ds(pl.multiple_of(i * PIECE, SUBLANES), PIECE)
+    for i in range(PLANE):
+        part = wide.at[i % wide.shape[0]]
         for c in range(SIDE):
-            piece = acc[rows, pl.ds(c * LANES, LANES)]
+            piece = acc[pl.ds(i * PIECE, PIECE), pl.ds(c * LANES, LANES)]
             for z in range(SIDE):
-                wide[z, pl.ds(GATE_ROWS * c, GATE_ROWS), :] = piece[GATE_ROWS * z : GATE_ROWS * (z + 1)]
+                part[z, pl.ds(GATE_ROWS * c, GATE_ROWS), :] = piece[GATE_ROWS * z : GATE_ROWS * (z + 1)]
         for z in range(SIDE):
-            stage[i // SIDE, i % SIDE, z] = wide[z].astype(BF16)
-        return 0
-
-    lax.fori_loop(0, PLANE, group, 0)
+            stage[i // SIDE, i % SIDE, z] = part[z].astype(BF16)
 
 
 def down_block(acc, stage):
@@ -469,9 +467,10 @@
 
 def gradients_kernel(*refs):
     (tall, wide, turned, deep), ws, (out, squares, terms), owns, scratch = refs[:4], refs[4:7], refs[7:10], refs[10:13], refs[13:]
-    (lhs, rhs, zs, dh, acc, acc2, stage, stage2, shift, ra, rf, qa, qf, r3, own, f1, f2, sums) = scratch[:18]
-    *windows, window_sem = scratch[18:22]
-    (in_sem, rhs_sem, zs_sem, put_sem, sent, first_a, first_f, second_a, second_f, recv3, load, send4, recv4) = scratch[22:]
+    (lhs, rhs, zs, dh, acc_a, acc_b, acc2, stage_a, stage_b, stage2, shift, ra, rf, qa, qf, r3, own, f1, f2, sums) = scratch[:20]
+    accs, stages = (acc_a, acc_b), (stage_a, stage_b)
+    *windows, window_sem = scratch[20:24]
+    (in_sem, rhs_sem, zs_sem, put_sem, sent, first_a, first_f, second_a, second_f, recv3, load, send4, recv4) = scratch[24:]
     at = place()
 
     def fetch_tall(l):
@@ -488,11 +487,16 @@
         rows = pl.ds(pl.multiple_of(t % SIDE * PLANE_ROWS, LANES), PLANE_ROWS)
         return pltpu.make_async_copy(turned.at[t // SIDE, rows], zs.at[t % 2], zs_sem.at[t % 2])
 
-    def put(m, h):
-        return pltpu.make_async_copy(stage, terms.at[m, :, :, :, pl.ds(pl.multiple_of(PIECE * h, SUBLANES), PIECE)], put_sem.at[0])
+    def arrange(m, h, odd):
+        rows = pl.ds(pl.multiple_of(PIECE * h, SUBLANES), PIECE)
+        gate_block(accs[odd], stages[odd], shift)
+        pltpu.make_async_copy(stages[odd], terms.at[m, :, :, :, rows], put_sem.at[odd]).start()
+
+    def emptied(odd):
+        whole(stages[odd], put_sem.at[odd])
 
     def put2(m, h):
-        return pltpu.make_async_copy(stage2, terms.at[m, h], put_sem.at[1])
+        return pltpu.make_async_copy(stage2, terms.at[m, h], put_sem.at[2])
 
     fetch_tall(0).start()
     fetch_wide(0).start()
@@ -592,12 +596,14 @@
     def tile(i, _):
         m, h = i // TILES, i % TILES
         kind, l = m % AXES, m // AXES
-
-        @pl.when((h == 0) & (m > 0) & (m < MATRICES + 1))
+        launched = (m > 0) & (m < MATRICES + 1)
+
+        @pl.when((h == 0) & launched)
         def _():
             @pl.when(kind > 0)
             def _():
-                put(0, 0).wait()
+                for odd in range(2):
+                    emptied(odd)
 
             @pl.when(kind == 0)
             def _():
@@ -623,14 +629,29 @@
             def _():
                 fetch_wide(t + 1).start()
 
-            acc[...] = dot(lhs[...], rhs[t % 2])
-
-            @pl.when(h > 0)
-            def _():
-                put(m, h).wait()
-
-            gate_block(acc, stage, shift)
-            put(m, h).start()
+            @pl.when(h == 0)
+            def _():
+                accs[0][...] = dot(lhs[...], rhs[t % 2])
+
+            @pl.when(h == AXES)
+            def _():
+                emptied(0)
+
+            @pl.when(h == SIDE)
+            def _():
+                emptied(1)
+
+            for odd in range(2):
+
+                @pl.when((h > 0) & (h % 2 == odd))
+                def _():
+                    accs[odd][...] = dot(lhs[...], rhs[t % 2])
+                    arrange(m, h - 1, 1 - odd)
+
+            @pl.when(h == SIDE)
+            def _():
+                emptied(0)
+                arrange(m, h, 0)
 
         @pl.when((m < MATRICES) & (kind == 2) & (h < SIDE))
         def _():
@@ -671,7 +692,7 @@
         def _():
             on_second_f(m - 2)
 
-        @pl.when((h == SIDE) & (m > 0) & (m < MATRICES + 1))
+        @pl.when((h == SIDE) & launched)
         def _():
             whole(own.at[:, 1], load.at[1])
             for j in range(2):
@@ -682,7 +703,7 @@
             for j in range(2, SIDE):
                 on_first_f(m - 2, j)
 
-        @pl.when(((h == 1) | (h == 2)) & (m > 0) & (m < MATRICES + 1))
+        @pl.when(((h == 1) | (h == 2)) & launched)
         def _():
             @pl.when(h == 1)
             def _():
@@ -690,7 +711,7 @@
 
             lax.fori_loop(h - 1, AXES * h - 2, lambda j, _: (on_first_a(m - 1, j), 0)[1], 0)
 
-        @pl.when((h == 0) & (m > 0) & (m < MATRICES + 1))
+        @pl.when((h == 0) & launched)
         def _():
             load_own(m - 1)
 
@@ -725,11 +746,11 @@
             pltpu.VMEM((2, TOKENS, TILE), BF16),
             pltpu.VMEM((2, PLANE_ROWS, TOKENS), BF16),
             pltpu.VMEM((TOKENS, D), BF16),
-            pltpu.VMEM((D, TILE), F32),
+            *[pltpu.VMEM((D, TILE), F32)] * 2,
             pltpu.VMEM((PLANE_ROWS, D), F32),
-            pltpu.VMEM((SIDE, SIDE, SIDE, PIECE, LANES), BF16),
+            *[pltpu.VMEM((SIDE, SIDE, SIDE, PIECE, LANES), BF16)] * 2,
             pltpu.VMEM((SIDE, SIDE, BLOCK, LANES), BF16),
-            pltpu.VMEM((SIDE, PIECE, LANES), F32),
+            pltpu.VMEM((SIDE, SIDE, PIECE, LANES), F32),
             pltpu.VMEM((WAYS, MATRICES, SIDE, SIDE, PART, LANES), BF16),
             pltpu.VMEM((WAYS, MATRICES, 2, SIDE, SIDE, PART, LANES), BF16),
             pltpu.VMEM((WAYS, MATRICES, SIDE, PART, LANES), BF16),
@@ -741,7 +762,7 @@
             pltpu.VMEM((PLANE + SIDE, SUBLANES, LANES), F32),
             *[pltpu.VMEM((LAYERS, w.shape[1] // n, w.shape[2]), BF16) for w, n in zip(weights, (PLANE, PLANE, DEVICES), strict=True)],
             DMA((AXES,)),
-            *[DMA((2,))] * 4,
+            *[DMA((2,))] * AXES, DMA((AXES,)),
             DMA((TILES,)),
             *[DMA((MATRICES, SIDE))] * 2, *[DMA((MATRICES,))] * 3,
             DMA((2,)),

time: 373 us -> 373 us (level)
  no operation moved by 1% of the time
where the time goes in v11:
time: 373 us
  Pallas kernels  372 us (100%)
    pallas_call x1, Pallas kernels, gradients(): pl.pallas_call(gradients_kernel, out_shape=(pltpu.VMEM((MATRICES, BLOCK,...  139 us
    pallas_call x1, Pallas kernels, by_rows(): pl.pallas_call(rows_kernel, grid=(TOKENS // ROWS,), out_shape=tuple((jax....  117 us
    pallas_call x1, Pallas kernels, all_gather(): pl.pallas_call(ag_kernel, out_shape=(pltpu.VMEM((SIDE, SIDE, SIDE, *mine....  102 us
    pallas_call x1, Pallas kernels, natural(): pl.pallas_call(natural_kernel, grid=(SUBLANES,), out_shape=tuple((jax.Sha...  11 us

profile of v11, /device:TPU:0, one launch (start us, length us, event | category | flops | bytes accessed | tf_op | source)
XLA Modules:
  0.0 373.1 jit_solution(4656706002893345327)
XLA Ops:
  0.6 116.7 %rows.1 = (bf16[2,896,2048]{2,1,0:T(8,128)(2,1)}, bf16[4,2048,2560]{2,1,0:T(8,128)(2,1)}, bf16[2,2560,2048]{2,1,0:T(8,128)(2,1)}, bf16[2,2048,896]{2,1,0:T(8,128)(2,1)}) custom-call(bf16[2048,896]{1,0:T(8,128)(2,1)} %bitcast.26, bf16[2048,896]{1,0:T(8,128)(2,1)} %bitcast.27, bf16[2,896,2560]{2,1,0:T(8,128)(2,1)} %refs_4_.1, bf16[2,896,2560]{2,1,0:T(8,128)(2,1)} %refs_5_.2, ...), custom_call_target="tpu_custom_call" | custom-call | tf_op jit(solution)/shard_map/rows/pallas_call | solution.py:401
  117.3 0.0 copy-start
  117.3 0.0 copy-start.1
  117.4 0.0 copy-start.2
  117.4 0.0 copy-start.3
  117.4 0.0 copy-start.4
  117.4 0.0 copy-start.5
  117.4 139.4 %gradients.1 = (bf16[6,280,128]{2,1,0:T(8,128)(2,1)S(1)}, f32[8,128]{1,0:T(8,128)S(1)}, bf16[6,4,4,4,280,128]{5,4,3,2,1,0:T(8,128)(2,1)}, f32[2,14,2560]{2,1,0:T...) custom-call(bf16[2,896,2048]{2,1,0:T(8,128)(2,1)} %get-tuple-element.34.refs_0_, ...), custom_call_target="tpu_custom_call" | custom-call | tf_op jit(solution)/shard_map/gradients/pallas_call | solution.py:734
  256.8 0.0 copy-done
  256.8 0.0 copy-done.1
  256.8 0.0 copy-done.2
  256.8 0.0 copy-done.3
  256.9 0.0 copy-done.4
  256.9 0.0 copy-done.5
  256.9 3.4 adam.1
  260.2 101.9 %gather.1 = (bf16[4,4,4,280,128]{4,3,2,1,0:T(8,128)(2,1)S(1)}, bf16[4,4,4,280,128]{4,3,2,1,0:T(8,128)(2,1)S(1)}, bf16[4,4,4,280,128]{4,3,2,1,0:T(8,128)(2,1)S(1)...) custom-call(bf16[6,280,128]{2,1,0:T(8,128)(2,1)S(1)} %get-tuple-elem, ...), custom_call_target="tpu_custom_call" | custom-call | tf_op jit(solution)/shard_map/gather/pallas_call | solution.py:164
  362.1 11.0 %natural.1 = (bf16[2,896,2560]{2,1,0:T(8,128)(2,1)}, bf16[2,896,2560]{2,1,0:T(8,128)(2,1)}, bf16[2,2560,896]{2,1,0:T(8,128)(2,1)}) custom-call(bf16[64,280,128]{2,1,0:T(8,128)(2,1)S(1)} %bitcast.16, bf16[64,280,128]{2,1,0:T(8,128)(2,1)S(1)} %bitcast.17, bf16[64,280,128]{2,1,0:T(8,128)(2,1)S(1)} %bitcast.18, bf16[64,280,128]{2,1,0:T(8,128)(2,1)S(1)} %bitcast.19, ...), custom_call_target="tpu_custom_call" | custom-call | tf_op jit(solution)/shard_map/natural/pallas_call | solution.py:235
Async XLA Ops:
  117.3 139.5 %copy-start = (f32[2,14,2560]{2,0,1:T(2,128)S(1)}, f32[2,14,2560]{2,0,1:T(2,128)}, u32[]{:S(2)}) copy-start(f32[2,14,2560]{2,0,1:T(2,128)} %param.16) | copy-start | bytes 860164
  117.3 139.5 %copy-start.1 = (f32[2,14,2560]{2,0,1:T(2,128)S(1)}, f32[2,14,2560]{2,0,1:T(2,128)}, u32[]{:S(2)}) copy-start(f32[2,14,2560]{2,0,1:T(2,128)} %param.17) | copy-start | bytes 860164
  117.4 139.5 %copy-start.2 = (f32[2,40,896]{2,1,0:T(8,128)S(1)}, f32[2,40,896]{2,1,0:T(8,128)}, u32[]{:S(2)}) copy-start(f32[2,40,896]{2,1,0:T(8,128)} %refs_5_.3) | copy-start | bytes 860164
  117.4 139.5 %copy-start.3 = (f32[2,14,2560]{2,0,1:T(2,128)S(1)}, f32[2,14,2560]{2,0,1:T(2,128)}, u32[]{:S(2)}) copy-start(f32[2,14,2560]{2,0,1:T(2,128)} %param.19) | copy-start | bytes 860164
  117.4 139.5 %copy-start.4 = (f32[2,14,2560]{2,0,1:T(2,128)S(1)}, f32[2,14,2560]{2,0,1:T(2,128)}, u32[]{:S(2)}) copy-start(f32[2,14,2560]{2,0,1:T(2,128)} %param.20) | copy-start | bytes 860164
  117.4 139.5 %copy-start.5 = (f32[2,40,896]{2,1,0:T(8,128)S(1)}, f32[2,40,896]{2,1,0:T(8,128)}, u32[]{:S(2)}) copy-start(f32[2,40,896]{2,1,0:T(8,128)} %refs_8_.1) | copy-start | bytes 860164

commit v12 on v11

--- a/solution.py
+++ b/solution.py
@@ -18,6 +18,8 @@
 MOST_VMEM, SPARE_VMEM = 62 * MIB, 2 * MIB
 ORDERS = tuple(tuple((way // 2 + i) % AXES for i in range(AXES)) for way in range(WAYS))
 SIGNS = (1, -1) * AXES
+TURNS = tuple(tuple((way + i) % AXES for i in range(AXES)) for way in range(WAYS))
+SENSES = (1,) * AXES + (-1,) * AXES
 TAKEN = (3, 0, 4, 1, 5, 2)
 
 
@@ -505,11 +507,11 @@
     enter(at, sorted({*LINES, *PLANE_PEERS}))
 
     def split(c):
-        o, s = ORDERS[c], SIGNS[c]
+        o, s = TURNS[c], SENSES[c]
         return o, s, at[o[0]], at[o[1]], at[o[2]]
 
     def block(m, c, a, i):
-        o = ORDERS[c]
+        o = TURNS[c]
         index = [slice(None)] * 3
         index[o[0]] = a
         if i is not None:
@@ -517,25 +519,27 @@
         return terms.at[(m, *index, pl.ds(STARTS[c], PART))]
 
     def piece(c, j):
-        return wrap(split(c)[3] + SIGNS[c] * (2 + j - j // 2 * (2 * j - 1)))
+        return wrap(split(c)[3] + SENSES[c] * (2 + j - j // 2 * (2 * j - 1)))
 
     def along(c, axis, src, there, sem, recv, steps=1):
-        return remote(src, there, sent.at[sem], recv, neighbour(at, ORDERS[c][axis], SIGNS[c] * steps))
-
-    def launch(m):
+        return remote(src, there, sent.at[sem], recv, neighbour(at, TURNS[c][axis], SENSES[c] * steps))
+
+    def launch_a(m, ways):
         for j in range(SIDE):
-            for c in range(WAYS):
-                src = block(m, c, wrap(split(c)[2] + 2 * SIGNS[c]), piece(c, j))
+            for c in ways:
+                src = block(m, c, wrap(split(c)[2] + 2 * SENSES[c]), piece(c, j))
                 along(c, 0, src, ra.at[c, m, j], 0, first_a.at[m, j]).start()
+
+    def launch_d(m, ways):
         for j in range(SIDE):
-            for c in range(WAYS):
-                src = block(m, c, wrap(split(c)[2] - SIGNS[c]), piece(c, j))
+            for c in ways:
+                src = block(m, c, wrap(split(c)[2] - SENSES[c]), piece(c, j))
                 along(c, 0, src, rf.at[c, m, 1, j], 1, first_f.at[m, j], -1).start()
 
     def load_own(m):
         for k in range(2):
             for c in range(WAYS):
-                mine = block(m, c, wrap(split(c)[2] + SIGNS[c] * (1 - k)), None)
+                mine = block(m, c, wrap(split(c)[2] + SENSES[c] * (1 - k)), None)
                 pltpu.make_async_copy(mine, own.at[c, k], load.at[k]).start()
 
     def whole(ref, sem):
@@ -543,7 +547,7 @@
 
     def term(c, k, j):
         i = piece(c, j)
-        mine = own[c, k, i] if ORDERS[c][1] < ORDERS[c][2] else own[c, k, :, i]
+        mine = own[c, k, i] if TURNS[c][1] < TURNS[c][2] else own[c, k, :, i]
         return mine.astype(F32)
 
     def on_first_a(m, j):
@@ -573,7 +577,7 @@
 
     def third(m, c, k):
         src = qf.at[c, m, 1, wrap(split(c)[4] + k + 1)]
-        return remote(src, r3.at[c, m, k], sent.at[4], recv3.at[m], neighbour(at, ORDERS[c][2], k + 1))
+        return remote(src, r3.at[c, m, k], sent.at[4], recv3.at[m], neighbour(at, TURNS[c][2], k + 1))
 
     def on_second_f(m):
         whole(qf.at[:, m], second_f.at[m])
@@ -598,6 +602,14 @@
         kind, l = m % AXES, m // AXES
         launched = (m > 0) & (m < MATRICES + 1)
 
+        early = i == SIDE
+        halves = (early | ((h == 0) & launched & (m > 1)), range(AXES)), ((h == 0) & launched, range(AXES, WAYS))
+
+        @pl.when(early)
+        def _():
+            for odd in range(2):
+                emptied(odd)
+
         @pl.when((h == 0) & launched)
         def _():
             @pl.when(kind > 0)
@@ -609,7 +621,12 @@
             def _():
                 put2(0, 0).wait()
 
-            launch(m - 1)
+        for send in (launch_a, launch_d):
+            for now, ways in halves:
+
+                @pl.when(now)
+                def _():
+                    send(jnp.where(early, m, m - 1), ways)
 
         @pl.when((m < MATRICES) & (kind < 2))
         def _():
@@ -637,7 +654,7 @@
             def _():
                 emptied(0)
 
-            @pl.when(h == SIDE)
+            @pl.when((h == SIDE) & (m > 0))
             def _():
                 emptied(1)
 
@@ -648,9 +665,12 @@
                     accs[odd][...] = dot(lhs[...], rhs[t % 2])
                     arrange(m, h - 1, 1 - odd)
 
+            @pl.when((h == SIDE) & (m > 0))
+            def _():
+                emptied(0)
+
             @pl.when(h == SIDE)
             def _():
-                emptied(0)
                 arrange(m, h, 0)
 
         @pl.when((m < MATRICES) & (kind == 2) & (h < SIDE))

time: 373 us -> 374 us (level)
  no operation moved by 1% of the time
where the time goes in v12:
time: 374 us
  Pallas kernels  373 us (100%)
    pallas_call x1, Pallas kernels, gradients(): pl.pallas_call(gradients_kernel, out_shape=(pltpu.VMEM((MATRICES, BLOCK,...  140 us
    pallas_call x1, Pallas kernels, by_rows(): pl.pallas_call(rows_kernel, grid=(TOKENS // ROWS,), out_shape=tuple((jax....  117 us
    pallas_call x1, Pallas kernels, all_gather(): pl.pallas_call(ag_kernel, out_shape=(pltpu.VMEM((SIDE, SIDE, SIDE, *mine....  102 us
    pallas_call x1, Pallas kernels, natural(): pl.pallas_call(natural_kernel, grid=(SUBLANES,), out_shape=tuple((jax.Sha...  11 us

profile of v12, /device:TPU:0, one launch (start us, length us, event | category | flops | bytes accessed | tf_op | source)
XLA Modules:
  0.0 373.9 jit_solution(9680759476668917617)
XLA Ops:
  0.6 116.7 %rows.1 = (bf16[2,896,2048]{2,1,0:T(8,128)(2,1)}, bf16[4,2048,2560]{2,1,0:T(8,128)(2,1)}, bf16[2,2560,2048]{2,1,0:T(8,128)(2,1)}, bf16[2,2048,896]{2,1,0:T(8,128)(2,1)}) custom-call(bf16[2048,896]{1,0:T(8,128)(2,1)} %bitcast.26, bf16[2048,896]{1,0:T(8,128)(2,1)} %bitcast.27, bf16[2,896,2560]{2,1,0:T(8,128)(2,1)} %refs_4_.1, bf16[2,896,2560]{2,1,0:T(8,128)(2,1)} %refs_5_.2, ...), custom_call_target="tpu_custom_call" | custom-call | tf_op jit(solution)/shard_map/rows/pallas_call | solution.py:403
  117.3 0.0 copy-start
  117.3 0.0 copy-start.1
  117.4 0.0 copy-start.2
  117.4 0.0 copy-start.3
  117.4 0.0 copy-start.4
  117.4 0.0 copy-start.5
  117.4 140.4 %gradients.1 = (bf16[6,280,128]{2,1,0:T(8,128)(2,1)S(1)}, f32[8,128]{1,0:T(8,128)S(1)}, bf16[6,4,4,4,280,128]{5,4,3,2,1,0:T(8,128)(2,1)}, f32[2,14,2560]{2,1,0:T...) custom-call(bf16[2,896,2048]{2,1,0:T(8,128)(2,1)} %get-tuple-element.34.refs_0_, ...), custom_call_target="tpu_custom_call" | custom-call | tf_op jit(solution)/shard_map/gradients/pallas_call | solution.py:754
  257.8 0.0 copy-done
  257.8 0.0 copy-done.1
  257.8 0.0 copy-done.2
  257.8 0.0 copy-done.3
  257.8 0.0 copy-done.4
  257.8 0.0 copy-done.5
  257.8 3.4 adam.1
  261.2 101.7 %gather.1 = (bf16[4,4,4,280,128]{4,3,2,1,0:T(8,128)(2,1)S(1)}, bf16[4,4,4,280,128]{4,3,2,1,0:T(8,128)(2,1)S(1)}, bf16[4,4,4,280,128]{4,3,2,1,0:T(8,128)(2,1)S(1)...) custom-call(bf16[6,280,128]{2,1,0:T(8,128)(2,1)S(1)} %get-tuple-elem, ...), custom_call_target="tpu_custom_call" | custom-call | tf_op jit(solution)/shard_map/gather/pallas_call | solution.py:166
  362.9 11.0 %natural.1 = (bf16[2,896,2560]{2,1,0:T(8,128)(2,1)}, bf16[2,896,2560]{2,1,0:T(8,128)(2,1)}, bf16[2,2560,896]{2,1,0:T(8,128)(2,1)}) custom-call(bf16[64,280,128]{2,1,0:T(8,128)(2,1)S(1)} %bitcast.16, bf16[64,280,128]{2,1,0:T(8,128)(2,1)S(1)} %bitcast.17, bf16[64,280,128]{2,1,0:T(8,128)(2,1)S(1)} %bitcast.18, bf16[64,280,128]{2,1,0:T(8,128)(2,1)S(1)} %bitcast.19, ...), custom_call_target="tpu_custom_call" | custom-call | tf_op jit(solution)/shard_map/natural/pallas_call | solution.py:237
Async XLA Ops:
  117.3 140.5 %copy-start = (f32[2,14,2560]{2,0,1:T(2,128)S(1)}, f32[2,14,2560]{2,0,1:T(2,128)}, u32[]{:S(2)}) copy-start(f32[2,14,2560]{2,0,1:T(2,128)} %param.16) | copy-start | bytes 860164
  117.3 140.4 %copy-start.1 = (f32[2,14,2560]{2,0,1:T(2,128)S(1)}, f32[2,14,2560]{2,0,1:T(2,128)}, u32[]{:S(2)}) copy-start(f32[2,14,2560]{2,0,1:T(2,128)} %param.17) | copy-start | bytes 860164
  117.4 140.4 %copy-start.2 = (f32[2,40,896]{2,1,0:T(8,128)S(1)}, f32[2,40,896]{2,1,0:T(8,128)}, u32[]{:S(2)}) copy-start(f32[2,40,896]{2,1,0:T(8,128)} %refs_5_.3) | copy-start | bytes 860164
  117.4 140.4 %copy-start.3 = (f32[2,14,2560]{2,0,1:T(2,128)S(1)}, f32[2,14,2560]{2,0,1:T(2,128)}, u32[]{:S(2)}) copy-start(f32[2,14,2560]{2,0,1:T(2,128)} %param.19) | copy-start | bytes 860164
  117.4 140.4 %copy-start.4 = (f32[2,14,2560]{2,0,1:T(2,128)S(1)}, f32[2,14,2560]{2,0,1:T(2,128)}, u32[]{:S(2)}) copy-start(f32[2,14,2560]{2,0,1:T(2,128)} %param.20) | copy-start | bytes 860164
  117.4 140.4 %copy-start.5 = (f32[2,40,896]{2,1,0:T(8,128)S(1)}, f32[2,40,896]{2,1,0:T(8,128)}, u32[]{:S(2)}) copy-start(f32[2,40,896]{2,1,0:T(8,128)} %refs_8_.1) | copy-start | bytes 860164

commit v13 on v11

--- a/solution.py
+++ b/solution.py
@@ -48,6 +48,7 @@
 LINES = tuple(tuple(k * (axis == line) for axis in range(AXES)) for line in range(AXES) for k in range(1, SIDE))
 PLANE_PEERS = tuple((0, k // SIDE, k % SIDE) for k in range(1, PLANE))
 LINE_PEERS = LINES[:STEPS]
+NEIGHBOURS = tuple(steps for steps in LINES if 2 not in steps)
 
 
 def enter(at, peers):
@@ -110,7 +111,7 @@
 def ag_kernel(*refs):
     mine, outs, (sends, recv1, recv2, recv3, recv4, local) = refs[0], refs[1 : 1 + WAYS], refs[1 + WAYS :]
     at = place()
-    enter(at, LINES)
+    enter(at, NEIGHBOURS)
 
     def where(c, key):
         index = [None] * AXES

time: 373 us -> 373 us (level)
  no operation moved by 1% of the time
where the time goes in v13:
time: 373 us
  Pallas kernels  372 us (100%)
    pallas_call x1, Pallas kernels, gradients(): pl.pallas_call(gradients_kernel, out_shape=(pltpu.VMEM((MATRICES, BLOCK,...  139 us
    pallas_call x1, Pallas kernels, by_rows(): pl.pallas_call(rows_kernel, grid=(TOKENS // ROWS,), out_shape=tuple((jax....  117 us
    pallas_call x1, Pallas kernels, all_gather(): pl.pallas_call(ag_kernel, out_shape=(pltpu.VMEM((SIDE, SIDE, SIDE, *mine....  102 us
    pallas_call x1, Pallas kernels, natural(): pl.pallas_call(natural_kernel, grid=(SUBLANES,), out_shape=tuple((jax.Sha...  11 us

profile of v13, /device:TPU:0, one launch (start us, length us, event | category | flops | bytes accessed | tf_op | source)
XLA Modules:
  0.0 373.1 jit_solution(9273443660929090131)
XLA Ops:
  0.6 116.7 %rows.1 = (bf16[2,896,2048]{2,1,0:T(8,128)(2,1)}, bf16[4,2048,2560]{2,1,0:T(8,128)(2,1)}, bf16[2,2560,2048]{2,1,0:T(8,128)(2,1)}, bf16[2,2048,896]{2,1,0:T(8,128)(2,1)}) custom-call(bf16[2048,896]{1,0:T(8,128)(2,1)} %bitcast.26, bf16[2048,896]{1,0:T(8,128)(2,1)} %bitcast.27, bf16[2,896,2560]{2,1,0:T(8,128)(2,1)} %refs_4_.1, bf16[2,896,2560]{2,1,0:T(8,128)(2,1)} %refs_5_.2, ...), custom_call_target="tpu_custom_call" | custom-call | tf_op jit(solution)/shard_map/rows/pallas_call | solution.py:402
  117.3 0.0 copy-start
  117.3 0.0 copy-start.1
  117.4 0.0 copy-start.2
  117.4 0.0 copy-start.3
  117.4 0.0 copy-start.4
  117.4 0.0 copy-start.5
  117.4 139.4 %gradients.1 = (bf16[6,280,128]{2,1,0:T(8,128)(2,1)S(1)}, f32[8,128]{1,0:T(8,128)S(1)}, bf16[6,4,4,4,280,128]{5,4,3,2,1,0:T(8,128)(2,1)}, f32[2,14,2560]{2,1,0:T...) custom-call(bf16[2,896,2048]{2,1,0:T(8,128)(2,1)} %get-tuple-element.34.refs_0_, ...), custom_call_target="tpu_custom_call" | custom-call | tf_op jit(solution)/shard_map/gradients/pallas_call | solution.py:735
  256.8 0.0 copy-done
  256.8 0.0 copy-done.1
  256.8 0.0 copy-done.2
  256.8 0.0 copy-done.3
  256.9 0.0 copy-done.4
  256.9 0.0 copy-done.5
  256.9 3.4 adam.1
  260.2 101.9 %gather.1 = (bf16[4,4,4,280,128]{4,3,2,1,0:T(8,128)(2,1)S(1)}, bf16[4,4,4,280,128]{4,3,2,1,0:T(8,128)(2,1)S(1)}, bf16[4,4,4,280,128]{4,3,2,1,0:T(8,128)(2,1)S(1)...) custom-call(bf16[6,280,128]{2,1,0:T(8,128)(2,1)S(1)} %get-tuple-elem, ...), custom_call_target="tpu_custom_call" | custom-call | tf_op jit(solution)/shard_map/gather/pallas_call | solution.py:165
  362.1 11.0 %natural.1 = (bf16[2,896,2560]{2,1,0:T(8,128)(2,1)}, bf16[2,896,2560]{2,1,0:T(8,128)(2,1)}, bf16[2,2560,896]{2,1,0:T(8,128)(2,1)}) custom-call(bf16[64,280,128]{2,1,0:T(8,128)(2,1)S(1)} %bitcast.16, bf16[64,280,128]{2,1,0:T(8,128)(2,1)S(1)} %bitcast.17, bf16[64,280,128]{2,1,0:T(8,128)(2,1)S(1)} %bitcast.18, bf16[64,280,128]{2,1,0:T(8,128)(2,1)S(1)} %bitcast.19, ...), custom_call_target="tpu_custom_call" | custom-call | tf_op jit(solution)/shard_map/natural/pallas_call | solution.py:236
Async XLA Ops:
  117.3 139.5 %copy-start = (f32[2,14,2560]{2,0,1:T(2,128)S(1)}, f32[2,14,2560]{2,0,1:T(2,128)}, u32[]{:S(2)}) copy-start(f32[2,14,2560]{2,0,1:T(2,128)} %param.16) | copy-start | bytes 860164
  117.3 139.5 %copy-start.1 = (f32[2,14,2560]{2,0,1:T(2,128)S(1)}, f32[2,14,2560]{2,0,1:T(2,128)}, u32[]{:S(2)}) copy-start(f32[2,14,2560]{2,0,1:T(2,128)} %param.17) | copy-start | bytes 860164
  117.4 139.5 %copy-start.2 = (f32[2,40,896]{2,1,0:T(8,128)S(1)}, f32[2,40,896]{2,1,0:T(8,128)}, u32[]{:S(2)}) copy-start(f32[2,40,896]{2,1,0:T(8,128)} %refs_5_.3) | copy-start | bytes 860164
  117.4 139.5 %copy-start.3 = (f32[2,14,2560]{2,0,1:T(2,128)S(1)}, f32[2,14,2560]{2,0,1:T(2,128)}, u32[]{:S(2)}) copy-start(f32[2,14,2560]{2,0,1:T(2,128)} %param.19) | copy-start | bytes 860164
  117.4 139.5 %copy-start.4 = (f32[2,14,2560]{2,0,1:T(2,128)S(1)}, f32[2,14,2560]{2,0,1:T(2,128)}, u32[]{:S(2)}) copy-start(f32[2,14,2560]{2,0,1:T(2,128)} %param.20) | copy-start | bytes 860164
  117.4 139.5 %copy-start.5 = (f32[2,40,896]{2,1,0:T(8,128)S(1)}, f32[2,40,896]{2,1,0:T(8,128)}, u32[]{:S(2)}) copy-start(f32[2,40,896]{2,1,0:T(8,128)} %refs_8_.1) | copy-start | bytes 860164

commit v14 on v13

--- a/solution.py
+++ b/solution.py
@@ -681,11 +681,11 @@
             down_block(acc2, stage2)
             put2(m, h).start()
 
-        @pl.when((h == 0) & (m > 2))
+        @pl.when((h == 1) & (m > 2))
         def _():
             on_third(m - AXES)
 
-        @pl.when((h == 2) & (m > 1))
+        @pl.when((h == 1) & (m > 1))
         def _():
             on_second_a(m - 2)
 
@@ -696,12 +696,11 @@
         @pl.when((h == SIDE) & launched)
         def _():
             whole(own.at[:, 1], load.at[1])
-            for j in range(2):
-                on_first_f(m - 1, j)
+            on_first_f(m - 1, 0)
 
         @pl.when((h == 0) & (m > 1))
         def _():
-            for j in range(2, SIDE):
+            for j in range(1, SIDE):
                 on_first_f(m - 2, j)
 
         @pl.when(((h == 1) | (h == 2)) & launched)

time: 373 us -> 374 us (level)
  no operation moved by 1% of the time
where the time goes in v14:
time: 374 us; the launch traced here: 373 us
  Pallas kernels  373 us (100%)
    pallas_call x1, Pallas kernels, gradients(): pl.pallas_call(gradients_kernel, out_shape=(pltpu.VMEM((MATRICES, BLOCK,...  140 us
    pallas_call x1, Pallas kernels, by_rows(): pl.pallas_call(rows_kernel, grid=(TOKENS // ROWS,), out_shape=tuple((jax....  117 us
    pallas_call x1, Pallas kernels, all_gather(): pl.pallas_call(ag_kernel, out_shape=(pltpu.VMEM((SIDE, SIDE, SIDE, *mine....  102 us
    pallas_call x1, Pallas kernels, natural(): pl.pallas_call(natural_kernel, grid=(SUBLANES,), out_shape=tuple((jax.Sha...  11 us

profile of v14, /device:TPU:0, one launch (start us, length us, event | category | flops | bytes accessed | tf_op | source)
XLA Modules:
  0.0 373.4 jit_solution(6546635558169414467)
XLA Ops:
  0.6 116.7 %rows.1 = (bf16[2,896,2048]{2,1,0:T(8,128)(2,1)}, bf16[4,2048,2560]{2,1,0:T(8,128)(2,1)}, bf16[2,2560,2048]{2,1,0:T(8,128)(2,1)}, bf16[2,2048,896]{2,1,0:T(8,128)(2,1)}) custom-call(bf16[2048,896]{1,0:T(8,128)(2,1)} %bitcast.26, bf16[2048,896]{1,0:T(8,128)(2,1)} %bitcast.27, bf16[2,896,2560]{2,1,0:T(8,128)(2,1)} %refs_4_.1, bf16[2,896,2560]{2,1,0:T(8,128)(2,1)} %refs_5_.2, ...), custom_call_target="tpu_custom_call" | custom-call | tf_op jit(solution)/shard_map/rows/pallas_call | solution.py:402
  117.3 0.0 copy-start
  117.3 0.0 copy-start.1
  117.4 0.0 copy-start.2
  117.4 0.0 copy-start.3
  117.4 0.0 copy-start.4
  117.4 0.0 copy-start.5
  117.4 139.7 %gradients.1 = (bf16[6,280,128]{2,1,0:T(8,128)(2,1)S(1)}, f32[8,128]{1,0:T(8,128)S(1)}, bf16[6,4,4,4,280,128]{5,4,3,2,1,0:T(8,128)(2,1)}, f32[2,14,2560]{2,1,0:T...) custom-call(bf16[2,896,2048]{2,1,0:T(8,128)(2,1)} %get-tuple-element.34.refs_0_, ...), custom_call_target="tpu_custom_call" | custom-call | tf_op jit(solution)/shard_map/gradients/pallas_call | solution.py:734
  257.1 0.0 copy-done
  257.1 0.0 copy-done.1
  257.1 0.0 copy-done.2
  257.2 0.0 copy-done.3
  257.2 0.0 copy-done.4
  257.2 0.0 copy-done.5
  257.2 3.4 adam.1
  260.6 101.8 %gather.1 = (bf16[4,4,4,280,128]{4,3,2,1,0:T(8,128)(2,1)S(1)}, bf16[4,4,4,280,128]{4,3,2,1,0:T(8,128)(2,1)S(1)}, bf16[4,4,4,280,128]{4,3,2,1,0:T(8,128)(2,1)S(1)...) custom-call(bf16[6,280,128]{2,1,0:T(8,128)(2,1)S(1)} %get-tuple-elem, ...), custom_call_target="tpu_custom_call" | custom-call | tf_op jit(solution)/shard_map/gather/pallas_call | solution.py:165
  362.4 11.0 %natural.1 = (bf16[2,896,2560]{2,1,0:T(8,128)(2,1)}, bf16[2,896,2560]{2,1,0:T(8,128)(2,1)}, bf16[2,2560,896]{2,1,0:T(8,128)(2,1)}) custom-call(bf16[64,280,128]{2,1,0:T(8,128)(2,1)S(1)} %bitcast.16, bf16[64,280,128]{2,1,0:T(8,128)(2,1)S(1)} %bitcast.17, bf16[64,280,128]{2,1,0:T(8,128)(2,1)S(1)} %bitcast.18, bf16[64,280,128]{2,1,0:T(8,128)(2,1)S(1)} %bitcast.19, ...), custom_call_target="tpu_custom_call" | custom-call | tf_op jit(solution)/shard_map/natural/pallas_call | solution.py:236
Async XLA Ops:
  117.3 139.8 %copy-start = (f32[2,14,2560]{2,0,1:T(2,128)S(1)}, f32[2,14,2560]{2,0,1:T(2,128)}, u32[]{:S(2)}) copy-start(f32[2,14,2560]{2,0,1:T(2,128)} %param.16) | copy-start | bytes 860164
  117.3 139.8 %copy-start.1 = (f32[2,14,2560]{2,0,1:T(2,128)S(1)}, f32[2,14,2560]{2,0,1:T(2,128)}, u32[]{:S(2)}) copy-start(f32[2,14,2560]{2,0,1:T(2,128)} %param.17) | copy-start | bytes 860164
  117.4 139.8 %copy-start.2 = (f32[2,40,896]{2,1,0:T(8,128)S(1)}, f32[2,40,896]{2,1,0:T(8,128)}, u32[]{:S(2)}) copy-start(f32[2,40,896]{2,1,0:T(8,128)} %refs_5_.3) | copy-start | bytes 860164
  117.4 139.8 %copy-start.3 = (f32[2,14,2560]{2,0,1:T(2,128)S(1)}, f32[2,14,2560]{2,0,1:T(2,128)}, u32[]{:S(2)}) copy-start(f32[2,14,2560]{2,0,1:T(2,128)} %param.19) | copy-start | bytes 860164
  117.4 139.8 %copy-start.4 = (f32[2,14,2560]{2,0,1:T(2,128)S(1)}, f32[2,14,2560]{2,0,1:T(2,128)}, u32[]{:S(2)}) copy-start(f32[2,14,2560]{2,0,1:T(2,128)} %param.20) | copy-start | bytes 860164
  117.4 139.8 %copy-start.5 = (f32[2,40,896]{2,1,0:T(8,128)S(1)}, f32[2,40,896]{2,1,0:T(8,128)}, u32[]{:S(2)}) copy-start(f32[2,40,896]{2,1,0:T(8,128)} %refs_8_.1) | copy-start | bytes 860164
